TPU v7x, 32 devices: a whole 2x2x4 slice. The times are simulated.
32 devices in a mesh: dp: 8 (over z, y), ep: 4 (over x, core).
Axes of the slice: x: 2, y: 2, z: 4, core: 2. Of those that a mesh axis runs over, the one named last changes fastest.
Arguments:
- x_tokens: bfloat16 [64, 512, 256], P(('dp', 'ep'))
- dy_tokens: bfloat16 [64, 512, 256], P(('dp', 'ep'))
- route_idx: int32 [64, 512, 8], P(('dp', 'ep'))
- norm1_gain: bfloat16 [256], replicated
- norm2_gain: bfloat16 [256], replicated
- w_qkv: bfloat16 [256, 768], replicated
- w_attn_out: bfloat16 [256, 256], replicated
- w_router: bfloat16 [256, 128], replicated
- w_gate: bfloat16 [128, 256, 768], P('ep')
- w_up: bfloat16 [128, 256, 768], P('ep')
- w_down: bfloat16 [128, 768, 256], P('ep')
Outputs:
- output 1: bfloat16 [64, 512, 256], P(('dp', 'ep'))
- output 2: float32 [256], replicated
- output 3: float32 [256], replicated
- output 4: float32 [256, 768], replicated
- output 5: float32 [256, 256], replicated
- output 6: float32 [256, 128], replicated
- output 7: float32 [128, 256, 768], P('ep')
- output 8: float32 [128, 256, 768], P('ep')
- output 9: float32 [128, 768, 256], P('ep')
All inputs are finite; a program needn't handle non-finite values.
Results may differ from a plain program's by a relative error of at most 0.0169938.
Values are sent between devices in bfloat16 or wider.
A program may use at most 1 GiB of HBM per device.

v0:
```python
import jax
import jax.numpy as jnp
from jax import lax
from jax.sharding import PartitionSpec as P

EPS = 1e-6
HEAD_DIM = 128
ROPE_BASE = 10000.0


def capacity_rows(num_tokens, top_k, num_experts):
    return 8 * ((5 * num_tokens * top_k + 32 * num_experts - 1) // (32 * num_experts))


def rms_norm(x_rows, gain_vec):
    x_f32 = x_rows.astype(jnp.float32)
    inv_rms = lax.rsqrt(jnp.mean(x_f32 * x_f32, axis=-1, keepdims=True) + EPS)
    return (x_f32 * inv_rms * gain_vec.astype(jnp.float32)).astype(jnp.bfloat16)


def rms_norm_bwd(x_rows, gain_vec, d_out):
    x_f32 = x_rows.astype(jnp.float32)
    inv_rms = lax.rsqrt(jnp.mean(x_f32 * x_f32, axis=-1, keepdims=True) + EPS)
    d_gain = jnp.sum(d_out * x_f32 * inv_rms, axis=0)
    d_scaled = d_out * gain_vec.astype(jnp.float32)
    d_x = inv_rms * d_scaled - x_f32 * inv_rms ** 3 * jnp.mean(d_scaled * x_f32, axis=-1, keepdims=True)
    return d_x, d_gain


def rope_rotate(head_vals):
    seq_len = head_vals.shape[1]
    half_dim = head_vals.shape[-1] // 2
    inv_freq = ROPE_BASE ** (-jnp.arange(half_dim, dtype=jnp.float32) / half_dim)
    angles = jnp.arange(seq_len, dtype=jnp.float32)[:, None] * inv_freq[None, :]
    cos_b = jnp.cos(angles)[None, :, None, :]
    sin_b = jnp.sin(angles)[None, :, None, :]
    lower_half = head_vals[..., :half_dim]
    upper_half = head_vals[..., half_dim:]
    return jnp.concatenate([lower_half * cos_b - upper_half * sin_b, upper_half * cos_b + lower_half * sin_b], axis=-1)


def attention_core(qkv_rows, num_seqs):
    num_tokens = qkv_rows.shape[0]
    seq_len = num_tokens // num_seqs
    model_width = qkv_rows.shape[1] // 3
    qkv_heads = qkv_rows.reshape(num_seqs, seq_len, 3, model_width // HEAD_DIM, HEAD_DIM)
    query_rot = rope_rotate(qkv_heads[:, :, 0]).astype(jnp.bfloat16)
    key_rot = rope_rotate(qkv_heads[:, :, 1]).astype(jnp.bfloat16)
    value_h = qkv_heads[:, :, 2].astype(jnp.bfloat16)
    scores = jnp.einsum('bqhd,bkhd->bhqk', query_rot, key_rot, preferred_element_type=jnp.float32) * HEAD_DIM ** -0.5
    causal = jnp.arange(seq_len)[:, None] >= jnp.arange(seq_len)[None, :]
    attn_probs = jax.nn.softmax(jnp.where(causal, scores, -1e30), axis=-1).astype(jnp.bfloat16)
    context = jnp.einsum('bhqk,bkhd->bqhd', attn_probs, value_h, preferred_element_type=jnp.float32)
    return context.astype(jnp.bfloat16).reshape(num_tokens, model_width)


def gate_probs(logits, idx_rows):
    probs_all = jax.nn.softmax(logits, axis=-1)
    picked = jnp.take_along_axis(probs_all, idx_rows, axis=1)
    return picked / jnp.sum(picked, axis=1, keepdims=True)


def route_slots(idx_rows, num_experts, capacity):
    num_tokens, top_k = idx_rows.shape
    hit_count = jnp.sum((idx_rows[:, :, None] == jnp.arange(num_experts)[None, None, :]).astype(jnp.int32), axis=1)
    earlier = jnp.cumsum(hit_count, axis=0) - hit_count
    position = jnp.take_along_axis(earlier, idx_rows, axis=1)
    slot_ids = jnp.where(position < capacity, idx_rows * capacity + position, num_experts * capacity)
    source_ids = jnp.full((num_experts * capacity,), num_tokens * top_k, jnp.int32).at[slot_ids.reshape(-1)].set(jnp.arange(num_tokens * top_k, dtype=jnp.int32), mode='drop')
    return slot_ids, source_ids


def take_rows(table, row_ids):
    return jnp.take(table, row_ids, axis=0, mode='fill', fill_value=0)


def dense_forward(x_rows, idx_rows, num_seqs, norm1_gain, norm2_gain, w_qkv, w_attn_out, w_router):
    normed1 = rms_norm(x_rows, norm1_gain)
    qkv_rows = jnp.dot(normed1, w_qkv, preferred_element_type=jnp.float32)
    context, attn_pullback = jax.vjp(lambda qkv_in: attention_core(qkv_in, num_seqs), qkv_rows)
    h_rows = (x_rows.astype(jnp.float32) + jnp.dot(context, w_attn_out, preferred_element_type=jnp.float32)).astype(jnp.bfloat16)
    normed2 = rms_norm(h_rows, norm2_gain)
    logits = jnp.dot(normed2, w_router, preferred_element_type=jnp.float32)
    gate_vals, gate_pullback = jax.vjp(lambda logit_in: gate_probs(logit_in, idx_rows), logits)
    saved_state = (normed1, attn_pullback, context, h_rows, normed2, gate_pullback)
    return normed2, gate_vals, saved_state


def dense_backward(saved_state, x_rows, dy_rows, d_gates, d_normed2_moe, norm1_gain, norm2_gain, w_qkv, w_attn_out, w_router):
    normed1, attn_pullback, context, h_rows, normed2, gate_pullback = saved_state
    d_logits = gate_pullback(d_gates)[0].astype(jnp.bfloat16)
    d_w_router = jnp.einsum('td,te->de', normed2, d_logits, preferred_element_type=jnp.float32)
    d_normed2 = d_normed2_moe + jnp.einsum('te,de->td', d_logits, w_router, preferred_element_type=jnp.float32)
    d_h_part, d_norm2_gain = rms_norm_bwd(h_rows, norm2_gain, d_normed2)
    d_h = (dy_rows.astype(jnp.float32) + d_h_part).astype(jnp.bfloat16)
    d_w_attn_out = jnp.einsum('td,te->de', context, d_h, preferred_element_type=jnp.float32)
    d_context = jnp.einsum('te,de->td', d_h, w_attn_out, preferred_element_type=jnp.float32).astype(jnp.bfloat16)
    d_qkv = attn_pullback(d_context)[0].astype(jnp.bfloat16)
    d_w_qkv = jnp.einsum('td,te->de', normed1, d_qkv, preferred_element_type=jnp.float32)
    d_normed1 = jnp.einsum('te,de->td', d_qkv, w_qkv, preferred_element_type=jnp.float32)
    d_x_part, d_norm1_gain = rms_norm_bwd(x_rows, norm1_gain, d_normed1)
    d_x = (d_h.astype(jnp.float32) + d_x_part).astype(jnp.bfloat16)
    return d_x, (d_norm1_gain, d_norm2_gain, d_w_qkv, d_w_attn_out, d_w_router)


def expert_forward(slot_rows, w_gate, w_up, w_down):
    act_gate = jnp.einsum('slcd,ldf->slcf', slot_rows, w_gate, preferred_element_type=jnp.float32)
    act_up = jnp.einsum('slcd,ldf->slcf', slot_rows, w_up, preferred_element_type=jnp.float32)
    hidden = (jax.nn.silu(act_gate) * act_up).astype(jnp.bfloat16)
    expert_out = jnp.einsum('slcf,lfd->slcd', hidden, w_down, preferred_element_type=jnp.float32).astype(jnp.bfloat16)
    return act_gate, act_up, hidden, expert_out


def expert_backward(slot_rows, act_gate, act_up, hidden, d_expert_out, w_gate, w_up, w_down):
    d_hidden = jnp.einsum('slcd,lfd->slcf', d_expert_out, w_down, preferred_element_type=jnp.float32)
    d_w_down = jnp.einsum('slcf,slcd->lfd', hidden, d_expert_out, preferred_element_type=jnp.float32)
    sigmoid_g = jax.nn.sigmoid(act_gate)
    d_act_up = (d_hidden * act_gate * sigmoid_g).astype(jnp.bfloat16)
    d_act_gate = (d_hidden * act_up * sigmoid_g * (1.0 + act_gate * (1.0 - sigmoid_g))).astype(jnp.bfloat16)
    d_w_gate = jnp.einsum('slcd,slcf->ldf', slot_rows, d_act_gate, preferred_element_type=jnp.float32)
    d_w_up = jnp.einsum('slcd,slcf->ldf', slot_rows, d_act_up, preferred_element_type=jnp.float32)
    d_slot_rows = jnp.einsum('slcf,ldf->slcd', d_act_gate, w_gate, preferred_element_type=jnp.float32) + jnp.einsum('slcf,ldf->slcd', d_act_up, w_up, preferred_element_type=jnp.float32)
    return d_slot_rows.astype(jnp.bfloat16), d_w_gate, d_w_up, d_w_down


def solution(mesh):
    ep_size = mesh.shape['ep']
    tok_spec = P(('dp', 'ep'), None, None)
    rep_spec = P()
    exp_spec = P('ep', None, None)

    def local_step(x_tokens, dy_tokens, route_idx, norm1_gain, norm2_gain, w_qkv, w_attn_out, w_router, w_gate, w_up, w_down):
        num_seqs, seq_len, model_width = x_tokens.shape
        num_tokens = num_seqs * seq_len
        top_k = route_idx.shape[-1]
        local_experts = w_gate.shape[0]
        num_experts = local_experts * ep_size
        capacity = capacity_rows(num_tokens, top_k, num_experts)
        x_rows = x_tokens.reshape(num_tokens, model_width)
        dy_rows = dy_tokens.reshape(num_tokens, model_width)
        idx_rows = route_idx.reshape(num_tokens, top_k)
        normed2, gate_vals, saved_state = dense_forward(x_rows, idx_rows, num_seqs, norm1_gain, norm2_gain, w_qkv, w_attn_out, w_router)
        slot_ids, source_ids = route_slots(idx_rows, num_experts, capacity)
        slot_flat = slot_ids.reshape(-1)
        token_of_slot = source_ids // top_k
        send_rows = take_rows(normed2, token_of_slot).reshape(ep_size, local_experts, capacity, model_width)
        recv_rows = lax.all_to_all(send_rows, 'ep', 0, 0, tiled=True)
        act_gate, act_up, hidden, expert_out = expert_forward(recv_rows, w_gate, w_up, w_down)
        back_rows = lax.all_to_all(expert_out, 'ep', 0, 0, tiled=True).reshape(num_experts * capacity, model_width)
        choice_rows = take_rows(back_rows, slot_flat).reshape(num_tokens, top_k, model_width)
        d_gates = jnp.einsum('td,tkd->tk', dy_rows, choice_rows, preferred_element_type=jnp.float32)
        gate_of_slot = take_rows(gate_vals.reshape(-1), source_ids)
        d_slot_out = (take_rows(dy_rows, token_of_slot).astype(jnp.float32) * gate_of_slot[:, None]).astype(jnp.bfloat16)
        d_expert_out = lax.all_to_all(d_slot_out.reshape(ep_size, local_experts, capacity, model_width), 'ep', 0, 0, tiled=True)
        d_recv, d_w_gate, d_w_up, d_w_down = expert_backward(recv_rows, act_gate, act_up, hidden, d_expert_out, w_gate, w_up, w_down)
        d_back = lax.all_to_all(d_recv, 'ep', 0, 0, tiled=True).reshape(num_experts * capacity, model_width)
        d_normed2_moe = jnp.sum(take_rows(d_back, slot_flat).reshape(num_tokens, top_k, model_width).astype(jnp.float32), axis=1)
        d_x, dense_grads = dense_backward(saved_state, x_rows, dy_rows, d_gates, d_normed2_moe, norm1_gain, norm2_gain, w_qkv, w_attn_out, w_router)
        expert_grads = lax.psum((d_w_gate, d_w_up, d_w_down), 'dp')
        dense_grads = lax.psum(dense_grads, ('dp', 'ep'))
        return (d_x.reshape(x_tokens.shape),) + tuple(dense_grads) + tuple(expert_grads)

    return jax.shard_map(local_step, mesh=mesh,
                         in_specs=(tok_spec, tok_spec, tok_spec, rep_spec, rep_spec, rep_spec, rep_spec, rep_spec, exp_spec, exp_spec, exp_spec),
                         out_specs=(tok_spec, rep_spec, rep_spec, rep_spec, rep_spec, rep_spec, exp_spec, exp_spec, exp_spec),
                         check_vma=False)
```

profile of v0, /device:TPU:0, one launch (start us, length us, event | category | flops | bytes accessed | tf_op | source)
XLA Modules:
  0.0 3187.4 jit_solution(11450963091214301021)
XLA Ops:
  20.4 50.7 %gather_fusion.1 = s32[8192]{0:T(1024)S(1)} fusion(s32[1024,128]{1,0:T(8,128)S(1)} %bitcast_subtract_fusion, s32[8192]{0:T(1024)S(1)} %reshape.431), kind=kCustom, calls=%fused_computation.5 | custom fusion | bytes 131072 | tf_op jit(solution)/shard_map/jit(take_along_axis)/gather | solution.py:67
  71.3 30.6 scatter_custom_fusion
  127.6 65.5 %gather_fusion.2 = f32[8192]{0:T(1024)S(1)} fusion(f32[1024,128]{0,1:T(8,128)S(1)} %fusion.100, s32[8192]{0:T(1024)S(1)} %reshape.431), kind=kCustom, calls=%fused_computation.6 | custom fusion | bytes 131072 | tf_op jit(solution)/shard_map/jvp(jit(take_along_axis))/gather | solution.py:59
  194.2 56.8 %gather_fusion = f32[10240]{0:T(1024)S(1)} fusion(f32[8192]{0:T(1024)S(1)} %select_divide_fusion, s32[10240]{0:T(1024)S(1)} %copy-done.44), kind=kCustom, calls=%fused_computation.4 | custom fusion | bytes 122880 | tf_op jit(solution)/shard_map/jit(_take)/gather | solution.py:74
  251.1 41.2 %gather_fusion.3 = bf16[10240,256]{1,0:T(8,128)(2,1)} fusion(bf16[1024,256]{1,0:T(8,128)(2,1)S(1)} %bitcast.219, s32[10240]{0:T(1024)S(1)} %copy-done.34), kind=kCustom, calls=%fused_computation.clone | custom fusion | bytes 10526720 | tf_op jit(solution)/shard_map/jit(_take)/gather | solution.py:74
  306.8 41.2 %gather_fusion.4 = bf16[10240,256]{1,0:T(8,128)(2,1)} fusion(bf16[1024,256]{1,0:T(8,128)(2,1)S(1)} %copy-done.2, s32[10240]{0:T(1024)S(1)} %copy-done.34), kind=kCustom, calls=%fused_computation.2.clone | custom fusion | bytes 10526720 | tf_op jit(solution)/shard_map/jit(_take)/gather | solution.py:74
  377.7 16.6 fusion.22
  394.3 37.3 %all-to-all-done.1 = bf16[4,32,80,256]{3,2,1,0:T(8,128)(2,1)} async-done(((bf16[4,32,80,256]{3,2,1,0:T(8,128)(2,1)}), bf16[4,32,80,256]{3,2,1,0:T(8,128)(2,1)}, u32[]{:S(2)}, u32[]{:S(2)}) %all-to-all-start.1) | async-done | bytes 5242912 | tf_op jit(solution)/shard_map/all_to_all | solution.py:147
  431.7 20.8 fusion.26
  452.5 43.4 %fusion.10 = (bf16[4,32,80,768]{3,2,0,1:T(8,128)(2,1)}, bf16[4,32,80,768]{3,2,0,1:T(8,128)(2,1)}, bf16[4,32,80,768]{3,2,0,1:T(8,128)(2,1)}) fusion(f32[32,4,80,768]{3,2,1,0:T(8,128)} %fusion.26, f32[32,4,80,768]{3,2,1,0:T(8,128)} %fusion.22, bf16[32,256,768]{2,1,0:T(8,128)(2,1)} %param.23, bf16[4,32,80,256]{3,2,1,0:T(8,128)(2,1)} %all-to-all-done.1), kind=kOutput, calls=%fused_computation.23 | convolution fusion | flops 4152360960 | bytes 127926272 | tf_op jit(solution)/shard_map/slcd,ldf->slcf/dot_general | solution.py:107
  515.5 15.5 fusion.16
  531.0 23.3 fusion.34
  559.6 15.3 all-to-all-done.3
  580.1 16.6 fusion.31
  596.7 16.4 fusion.28
  613.1 34.4 %gather_fusion.6 = bf16[8192,256]{1,0:T(8,128)(2,1)} fusion(bf16[10240,256]{1,0:T(8,128)(2,1)} %bitcast.37, s32[8192]{0:T(1024)S(1)} %copy-done.36), kind=kCustom, calls=%fused_computation.3.clone | custom fusion | bytes 8421376 | tf_op jit(solution)/shard_map/jit(_take)/gather | solution.py:74
  658.0 57.1 %scatter_custom_fusion.1 = f32[131072]{0:T(1024)S(1)} fusion(s32[8192]{0:T(1024)} %reshape.451, f32[8192]{0:T(1024)S(1)} %reshape.453, f32[]{:T(128)} %constant.67.clone.1), kind=kCustom, calls=%fused_computation.159 | custom fusion | flops 8192 | bytes 524800
  716.6 34.3 %gather_fusion.5 = bf16[8192,256]{1,0:T(8,128)(2,1)} fusion(bf16[10240,256]{1,0:T(8,128)(2,1)} %bitcast.33, s32[8192]{0:T(1024)S(1)} %copy-done.36), kind=kCustom, calls=%fused_computation.1.clone | custom fusion | bytes 8421376 | tf_op jit(solution)/shard_map/jit(_take)/gather | solution.py:74
  780.5 19.0 convolution_bitcast_fusion
  802.3 41.7 %all-reduce.7 = (f32[256]{0:T(256)}, f32[256]{0:T(256)}) all-reduce(f32[256]{0:T(256)S(1)} %get-tuple-element.13, f32[256]{0:T(256)S(1)} %get-tuple-element.11), channel_id=1, replica_groups=mesh['dp'=8,'ep'=4] {'dp','ep'}, use_global_device_ids=true, to_apply=%region_19.22 | all-reduce | flops 512 | bytes 4096 | tf_op jit(solution)/shard_map/psum | solution.py:160
  846.5 69.1 %all-reduce.13.cloned.1.call-done = (f32[256,768]{1,0:T(8,128)}, f32[256,256]{1,0:T(8,128)}, f32[256,128]{1,0:T(8,128)}) async-done(((f32[256,768]{1,0:T(8,128)}, f32[256,256]{1,0:T(8,128)}, f32[256,128]{1,0:T(8,128)}), (f32[256,768]{1,0:T(8,128)}, f32[256,256]{1,0:T(8,128)}, f32[256,128]{1,0:T(8,128)})) %all-reduce.13.cloned.1.call-update) | async-done | bytes 1179664 | tf_op jit(solution)/shard_map/psum | solution.py:160
  915.6 2210.5 %all-reduce.15.cloned.1.call-done = (f32[32,256,768]{2,1,0:T(8,128)}, f32[32,256,768]{2,1,0:T(8,128)}, f32[32,768,256]{2,1,0:T(8,128)}) async-done(((f32[32,256,768]{2,1,0:T(8,128)}, f32[32,256,768]{2,1,0:T(8,128)}, f32[32,768,256]{2,1,0:T(8,128)}), (f32[32,256,768]{2,1,0:T(8,128)}, f32[32,256,768]{2,1,0:T(8,128)}, f32[32,768,256]{2,1,0:T(8,128)})) %all-reduce.15.cloned.1.call-update) | async-done | bytes 75497488 | tf_op jit(solution)/shard_map/psum | solution.py:159
  3131.5 19.7 copy.230
  3151.1 19.6 copy.231
  (280 shorter events, 175.0 us)
Async XLA Ops:
  7.2 116.0 %copy-start = (bf16[256,256]{1,0:T(8,128)(2,1)S(1)}, bf16[256,256]{1,0:T(8,128)(2,1)}, u32[]{:S(2)}) copy-start(bf16[256,256]{1,0:T(8,128)(2,1)} %param.21) | copy-start | bytes 393220
  20.3 82.9 %copy-start.73 = (bf16[256]{0:T(256)(128)(2,1)S(1)}, bf16[256]{0:T(256)(128)(2,1)}, u32[]{:S(2)}) copy-start(bf16[256]{0:T(256)(128)(2,1)} %param.18) | copy-start | bytes 1540
  20.4 82.9 %copy-start.74 = (bf16[256]{0:T(256)(128)(2,1)S(1)}, bf16[256]{0:T(256)(128)(2,1)}, u32[]{:S(2)}) copy-start(bf16[256]{0:T(256)(128)(2,1)} %param.19) | copy-start | bytes 1540
  20.4 82.9 %copy-start.18 = (bf16[2,512,256]{2,1,0:T(8,128)(2,1)S(1)}, bf16[2,512,256]{2,1,0:T(8,128)(2,1)}, u32[]{:S(2)}) copy-start(bf16[2,512,256]{2,1,0:T(8,128)(2,1)} %param.15) | copy-start | bytes 1572868
  20.4 83.7 %copy-start.72 = (f32[64]{0:T(128)S(1)}, f32[64]{0:T(128)}, u32[]{:S(2)}) copy-start(f32[64]{0:T(128)} %multiply_power_fusion) | copy-start | bytes 772
  20.4 84.9 %copy-start.32 = (bf16[256,768]{1,0:T(8,128)(2,1)S(1)}, bf16[256,768]{1,0:T(8,128)(2,1)}, u32[]{:S(2)}) copy-start(bf16[256,768]{1,0:T(8,128)(2,1)} %param.20) | copy-start | bytes 1179652
  127.6 66.0 %copy-start.25 = (s32[2,512,8]{1,2,0:T(8,128)S(1)}, s32[2,512,8]{1,2,0:T(8,128)}, u32[]{:S(2)}) copy-start(s32[2,512,8]{1,2,0:T(8,128)} %param.17) | copy-start | bytes 98308
  127.6 66.5 %copy-start.29 = (s32[8192]{0:T(1024)S(1)}, s32[8192]{0:T(1024)}, u32[]{:S(2)}) copy-start(s32[8192]{0:T(1024)} %reshape.377) | copy-start | bytes 98308
  127.6 66.6 %copy-start.44 = (s32[10240]{0:T(1024)S(1)}, s32[10240]{0:T(1024)}, u32[]{:S(2)}) copy-start(s32[10240]{0:T(1024)} %get-tuple-element.40) | copy-start | bytes 122884
  193.7 181.5 %copy-start.55 = (f32[1,4,2,128]{3,1,2,0:T(4,128)}, f32[1,4,2,128]{3,1,2,0:T(4,128)S(1)}, u32[]{:S(2)}) copy-start(f32[1,4,2,128]{3,1,2,0:T(4,128)S(1)} %copy.187) | copy-start | bytes 12292
  194.2 56.8 %copy-start.28 = (s32[10240]{0:T(1024)S(1)}, s32[10240]{0:T(1024)}, u32[]{:S(2)}) copy-start(s32[10240]{0:T(1024)} %copy-done.27) | copy-start | bytes 122884
  194.2 56.9 %copy-start.4 = (bf16[2,512,256]{2,1,0:T(8,128)(2,1)S(1)}, bf16[2,512,256]{2,1,0:T(8,128)(2,1)}, u32[]{:S(2)}) copy-start(bf16[2,512,256]{2,1,0:T(8,128)(2,1)} %param.16) | copy-start | bytes 1572868
  194.2 56.8 %copy-start.34 = (s32[10240]{0:T(1024)S(1)}, s32[10240]{0:T(1024)}, u32[]{:S(2)}) copy-start(s32[10240]{0:T(1024)} %get-tuple-element.41) | copy-start | bytes 122884
  301.5 65.3 %all-to-all-start = ((bf16[4,32,80,256]{3,2,1,0:T(8,128)(2,1)}), bf16[4,32,80,256]{3,2,1,0:T(8,128)(2,1)}, u32[]{:S(2)}, u32[]{:S(2)}) async-start(bf16[4,32,80,256]{3,2,1,0:T(8,128)(2,1)} %bitcast.224), calls=%async_computation | async-start | bytes 10485760 | tf_op jit(solution)/shard_map/all_to_all | solution.py:154
  366.8 64.9 %all-to-all-start.1 = ((bf16[4,32,80,256]{3,2,1,0:T(8,128)(2,1)}), bf16[4,32,80,256]{3,2,1,0:T(8,128)(2,1)}, u32[]{:S(2)}, u32[]{:S(2)}) async-start(bf16[4,32,80,256]{3,2,1,0:T(8,128)(2,1)} %bitcast.223), calls=%async_computation.1 | async-start | bytes 10485760 | tf_op jit(solution)/shard_map/all_to_all | solution.py:147
  510.4 64.5 %all-to-all-start.3 = ((bf16[4,32,80,256]{3,2,1,0:T(8,128)(2,1)}), bf16[4,32,80,256]{3,2,1,0:T(8,128)(2,1)}, u32[]{:S(2)}, u32[]{:S(2)}) async-start(bf16[4,32,80,256]{3,2,1,0:T(8,128)(2,1)} %copy.155), calls=%async_computation.3 | async-start | bytes 10485760 | tf_op jit(solution)/shard_map/all_to_all | solution.py:149
  574.9 141.7 %all-to-all-start.2 = ((bf16[4,32,80,256]{3,2,1,0:T(8,128)(2,1)}), bf16[4,32,80,256]{3,2,1,0:T(8,128)(2,1)}, u32[]{:S(2)}, u32[]{:S(2)}) async-start(bf16[4,32,80,256]{3,2,1,0:T(8,128)(2,1)} %copy.153), calls=%async_computation.2 | async-start | bytes 10485760 | tf_op jit(solution)/shard_map/all_to_all | solution.py:156
  580.0 335.6 %all-reduce.13.cloned.1.call-start = ((), (), s32[]{:S(2)}) async-start(), calls=%async_computation.4 | async-start | bytes 2359296 | tf_op jit(solution)/shard_map/psum | solution.py:160
  647.6 67.8 %copy-start.11 = (f32[1024,128]{0,1:T(8,128)S(1)}, f32[1024,128]{0,1:T(8,128)}, u32[]{:S(2)}) copy-start(f32[1024,128]{0,1:T(8,128)} %copy-done.10) | copy-start | bytes 1572868
  647.6 67.8 %copy-start.48 = (f32[1024]{0:T(1024)S(1)}, f32[1024]{0:T(1024)}, u32[]{:S(2)}) copy-start(f32[1024]{0:T(1024)} %copy-done.47) | copy-start | bytes 12292
  647.6 67.8 %copy-start.63 = (f32[1024]{0:T(1024)S(1)}, f32[1024]{0:T(1024)}, u32[]{:S(2)}) copy-start(f32[1024]{0:T(1024)} %multiply_divide_fusion.1) | copy-start | bytes 12292
  647.6 67.9 %copy-start.54 = (f32[1024]{0:T(1024)S(1)}, f32[1024]{0:T(1024)}, u32[]{:S(2)}) copy-start(f32[1024]{0:T(1024)} %copy-done.52) | copy-start | bytes 12292
  657.2 58.5 %copy-start.3 = (bf16[1024,256]{1,0:T(8,128)(2,1)S(1)}, bf16[1024,256]{1,0:T(8,128)(2,1)}, u32[]{:S(2)}) copy-start(bf16[1024,256]{1,0:T(8,128)(2,1)} %copy-done.1) | copy-start | bytes 1572868
  780.5 2345.7 %all-reduce.15.cloned.1.call-start = ((), (), s32[]{:S(2)}) async-start(), calls=%async_computation.5 | async-start | bytes 150994944 | tf_op jit(solution)/shard_map/psum | solution.py:159
  (63 other events, 705.2 us)
Sparse Core Ops, SparseCore 0:
  780.6 135.0 all-reduce.12
  921.6 2204.5 all-reduce.14
where the time goes:
time: 3190 us
  waiting for transfers between devices  2340 us (73%)
  local copies, waits for them, and re-layouts  436 us (14%)
  matrix products  217 us (7%)
  other arithmetic  111 us (3%)
  blocking collectives  41.7 us (1%)
    psum x1, waiting for transfers between devices, local_step(): expert_grads = lax.psum((d_w_gate, d_w_up, d_w_down), 'dp')  2210 us
    gather x5, local copies, waits for them, and re-layouts, take_rows(): return jnp.take(table, row_ids, axis=0, mode='fill', fill_value=0)  208 us
    psum x1, waiting for transfers between devices, local_step(): dense_grads = lax.psum(dense_grads, ('dp', 'ep'))  69.1 us
    gather x5, local copies, waits for them, and re-layouts, gate_probs(): picked = jnp.take_along_axis(probs_all, idx_rows, axis=1)  67.1 us
  transfers between devices with their start and end apart: 6, of which 5 were waited for; matrix products, arithmetic and copies ran while one was open for 9% of the time, Pallas kernels for 0%

commit v1 on v0

v1 whole, which is shorter than its diff:
```python
import functools

import jax
import jax.numpy as jnp
from jax import lax
from jax.experimental import pallas as pl
from jax.experimental.pallas import tpu as pltpu
from jax.sharding import PartitionSpec as P


F32 = jnp.float32
BF16 = jnp.bfloat16
EPS = 1e-6
HEAD_DIM = 128
ROPE_BASE = 10000.0


def capacity_rows(num_tokens, top_k, num_experts):
    return 8 * ((5 * num_tokens * top_k + 32 * num_experts - 1) // (32 * num_experts))


def rms_norm(x_rows, gain_vec):
    x_f32 = x_rows.astype(jnp.float32)
    inv_rms = lax.rsqrt(jnp.mean(x_f32 * x_f32, axis=-1, keepdims=True) + EPS)
    return (x_f32 * inv_rms * gain_vec.astype(jnp.float32)).astype(jnp.bfloat16)


def rms_norm_bwd(x_rows, gain_vec, d_out):
    x_f32 = x_rows.astype(jnp.float32)
    inv_rms = lax.rsqrt(jnp.mean(x_f32 * x_f32, axis=-1, keepdims=True) + EPS)
    d_gain = jnp.sum(d_out * x_f32 * inv_rms, axis=0)
    d_scaled = d_out * gain_vec.astype(jnp.float32)
    d_x = inv_rms * d_scaled - x_f32 * inv_rms ** 3 * jnp.mean(d_scaled * x_f32, axis=-1, keepdims=True)
    return d_x, d_gain


def rope_rotate(head_vals):
    seq_len = head_vals.shape[1]
    half_dim = head_vals.shape[-1] // 2
    inv_freq = ROPE_BASE ** (-jnp.arange(half_dim, dtype=jnp.float32) / half_dim)
    angles = jnp.arange(seq_len, dtype=jnp.float32)[:, None] * inv_freq[None, :]
    cos_b = jnp.cos(angles)[None, :, None, :]
    sin_b = jnp.sin(angles)[None, :, None, :]
    lower_half = head_vals[..., :half_dim]
    upper_half = head_vals[..., half_dim:]
    return jnp.concatenate([lower_half * cos_b - upper_half * sin_b, upper_half * cos_b + lower_half * sin_b], axis=-1)


def attention_core(qkv_rows, num_seqs):
    num_tokens = qkv_rows.shape[0]
    seq_len = num_tokens // num_seqs
    model_width = qkv_rows.shape[1] // 3
    qkv_heads = qkv_rows.reshape(num_seqs, seq_len, 3, model_width // HEAD_DIM, HEAD_DIM)
    query_rot = rope_rotate(qkv_heads[:, :, 0]).astype(jnp.bfloat16)
    key_rot = rope_rotate(qkv_heads[:, :, 1]).astype(jnp.bfloat16)
    value_h = qkv_heads[:, :, 2].astype(jnp.bfloat16)
    scores = jnp.einsum('bqhd,bkhd->bhqk', query_rot, key_rot, preferred_element_type=jnp.float32) * HEAD_DIM ** -0.5
    causal = jnp.arange(seq_len)[:, None] >= jnp.arange(seq_len)[None, :]
    attn_probs = jax.nn.softmax(jnp.where(causal, scores, -1e30), axis=-1).astype(jnp.bfloat16)
    context = jnp.einsum('bhqk,bkhd->bqhd', attn_probs, value_h, preferred_element_type=jnp.float32)
    return context.astype(jnp.bfloat16).reshape(num_tokens, model_width)


def gate_probs(logits, idx_cols):
    probs_all = jax.nn.softmax(logits, axis=-1)
    chosen = idx_cols[:, :, None] == jnp.arange(logits.shape[1], dtype=jnp.int32)[None, None, :]
    picked = jnp.sum(jnp.where(chosen, probs_all[None], 0.0), axis=2)
    return picked / jnp.sum(picked, axis=0, keepdims=True)


def slot_positions(local_idx, local_experts, capacity):
    num_tokens = local_idx.shape[-1]
    expert_ids = jnp.arange(local_experts, dtype=jnp.int32)
    member = jnp.any(local_idx[None] == expert_ids[:, None, None, None], axis=2)
    before = (jnp.arange(num_tokens)[:, None] < jnp.arange(num_tokens)[None, :]).astype(BF16)
    earlier = jnp.einsum('est,tv->esv', member.astype(BF16), before, preferred_element_type=F32)
    return jnp.where(member & (earlier < capacity), earlier.astype(jnp.int32), -1)


def mat_nn(left, right):
    return lax.dot_general(left, right, (((1,), (0,)), ((), ())), preferred_element_type=F32)


def mat_nt(left, right):
    return lax.dot_general(left, right, (((1,), (1,)), ((), ())), preferred_element_type=F32)


def mat_tn(left, right):
    return lax.dot_general(left, right, (((0,), (0,)), ((), ())), preferred_element_type=F32)


def select_slots(capacity, group, pos_ref, idx_ref, gate_ref, source, first):
    num_tokens = pos_ref.shape[-1]
    slot_iota = lax.broadcasted_iota(jnp.int32, (capacity, num_tokens), 0)
    selectors, gate_cols = [], []
    for member in range(group):
        hit = slot_iota == pos_ref[member, pl.ds(source, 1), :]
        gate_row = jnp.sum(jnp.where(idx_ref[source] == first + member, gate_ref[source], 0.0), axis=0, keepdims=True)
        gate_cols.append(jnp.sum(jnp.where(hit, gate_row, 0.0), axis=1, keepdims=True))
        selectors.append(jnp.where(hit, 1.0, 0.0).astype(BF16))
    return jnp.concatenate(selectors, axis=0), jnp.concatenate(gate_cols, axis=0)


def swiglu_bwd(act_gate, act_up, d_hidden):
    sig = 0.5 * jnp.tanh(0.5 * act_gate) + 0.5
    silu = act_gate * sig
    hidden = (silu * act_up).astype(BF16)
    d_act_up = (d_hidden * silu).astype(BF16)
    d_act_gate = (d_hidden * act_up * (sig + silu * (1.0 - sig))).astype(BF16)
    return hidden, d_act_gate, d_act_up


def token_grad_kernel(capacity, group, pos_ref, idx_ref, gate_ref, rows_ref, dy_ref, w_gate_ref, w_up_ref, w_down_ref,
                      d_rows_ref, d_gates_ref, select_scr, in_scr, raw_scr, dout_scr, din_scr):
    sources = rows_ref.shape[0]
    num_tokens = rows_ref.shape[1]
    first = pl.program_id(0) * group

    @pl.when(pl.program_id(0) == 0)
    def _():
        d_rows_ref[...] = jnp.zeros_like(d_rows_ref)
        d_gates_ref[...] = jnp.zeros_like(d_gates_ref)

    @pl.loop(0, sources)
    def _(source):
        selector, gate_col = select_slots(capacity, group, pos_ref, idx_ref, gate_ref, source, first)
        select_scr[source] = selector
        slot_rows = mat_nn(selector, rows_ref[source]).astype(BF16)
        raw_dy = mat_nn(selector, dy_ref[source])
        scaled_dy = (raw_dy * gate_col).astype(BF16)
        raw_dy = raw_dy.astype(BF16)
        for member in range(group):
            span = pl.ds(source * capacity, capacity)
            part = slice(member * capacity, (member + 1) * capacity)
            in_scr[member, span] = slot_rows[part]
            raw_scr[member, span] = raw_dy[part]
            dout_scr[member, span] = scaled_dy[part]

    slot_iota = lax.broadcasted_iota(jnp.int32, (capacity, num_tokens), 0)
    for member in range(group):
        slot_rows = in_scr[member]
        d_out = dout_scr[member]
        act_gate = mat_nn(slot_rows, w_gate_ref[member])
        act_up = mat_nn(slot_rows, w_up_ref[member])
        d_hidden = mat_nt(d_out, w_down_ref[member])
        hidden, d_act_gate, d_act_up = swiglu_bwd(act_gate, act_up, d_hidden)
        expert_out = mat_nn(hidden, w_down_ref[member]).astype(BF16)
        d_gate = jnp.sum(raw_scr[member].astype(F32) * expert_out.astype(F32), axis=1, keepdims=True)
        d_in = (mat_nt(d_act_gate, w_gate_ref[member]) + mat_nt(d_act_up, w_up_ref[member])).astype(BF16)
        for source in range(sources):
            part = slice(source * capacity, (source + 1) * capacity)
            din_scr[source, member * capacity:(member + 1) * capacity] = d_in[part]
            hit = slot_iota == pos_ref[member, source:source + 1, :]
            d_gate_row = jnp.sum(jnp.where(hit, d_gate[part], 0.0), axis=0, keepdims=True)
            d_gates_ref[source] += jnp.where(idx_ref[source] == first + member, d_gate_row, 0.0)

    @pl.loop(0, sources)
    def _(source):
        d_rows_ref[source] += mat_tn(select_scr[source], din_scr[source])


def token_grads(positions, local_idx, gates, rows, dy_rows, w_gate, w_up, w_down, capacity):
    group = 4
    sources, num_tokens, width = rows.shape
    num_experts, _, _ = w_gate.shape
    slots = sources * capacity

    def whole(arr):
        return pl.BlockSpec(arr.shape, lambda step: (0,) * arr.ndim, pipeline_mode=pl.Buffered(1))

    def per_step(arr):
        return pl.BlockSpec((group,) + arr.shape[1:], lambda step: (step, 0, 0))

    return pl.pallas_call(
        functools.partial(token_grad_kernel, capacity, group),
        grid=(num_experts // group,),
        in_specs=[per_step(positions), whole(local_idx), whole(gates), whole(rows), whole(dy_rows),
                  per_step(w_gate), per_step(w_up), per_step(w_down)],
        out_specs=[pl.BlockSpec(rows.shape, lambda step: (0, 0, 0)), pl.BlockSpec(gates.shape, lambda step: (0, 0, 0))],
        out_shape=[jax.ShapeDtypeStruct(rows.shape, F32), jax.ShapeDtypeStruct(gates.shape, F32)],
        scratch_shapes=[pltpu.VMEM((sources, group * capacity, num_tokens), BF16),
                        pltpu.VMEM((group, slots, width), BF16), pltpu.VMEM((group, slots, width), BF16),
                        pltpu.VMEM((group, slots, width), BF16), pltpu.VMEM((sources, group * capacity, width), BF16)],
        compiler_params=pltpu.CompilerParams(vmem_limit_bytes=60_000_000, dimension_semantics=("arbitrary",)),
        cost_estimate=pl.CostEstimate(flops=45_000_000_000, bytes_accessed=60_000_000, transcendentals=0),
        name="expert_token_grads",
    )(positions, local_idx, gates, rows, dy_rows, w_gate, w_up, w_down)


def weight_grad_kernel(capacity, group, chunk, pos_ref, idx_ref, gate_ref, rows_ref, dy_ref, w_gate_ref, w_up_ref, w_down_ref,
                       d_w_gate_ref, d_w_up_ref, d_w_down_ref, in_scr, dout_scr, down_scr):
    expert = pl.program_id(0)
    member = lax.rem(expert, group)
    sources = rows_ref.shape[0]

    @pl.when(member == 0)
    def _():
        @pl.loop(0, sources)
        def _(source):
            selector, gate_col = select_slots(capacity, group, pos_ref, idx_ref, gate_ref, source, expert)
            slot_rows = mat_nn(selector, rows_ref[source]).astype(BF16)
            scaled_dy = (mat_nn(selector, dy_ref[source]) * gate_col).astype(BF16)
            for k in range(group):
                span = pl.ds(source * capacity, capacity)
                part = slice(k * capacity, (k + 1) * capacity)
                in_scr[k, span] = slot_rows[part]
                dout_scr[k, span] = scaled_dy[part]

    d_w_gate_ref[...] = jnp.zeros_like(d_w_gate_ref)
    d_w_up_ref[...] = jnp.zeros_like(d_w_up_ref)
    down_scr[...] = jnp.zeros_like(down_scr)

    def forward(start):
        span = pl.ds(start, chunk)
        slot_rows = in_scr[member, span]
        d_out = dout_scr[member, span]
        return slot_rows, d_out, mat_nn(slot_rows, w_gate_ref[0]), mat_nn(slot_rows, w_up_ref[0]), mat_nt(d_out, w_down_ref[0])

    ahead = forward(0)
    for start in range(0, sources * capacity, chunk):
        slot_rows, d_out, act_gate, act_up, d_hidden = ahead
        if start + chunk < sources * capacity:
            ahead = forward(start + chunk)
        hidden, d_act_gate, d_act_up = swiglu_bwd(act_gate, act_up, d_hidden)
        d_w_gate_ref[0] += mat_tn(slot_rows, d_act_gate)
        d_w_up_ref[0] += mat_tn(slot_rows, d_act_up)
        down_scr[...] += mat_tn(d_out, hidden)

    d_w_down_ref[0] = down_scr[...].T


def weight_grads(positions, local_idx, gates, rows, dy_rows, w_gate, w_up, w_down, capacity):
    group = 4
    chunk = 256
    sources, num_tokens, width = rows.shape
    num_experts, _, ff = w_gate.shape
    slots = sources * capacity

    def whole(arr):
        return pl.BlockSpec(arr.shape, lambda step: (0,) * arr.ndim, pipeline_mode=pl.Buffered(1))

    def per_step(arr):
        return pl.BlockSpec((1,) + arr.shape[1:], lambda step: (step, 0, 0))

    return pl.pallas_call(
        functools.partial(weight_grad_kernel, capacity, group, chunk),
        grid=(num_experts,),
        in_specs=[pl.BlockSpec((group, sources, num_tokens), lambda step: (step // group, 0, 0)), whole(local_idx), whole(gates),
                  whole(rows), whole(dy_rows), per_step(w_gate), per_step(w_up), per_step(w_down)],
        out_specs=[per_step(w_gate), per_step(w_up), per_step(w_down)],
        out_shape=[jax.ShapeDtypeStruct(arr.shape, F32) for arr in (w_gate, w_up, w_down)],
        scratch_shapes=[pltpu.VMEM((group, slots, width), BF16), pltpu.VMEM((group, slots, width), BF16), pltpu.VMEM((width, ff), F32)],
        compiler_params=pltpu.CompilerParams(vmem_limit_bytes=67_000_000, dimension_semantics=("arbitrary",)),
        cost_estimate=pl.CostEstimate(flops=280_000_000_000, bytes_accessed=150_000_000, transcendentals=0),
        name="expert_weight_grads",
    )(positions, local_idx, gates, rows, dy_rows, w_gate, w_up, w_down)


def dense_forward(x_rows, idx_cols, num_seqs, norm1_gain, norm2_gain, w_qkv, w_attn_out, w_router):
    normed1 = rms_norm(x_rows, norm1_gain)
    qkv_rows = jnp.dot(normed1, w_qkv, preferred_element_type=jnp.float32)
    context, attn_pullback = jax.vjp(lambda qkv_in: attention_core(qkv_in, num_seqs), qkv_rows)
    h_rows = (x_rows.astype(jnp.float32) + jnp.dot(context, w_attn_out, preferred_element_type=jnp.float32)).astype(jnp.bfloat16)
    normed2 = rms_norm(h_rows, norm2_gain)
    logits = jnp.dot(normed2, w_router, preferred_element_type=jnp.float32)
    gate_vals, gate_pullback = jax.vjp(lambda logit_in: gate_probs(logit_in, idx_cols), logits)
    saved_state = (normed1, attn_pullback, context, h_rows, normed2, gate_pullback)
    return normed2, gate_vals, saved_state


def dense_backward(saved_state, x_rows, dy_rows, d_gates, d_normed2_moe, norm1_gain, norm2_gain, w_qkv, w_attn_out, w_router):
    normed1, attn_pullback, context, h_rows, normed2, gate_pullback = saved_state
    d_logits = gate_pullback(d_gates)[0].astype(jnp.bfloat16)
    d_w_router = jnp.einsum('td,te->de', normed2, d_logits, preferred_element_type=jnp.float32)
    d_normed2 = d_normed2_moe + jnp.einsum('te,de->td', d_logits, w_router, preferred_element_type=jnp.float32)
    d_h_part, d_norm2_gain = rms_norm_bwd(h_rows, norm2_gain, d_normed2)
    d_h = (dy_rows.astype(jnp.float32) + d_h_part).astype(jnp.bfloat16)
    d_w_attn_out = jnp.einsum('td,te->de', context, d_h, preferred_element_type=jnp.float32)
    d_context = jnp.einsum('te,de->td', d_h, w_attn_out, preferred_element_type=jnp.float32).astype(jnp.bfloat16)
    d_qkv = attn_pullback(d_context)[0].astype(jnp.bfloat16)
    d_w_qkv = jnp.einsum('td,te->de', normed1, d_qkv, preferred_element_type=jnp.float32)
    d_normed1 = jnp.einsum('te,de->td', d_qkv, w_qkv, preferred_element_type=jnp.float32)
    d_x_part, d_norm1_gain = rms_norm_bwd(x_rows, norm1_gain, d_normed1)
    d_x = (d_h.astype(jnp.float32) + d_x_part).astype(jnp.bfloat16)
    return d_x, (d_norm1_gain, d_norm2_gain, d_w_qkv, d_w_attn_out, d_w_router)


def solution(mesh):
    ep_size = mesh.shape['ep']
    tok_spec = P(('dp', 'ep'), None, None)
    rep_spec = P()
    exp_spec = P('ep', None, None)

    def local_step(x_tokens, dy_tokens, route_idx, norm1_gain, norm2_gain, w_qkv, w_attn_out, w_router, w_gate, w_up, w_down):
        num_seqs, seq_len, model_width = x_tokens.shape
        num_tokens = num_seqs * seq_len
        top_k = route_idx.shape[-1]
        local_experts = w_gate.shape[0]
        num_experts = local_experts * ep_size
        capacity = capacity_rows(num_tokens, top_k, num_experts)
        x_rows = x_tokens.reshape(num_tokens, model_width)
        dy_rows = dy_tokens.reshape(num_tokens, model_width)
        idx_cols = route_idx.reshape(num_tokens, top_k).T
        dy_all = lax.all_gather(dy_rows, ('dp', 'ep'))
        idx_all = lax.all_gather(idx_cols, ('dp', 'ep'))
        local_idx = idx_all - lax.axis_index('ep') * local_experts
        positions = slot_positions(local_idx, local_experts, capacity)
        normed2, gate_vals, saved_state = dense_forward(x_rows, idx_cols, num_seqs, norm1_gain, norm2_gain, w_qkv, w_attn_out, w_router)
        near_rows = lax.all_gather(normed2, 'ep')
        near_gates = lax.all_gather(gate_vals, 'ep')
        rows_all = lax.all_gather(normed2, ('dp', 'ep'))
        gates_all = lax.all_gather(gate_vals, ('dp', 'ep'))
        near = lax.axis_index('dp') * ep_size
        d_near, d_gate_near = token_grads(lax.dynamic_slice_in_dim(positions, near, ep_size, 1), lax.dynamic_slice_in_dim(local_idx, near, ep_size, 0),
                                          near_gates, near_rows, lax.all_gather(dy_rows, 'ep'), w_gate, w_up, w_down, capacity)
        d_normed2_moe = jnp.sum(lax.all_to_all(d_near, 'ep', 0, 0, tiled=True), axis=0)
        d_gates = jnp.sum(lax.all_to_all(d_gate_near, 'ep', 0, 0, tiled=True), axis=0)
        d_x, dense_grads = dense_backward(saved_state, x_rows, dy_rows, d_gates, d_normed2_moe, norm1_gain, norm2_gain, w_qkv, w_attn_out, w_router)
        gain_cols = jnp.zeros((model_width, 128), F32).at[:, 0].set(dense_grads[0]).at[:, 1].set(dense_grads[1])
        packed = jnp.concatenate(dense_grads[2:] + (gain_cols,), axis=1)
        packed, gates_all = lax.optimization_barrier((packed, gates_all))
        expert_grads = weight_grads(positions, local_idx, gates_all, rows_all, dy_all, w_gate, w_up, w_down, capacity)
        packed = lax.psum(packed, ('dp', 'ep'))
        qkv_end = w_qkv.shape[1]
        out_end = qkv_end + w_attn_out.shape[1]
        router_end = out_end + num_experts
        dense_out = (packed[:, router_end], packed[:, router_end + 1], packed[:, :qkv_end], packed[:, qkv_end:out_end], packed[:, out_end:router_end])
        return (d_x.reshape(x_tokens.shape),) + dense_out + tuple(expert_grads)

    return jax.shard_map(local_step, mesh=mesh,
                          in_specs=(tok_spec, tok_spec, tok_spec, rep_spec, rep_spec, rep_spec, rep_spec, rep_spec, exp_spec, exp_spec, exp_spec),
                          out_specs=(tok_spec, rep_spec, rep_spec, rep_spec, rep_spec, rep_spec, exp_spec, exp_spec, exp_spec),
                          check_vma=False)
```

time: 3190 us -> 1100 us (0.34)
  waiting for transfers between devices: 2340 us -> 445 us
  Pallas kernels: 0 us -> 509 us
  local copies, waits for them, and re-layouts: 436 us -> 27.6 us
  matrix products: 217 us -> 27.4 us
  other arithmetic: 111 us -> 47.6 us
    psum x2 -> x1, waiting for transfers between devices: 2280 us -> 128 us  [local_step(): packed = lax.psum(packed, ('dp', 'ep'))]
    pallas_call x0 -> x2, Pallas kernels: none -> 509 us  [the longest x1 430 us: weight_grads(): pl.pallas_call(functools.partial(weight_grad_kernel, capacity, group, chu...]
    gather x14 -> x0, local copies, waits for them, and re-layouts: 326 us -> none  [the longest x5 208 us: take_rows(): return jnp.take(table, row_ids, axis=0, mode='fill', fill_value=0)]
    all_gather x0 -> x6, waiting for transfers between devices: none -> 274 us  [the longest x1 115 us: local_step(): rows_all = lax.all_gather(normed2, ('dp', 'ep'))]
    dot_general x10 -> x1, matrix products: 193 us -> 2.8 us  [slot_positions(): jnp.einsum('est,tv->esv', member.astype(BF16), before, preferred_element_...]
    unnamed x6 -> x1, other arithmetic: 57.9 us -> 0.01 us
    unnamed x173 -> x77, local copies, waits for them, and re-layouts: 61.5 us -> 5.47 us
    psum x1 -> x0, blocking collectives: 41.7 us -> none  [local_step(): dense_grads = lax.psum(dense_grads, ('dp', 'ep'))]
  transfers between devices with their start and end apart: 6 -> 8, of which waited for: 5 -> 7; matrix products, arithmetic and copies ran while one was open for 9% -> 9% of each run, Pallas kernels for 0% -> 0%
where the time goes in v1:
time: 1100 us; the launch traced here: 1090 us
  Pallas kernels  509 us (46%)
  waiting for transfers between devices  445 us (40%)
  other arithmetic  47.6 us (4%)
  local copies, waits for them, and re-layouts  27.6 us (3%)
  matrix products  27.4 us (2%)
  blocking collectives  15.3 us (1%)
  between operations  15.1 us (1%)
    pallas_call x1, Pallas kernels, weight_grads(): pl.pallas_call(functools.partial(weight_grad_kernel, capacity, group, chu...  430 us
    psum x1, waiting for transfers between devices, local_step(): packed = lax.psum(packed, ('dp', 'ep'))  128 us
    all_gather x1, waiting for transfers between devices, local_step(): rows_all = lax.all_gather(normed2, ('dp', 'ep'))  115 us
    all_gather x1, waiting for transfers between devices, local_step(): dy_all = lax.all_gather(dy_rows, ('dp', 'ep'))  109 us
    pallas_call x1, Pallas kernels, token_grads(): pl.pallas_call(functools.partial(token_grad_kernel, capacity, group), gri...  78.9 us
    all_to_all x1, waiting for transfers between devices, local_step(): lax.all_to_all(d_near, 'ep', 0, 0, tiled=True)  39.3 us
    all_gather x1, waiting for transfers between devices, local_step(): near_rows = lax.all_gather(normed2, 'ep')  24.2 us
    all_gather x1, waiting for transfers between devices, local_step(): idx_all = lax.all_gather(idx_cols, ('dp', 'ep'))  22.5 us
  transfers between devices with their start and end apart: 8, of which 7 were waited for; matrix products, arithmetic and copies ran while one was open for 9% of the time, Pallas kernels for 0%

profile of v1, /device:TPU:0, one launch (start us, length us, event | category | flops | bytes accessed | tf_op | source)
XLA Modules:
  0.0 1091.7 jit_solution(4060330706145483029)
XLA Ops:
  18.1 3.7 fusion.74
  21.9 2.9 divide_convert_fusion
  34.5 2.8 select_reduce_fusion
  37.3 7.4 all_gather.32.gate_ref
  44.7 22.5 %all-gather.16.cloned.1.call-done = s32[256,1024]{1,0:T(8,128)} async-done(((s32[8,1024]{1,0:T(8,128)}), s32[256,1024]{1,0:T(8,128)}) %all-gather.16.cloned.1.call-update) | async-done | bytes 1048592 | tf_op jit(solution)/shard_map/all_gather | solution.py:305
  69.5 11.9 %fusion.1 = pred[32,32,1024]{2,1,0:T(8,128)(4,1)S(1)} fusion(s32[32,8,1024]{2,1,0:T(8,128)S(1)} %subtract_bitcast_fusion.idx_ref), kind=kLoop, calls=%fused_computation.2 | loop fusion | flops 15728640 | bytes 2097152 | tf_op jit(solution)/shard_map/reduce_or | solution.py:74
  81.5 2.8 convert_select_fusion.pos_ref
  87.3 3.0 all-gather.10.cloned.1.call-done.dy_ref
  90.3 24.2 %all-gather.18.cloned.1.call-done = bf16[4096,256]{1,0:T(8,128)(2,1)} async-done(((bf16[1024,256]{1,0:T(8,128)(2,1)}), bf16[4096,256]{1,0:T(8,128)(2,1)}) %all-gather.18.cloned.1.call-update) | async-done | bytes 2097168 | tf_op jit(solution)/shard_map/all_gather | solution.py:309
  114.5 78.9 %expert_token_grads.1 = (f32[4,1024,256]{2,1,0:T(8,128)}, f32[4,8,1024]{2,1,0:T(8,128)}) custom-call(s32[32,4,1024]{2,1,0:T(4,128)} %constant_dynamic-slice_fusion.1.pos_ref, s32[4,8,1024]{2,1,0:T(8,128)} %constant_dynamic-slice_fusion.idx_ref, f32[4,8,1024]{2,1,0:T(8,128)} %all_gather.32.gate_ref, bf16[4,1024,256]{2,1,0:T(8,128)(2,1)} %bitcast.131, ...), custom_call_target="tpu_custom_call" | custom-call | flops 44999999488 | bytes 60000000 | tf_op jit(solution)/shard_map/expert_token_grads/pallas_call | solution.py:174
  193.4 7.9 all_to_all.10
  201.3 4.8 all-to-all-start
  209.0 3.6 select_reduce_fusion.2
  218.0 39.3 %all-to-all-done = f32[4,1024,256]{2,1,0:T(8,128)} async-done(((f32[4,1024,256]{2,1,0:T(8,128)}), f32[4,1024,256]{2,1,0:T(8,128)}, u32[]{:S(2)}, u32[]{:S(2)}) %all-to-all-start) | async-done | bytes 4194336 | tf_op jit(solution)/shard_map/all_to_all | solution.py:316
  257.3 3.6 reduce_sum.178
  260.9 2.4 fusion.33
  268.6 3.4 fusion.7
  280.1 2.2 copy.81
  283.2 2.9 fusion.43
  292.6 2.5 fusion.40
  295.1 128.4 %all-reduce.10.cloned.1.call-done = f32[256,1280]{1,0:T(8,128)} async-done(((f32[256,1280]{1,0:T(8,128)}), f32[256,1280]{1,0:T(8,128)}) %all-reduce.10.cloned.1.call-update) | async-done | bytes 1310736 | tf_op jit(solution)/shard_map/psum | solution.py:323
  430.5 108.9 %all-gather.14.cloned.1.call-done.dy_ref = bf16[32,1024,256]{2,1,0:T(8,128)(2,1)} async-done(((bf16[1,1024,256]{2,1,0:T(8,128)(2,1)}), bf16[32,1024,256]{2,1,0:T(8,128)(2,1)}) %all-gather.14.cloned.1.call-update) | async-done | bytes 16777232 | tf_op jit(solution)/shard_map/all_gather | solution.py:304
  539.5 115.4 %all-gather.20.cloned.1.call-done = bf16[32768,256]{1,0:T(8,128)(2,1)} async-done(((bf16[1024,256]{1,0:T(8,128)(2,1)}), bf16[32768,256]{1,0:T(8,128)(2,1)}) %all-gather.20.cloned.1.call-update) | async-done | bytes 16777232 | tf_op jit(solution)/shard_map/all_gather | solution.py:311
  654.9 429.7 %expert_weight_grads.1 = (f32[32,256,768]{2,1,0:T(8,128)}, f32[32,256,768]{2,1,0:T(8,128)}, f32[32,768,256]{2,1,0:T(8,128)}) custom-call(s32[32,32,1024]{2,1,0:T(8,128)} %copy-done.30, s32[32,8,1024]{2,1,0:T(8,128)} %copy-done.3, f32[32,8,1024]{2,1,0:T(8,128)} %all-gather.12.cloned.1.call-done.gate_ref, bf16[32,1024,256]{2,1,0:T(8,128)(2,1)} %bitcast.130, ...), custom_call_target="tpu_custom_call" | custom-call | flops 280000004096 | bytes 150000000 | tf_op jit(solution)/shard_map/expert_weight_grads/pallas_call | solution.py:245
  (159 shorter events, 61.4 us)
Async XLA Ops:
  7.2 60.0 %all-gather.16.cloned.1.call-start = ((), (), s32[]{:S(2)}) async-start(), calls=%async_computation.6 | async-start | bytes 1081344 | tf_op jit(solution)/shard_map/all_gather | solution.py:305
  7.9 82.4 %all-gather.10.cloned.1.call-start = ((), (), s32[]{:S(2)}) async-start(), calls=%async_computation.2 | async-start | bytes 2621440 | tf_op jit(solution)/shard_map/all_gather | solution.py:315
  8.7 105.8 %all-gather.18.cloned.1.call-start = ((), (), s32[]{:S(2)}) async-start(), calls=%async_computation.7 | async-start | bytes 2621440 | tf_op jit(solution)/shard_map/all_gather | solution.py:309
  8.8 9.3 copy-start.19
  9.5 8.2 copy-start.36
  11.3 6.4 copy-start.12
  12.0 17.8 %copy-start.34 = (f32[256]{0:T(256)}, f32[256]{0:T(256)S(1)}, u32[]{:S(2)}) copy-start(f32[256]{0:T(256)S(1)} %convert_element_type.135) | copy-start | bytes 3076
  21.9 186.5 %copy-start.31 = (f32[2,2,512]{2,1,0:T(2,128)}, f32[2,2,512]{2,1,0:T(2,128)S(1)}, u32[]{:S(2)}) copy-start(f32[2,2,512]{2,1,0:T(2,128)S(1)} %get-tuple-element.75) | copy-start | bytes 24580
  24.8 6.2 copy-start.18
  26.5 8.0 copy-start.16
  37.3 47.0 %copy-start.17 = (f32[1,8,1024]{2,1,0:T(8,128)}, f32[1,8,1024]{2,1,0:T(8,128)S(1)}, u32[]{:S(2)}) copy-start(f32[1,8,1024]{2,1,0:T(8,128)S(1)} %bitcast_divide_fusion) | copy-start | bytes 98308
  201.3 56.1 %all-to-all-start = ((f32[4,1024,256]{2,1,0:T(8,128)}), f32[4,1024,256]{2,1,0:T(8,128)}, u32[]{:S(2)}, u32[]{:S(2)}) async-start(f32[4,1024,256]{2,1,0:T(8,128)} %get-tuple-element.40), calls=%async_computation | async-start | bytes 8388608 | tf_op jit(solution)/shard_map/all_to_all | solution.py:316
  206.1 10.9 %copy-start.2 = (bf16[1024,256]{1,0:T(8,128)(2,1)S(1)}, bf16[1024,256]{1,0:T(8,128)(2,1)}, u32[]{:S(2)}) copy-start(bf16[1024,256]{1,0:T(8,128)(2,1)} %fusion.26) | copy-start | bytes 1572868
  206.1 85.1 %all-gather.12.cloned.1.call-start = ((), (), s32[]{:S(2)}) async-start(), calls=%async_computation.3 | async-start | bytes 1081344 | tf_op jit(solution)/shard_map/all_gather | solution.py:312
  206.7 216.8 %all-reduce.10.cloned.1.call-start = ((), (), s32[]{:S(2)}) async-start(), calls=%async_computation.4 | async-start | bytes 2621440 | tf_op jit(solution)/shard_map/psum | solution.py:323
  217.0 43.9 %copy-start.5 = (bf16[1024,256]{1,0:T(8,128)(2,1)S(1)}, bf16[1024,256]{1,0:T(8,128)(2,1)}, u32[]{:S(2)}) copy-start(bf16[1024,256]{1,0:T(8,128)(2,1)} %copy-done.4) | copy-start | bytes 1572868
  218.0 45.3 %copy-start.33 = (f32[1024]{0:T(1024)S(1)}, f32[1024]{0:T(1024)}, u32[]{:S(2)}) copy-start(f32[1024]{0:T(1024)} %get-tuple-element.71) | copy-start | bytes 12292
  264.9 7.1 copy-start.6
  283.2 5.9 copy-start.7
  283.2 5.9 copy-start.15
  283.2 6.3 copy-start.11
  283.2 6.9 copy-start.14
  291.3 248.2 %all-gather.14.cloned.1.call-start = ((), (), s32[]{:S(2)}) async-start(), calls=%async_computation.5 | async-start | bytes 17301504 | tf_op jit(solution)/shard_map/all_gather | solution.py:304
  291.8 363.1 %all-gather.20.cloned.1.call-start = ((), (), s32[]{:S(2)}) async-start(), calls=%async_computation.8 | async-start | bytes 17301504 | tf_op jit(solution)/shard_map/all_gather | solution.py:311
  (22 other events, 63.9 us)
Sparse Core Ops, SparseCore 0:
  10.8 56.3 all-gather.15
  68.8 21.5 all-gather.9
  91.9 22.5 all-gather.17
  209.5 56.8 all-gather.11
  291.4 132.0 all-reduce.9
  426.2 113.2 all-gather.13
  542.3 112.5 all-gather.19

commit v2 on v1

--- a/solution.py
+++ b/solution.py
@@ -89,18 +89,6 @@
     return lax.dot_general(left, right, (((0,), (0,)), ((), ())), preferred_element_type=F32)
 
 
-def select_slots(capacity, group, pos_ref, idx_ref, gate_ref, source, first):
-    num_tokens = pos_ref.shape[-1]
-    slot_iota = lax.broadcasted_iota(jnp.int32, (capacity, num_tokens), 0)
-    selectors, gate_cols = [], []
-    for member in range(group):
-        hit = slot_iota == pos_ref[member, pl.ds(source, 1), :]
-        gate_row = jnp.sum(jnp.where(idx_ref[source] == first + member, gate_ref[source], 0.0), axis=0, keepdims=True)
-        gate_cols.append(jnp.sum(jnp.where(hit, gate_row, 0.0), axis=1, keepdims=True))
-        selectors.append(jnp.where(hit, 1.0, 0.0).astype(BF16))
-    return jnp.concatenate(selectors, axis=0), jnp.concatenate(gate_cols, axis=0)
-
-
 def swiglu_bwd(act_gate, act_up, d_hidden):
     sig = 0.5 * jnp.tanh(0.5 * act_gate) + 0.5
     silu = act_gate * sig
@@ -111,38 +99,54 @@
 
 
 def token_grad_kernel(capacity, group, pos_ref, idx_ref, gate_ref, rows_ref, dy_ref, w_gate_ref, w_up_ref, w_down_ref,
-                      d_rows_ref, d_gates_ref, select_scr, in_scr, raw_scr, dout_scr, din_scr):
-    sources = rows_ref.shape[0]
-    num_tokens = rows_ref.shape[1]
+                      d_rows_ref, d_gates_ref, slot_gate_ref, select_scr, in_scr, raw_scr, dout_scr, din_scr):
+    sources, num_tokens, _ = rows_ref.shape
     first = pl.program_id(0) * group
+    slot_iota = lax.broadcasted_iota(jnp.int32, (capacity, num_tokens), 0)
+    diagonal = lax.broadcasted_iota(jnp.int32, (capacity, 128), 0) == lax.broadcasted_iota(jnp.int32, (capacity, 128), 1)
 
     @pl.when(pl.program_id(0) == 0)
     def _():
         d_rows_ref[...] = jnp.zeros_like(d_rows_ref)
         d_gates_ref[...] = jnp.zeros_like(d_gates_ref)
 
-    @pl.loop(0, sources)
-    def _(source):
-        selector, gate_col = select_slots(capacity, group, pos_ref, idx_ref, gate_ref, source, first)
+    def select(source):
+        selectors, gate_cols = [], []
+        for member in range(group):
+            hit = slot_iota == pos_ref[member, source:source + 1, :]
+            gate_row = jnp.sum(jnp.where(idx_ref[source] == first + member, gate_ref[source], 0.0), axis=0, keepdims=True)
+            gate_col = jnp.sum(jnp.where(hit, gate_row, 0.0), axis=1, keepdims=True)
+            slot_gate_ref[member, source:source + 1, :] = jnp.sum(jnp.where(diagonal, gate_col, 0.0), axis=0, keepdims=True)
+            gate_cols.append(gate_col)
+            selectors.append(jnp.where(hit, 1.0, 0.0).astype(BF16))
+        return jnp.concatenate(selectors, axis=0), jnp.concatenate(gate_cols, axis=0)
+
+    ahead = select(0)
+    for source in range(sources):
+        selector, gate_col = ahead
+        if source + 1 < sources:
+            ahead = select(source + 1)
         select_scr[source] = selector
         slot_rows = mat_nn(selector, rows_ref[source]).astype(BF16)
-        raw_dy = mat_nn(selector, dy_ref[source])
+        raw_dy = mat_nn(selector, dy_ref[source, :num_tokens])
         scaled_dy = (raw_dy * gate_col).astype(BF16)
         raw_dy = raw_dy.astype(BF16)
         for member in range(group):
-            span = pl.ds(source * capacity, capacity)
+            span = slice(source * capacity, (source + 1) * capacity)
             part = slice(member * capacity, (member + 1) * capacity)
             in_scr[member, span] = slot_rows[part]
             raw_scr[member, span] = raw_dy[part]
             dout_scr[member, span] = scaled_dy[part]
 
-    slot_iota = lax.broadcasted_iota(jnp.int32, (capacity, num_tokens), 0)
+    def forward(member):
+        slot_rows = in_scr[member]
+        return mat_nn(slot_rows, w_gate_ref[member]), mat_nn(slot_rows, w_up_ref[member]), mat_nt(dout_scr[member], w_down_ref[member])
+
+    ahead = forward(0)
     for member in range(group):
-        slot_rows = in_scr[member]
-        d_out = dout_scr[member]
-        act_gate = mat_nn(slot_rows, w_gate_ref[member])
-        act_up = mat_nn(slot_rows, w_up_ref[member])
-        d_hidden = mat_nt(d_out, w_down_ref[member])
+        act_gate, act_up, d_hidden = ahead
+        if member + 1 < group:
+            ahead = forward(member + 1)
         hidden, d_act_gate, d_act_up = swiglu_bwd(act_gate, act_up, d_hidden)
         expert_out = mat_nn(hidden, w_down_ref[member]).astype(BF16)
         d_gate = jnp.sum(raw_scr[member].astype(F32) * expert_out.astype(F32), axis=1, keepdims=True)
@@ -154,15 +158,14 @@
             d_gate_row = jnp.sum(jnp.where(hit, d_gate[part], 0.0), axis=0, keepdims=True)
             d_gates_ref[source] += jnp.where(idx_ref[source] == first + member, d_gate_row, 0.0)
 
-    @pl.loop(0, sources)
-    def _(source):
+    for source in range(sources):
         d_rows_ref[source] += mat_tn(select_scr[source], din_scr[source])
 
 
 def token_grads(positions, local_idx, gates, rows, dy_rows, w_gate, w_up, w_down, capacity):
     group = 4
     sources, num_tokens, width = rows.shape
-    num_experts, _, _ = w_gate.shape
+    num_experts = w_gate.shape[0]
     slots = sources * capacity
 
     def whole(arr):
@@ -171,13 +174,14 @@
     def per_step(arr):
         return pl.BlockSpec((group,) + arr.shape[1:], lambda step: (step, 0, 0))
 
+    slot_gates = jax.ShapeDtypeStruct((num_experts, sources, 128), F32)
     return pl.pallas_call(
         functools.partial(token_grad_kernel, capacity, group),
         grid=(num_experts // group,),
         in_specs=[per_step(positions), whole(local_idx), whole(gates), whole(rows), whole(dy_rows),
                   per_step(w_gate), per_step(w_up), per_step(w_down)],
-        out_specs=[pl.BlockSpec(rows.shape, lambda step: (0, 0, 0)), pl.BlockSpec(gates.shape, lambda step: (0, 0, 0))],
-        out_shape=[jax.ShapeDtypeStruct(rows.shape, F32), jax.ShapeDtypeStruct(gates.shape, F32)],
+        out_specs=[pl.BlockSpec(rows.shape, lambda step: (0, 0, 0)), pl.BlockSpec(gates.shape, lambda step: (0, 0, 0)), per_step(slot_gates)],
+        out_shape=[jax.ShapeDtypeStruct(rows.shape, F32), jax.ShapeDtypeStruct(gates.shape, F32), slot_gates],
         scratch_shapes=[pltpu.VMEM((sources, group * capacity, num_tokens), BF16),
                         pltpu.VMEM((group, slots, width), BF16), pltpu.VMEM((group, slots, width), BF16),
                         pltpu.VMEM((group, slots, width), BF16), pltpu.VMEM((sources, group * capacity, width), BF16)],
@@ -187,24 +191,149 @@
     )(positions, local_idx, gates, rows, dy_rows, w_gate, w_up, w_down)
 
 
-def weight_grad_kernel(capacity, group, chunk, pos_ref, idx_ref, gate_ref, rows_ref, dy_ref, w_gate_ref, w_up_ref, w_down_ref,
+def near_peers():
+    ep = lax.axis_index('ep')
+    return {'ep': ep + 1 - 2 * lax.rem(ep, 2)}, {'ep': lax.rem(ep + 2, 4)}
+
+
+def meet(peers):
+    barrier = pltpu.get_barrier_semaphore()
+    for peer in peers:
+        pl.semaphore_signal(barrier, inc=1, device_id=peer, device_id_type=pl.DeviceIdType.MESH)
+    pl.semaphore_wait(barrier, len(peers))
+
+
+def remote(src, dst, send_sem, recv_sem, peer):
+    return pltpu.make_async_remote_copy(src_ref=src, dst_ref=dst, send_sem=send_sem, recv_sem=recv_sem,
+                                        device_id=peer, device_id_type=pl.DeviceIdType.MESH)
+
+
+def near_gather_kernel(rows_ref, gates_ref, rows_out, gates_out, send_sem, recv_sem):
+    core_peer, chip_peer = near_peers()
+    meet((core_peer, chip_peer))
+    half = rows_ref.shape[0] // 2
+    pieces = [(rows_ref.at[pl.ds(0, half)], lambda slot: rows_out.at[slot, pl.ds(0, half)]),
+              (rows_ref.at[pl.ds(half, half)], lambda slot: rows_out.at[slot, pl.ds(half, half)]),
+              (gates_ref, lambda slot: gates_out.at[slot])]
+    across = [remote(src, place(2), send_sem.at[0, i], recv_sem.at[0, i], chip_peer) for i, (src, place) in enumerate(pieces)]
+    beside = [remote(src, place(1), send_sem.at[1, i], recv_sem.at[1, i], core_peer) for i, (src, place) in enumerate(pieces)]
+    onward = [remote(place(2), place(3), send_sem.at[2, i], recv_sem.at[2, i], core_peer) for i, (_, place) in enumerate(pieces)]
+    for copy in across + beside:
+        copy.start()
+    rows_out[0] = rows_ref[...]
+    gates_out[0] = gates_ref[...]
+    for copy, forward in zip(across, onward):
+        copy.wait_recv()
+        forward.start()
+    for copy in beside + onward:
+        copy.wait()
+    for copy in across:
+        copy.wait_send()
+
+
+def near_gather(rows, gates):
+    vmem = pl.BlockSpec(memory_space=pltpu.VMEM)
+    return pl.pallas_call(
+        near_gather_kernel,
+        in_specs=[vmem, vmem], out_specs=[vmem, vmem],
+        out_shape=[jax.ShapeDtypeStruct((4,) + rows.shape, rows.dtype), jax.ShapeDtypeStruct((4,) + gates.shape, gates.dtype)],
+        scratch_shapes=[pltpu.SemaphoreType.DMA((3, 3)), pltpu.SemaphoreType.DMA((3, 3))],
+        compiler_params=pltpu.CompilerParams(collective_id=0, has_side_effects=True),
+        cost_estimate=pl.CostEstimate(flops=10_000_000_000, bytes_accessed=10_000_000, transcendentals=0),
+        name="near_gather",
+    )(rows, gates)
+
+
+def near_return_kernel(d_rows_ref, d_gates_ref, slot_gates_ref, rows_out, gates_out, slot_gates_out,
+                       own_rows, pass_rows, sum_rows, last_rows, own_gates, pass_gates, sum_gates, last_gates,
+                       send_sem, recv_sem, far_send_sem, far_recv_sem):
+    core_peer, chip_peer = near_peers()
+    dp = lax.axis_index('dp')
+    dp_size = slot_gates_out.shape[0]
+    far_peers = [{'dp': lax.rem(dp + k, dp_size)} for k in range(1, dp_size)]
+    meet([core_peer, chip_peer] + far_peers)
+    first = [remote(d_rows_ref.at[3], pass_rows, send_sem.at[0], recv_sem.at[0], core_peer),
+             remote(d_gates_ref.at[3], pass_gates, send_sem.at[1], recv_sem.at[1], core_peer)]
+    second = [remote(d_rows_ref.at[1], own_rows, send_sem.at[2], recv_sem.at[2], core_peer),
+              remote(d_gates_ref.at[1], own_gates, send_sem.at[3], recv_sem.at[3], core_peer)]
+    third = [remote(sum_rows, last_rows, send_sem.at[4], recv_sem.at[4], chip_peer),
+             remote(sum_gates, last_gates, send_sem.at[5], recv_sem.at[5], chip_peer)]
+    far = [remote(slot_gates_ref, slot_gates_out.at[dp], far_send_sem.at[k], far_recv_sem.at[k], peer) for k, peer in enumerate(far_peers)]
+    for copy in first + second:
+        copy.start()
+    for copy in first:
+        copy.wait_recv()
+    sum_rows[...] = d_rows_ref[2] + pass_rows[...]
+    sum_gates[...] = d_gates_ref[2] + pass_gates[...]
+    for copy in second:
+        copy.wait_recv()
+    rows_out[...] = d_rows_ref[0] + own_rows[...]
+    gates_out[...] = d_gates_ref[0] + own_gates[...]
+    for copy in third + far:
+        copy.start()
+    slot_gates_out[dp] = slot_gates_ref[...]
+    for copy in third:
+        copy.wait_recv()
+    rows_out[...] += last_rows[...]
+    gates_out[...] += last_gates[...]
+    for copy in far:
+        copy.wait()
+    for copy in first + second + third:
+        copy.wait_send()
+
+
+def near_return(d_rows, d_gates, slot_gates, dp_size):
+    vmem = pl.BlockSpec(memory_space=pltpu.VMEM)
+    rows = jax.ShapeDtypeStruct(d_rows.shape[1:], F32)
+    gates = jax.ShapeDtypeStruct(d_gates.shape[1:], F32)
+    return pl.pallas_call(
+        near_return_kernel,
+        in_specs=[vmem] * 3, out_specs=[vmem] * 3,
+        out_shape=[rows, gates, jax.ShapeDtypeStruct((dp_size,) + slot_gates.shape, F32)],
+        scratch_shapes=[pltpu.VMEM(rows.shape, F32)] * 4 + [pltpu.VMEM(gates.shape, F32)] * 4
+        + [pltpu.SemaphoreType.DMA((6,)), pltpu.SemaphoreType.DMA((6,)), pltpu.SemaphoreType.DMA((dp_size - 1,)), pltpu.SemaphoreType.DMA((dp_size - 1,))],
+        compiler_params=pltpu.CompilerParams(collective_id=1, has_side_effects=True, vmem_limit_bytes=40_000_000),
+        cost_estimate=pl.CostEstimate(flops=15_000_000_000, bytes_accessed=20_000_000, transcendentals=0),
+        name="near_return",
+    )(d_rows, d_gates, slot_gates)
+
+
+def weight_grad_kernel(capacity, group, chunk, pos_ref, slot_gate_ref, rows_ref, dy_ref, w_gate_ref, w_up_ref, w_down_ref,
                        d_w_gate_ref, d_w_up_ref, d_w_down_ref, in_scr, dout_scr, down_scr):
     expert = pl.program_id(0)
     member = lax.rem(expert, group)
-    sources = rows_ref.shape[0]
+    sources, num_tokens, _ = rows_ref.shape
+    ep = lax.axis_index('ep')
+    slot_iota = lax.broadcasted_iota(jnp.int32, (capacity, num_tokens), 0)
+    diagonal = lax.broadcasted_iota(jnp.int32, (capacity, 128), 0) == lax.broadcasted_iota(jnp.int32, (capacity, 128), 1)
+
+    def select(source):
+        gate_at = source - lax.rem(source, 4) + jnp.bitwise_xor(lax.rem(source, 4), ep)
+        selectors, gate_cols = [], []
+        for k in range(group):
+            selectors.append(jnp.where(slot_iota == pos_ref[k, pl.ds(source, 1), :], 1.0, 0.0).astype(BF16))
+            gate_cols.append(jnp.sum(jnp.where(diagonal, slot_gate_ref[k, pl.ds(gate_at, 1), :], 0.0), axis=1, keepdims=True))
+        return jnp.concatenate(selectors, axis=0), jnp.concatenate(gate_cols, axis=0)
 
     @pl.when(member == 0)
     def _():
-        @pl.loop(0, sources)
-        def _(source):
-            selector, gate_col = select_slots(capacity, group, pos_ref, idx_ref, gate_ref, source, expert)
-            slot_rows = mat_nn(selector, rows_ref[source]).astype(BF16)
-            scaled_dy = (mat_nn(selector, dy_ref[source]) * gate_col).astype(BF16)
-            for k in range(group):
-                span = pl.ds(source * capacity, capacity)
-                part = slice(k * capacity, (k + 1) * capacity)
-                in_scr[k, span] = slot_rows[part]
-                dout_scr[k, span] = scaled_dy[part]
+        unroll = 2
+
+        @pl.loop(0, sources // unroll)
+        def _(step):
+            ahead = select(step * unroll)
+            for j in range(unroll):
+                source = step * unroll + j
+                selector, gate_col = ahead
+                if j + 1 < unroll:
+                    ahead = select(source + 1)
+                slot_rows = mat_nn(selector, rows_ref[source]).astype(BF16)
+                scaled_dy = (mat_nn(selector, dy_ref[source, :num_tokens]) * gate_col).astype(BF16)
+                for k in range(group):
+                    span = pl.ds(source * capacity, capacity)
+                    part = slice(k * capacity, (k + 1) * capacity)
+                    in_scr[k, span] = slot_rows[part]
+                    dout_scr[k, span] = scaled_dy[part]
 
     d_w_gate_ref[...] = jnp.zeros_like(d_w_gate_ref)
     d_w_up_ref[...] = jnp.zeros_like(d_w_up_ref)
@@ -229,7 +358,7 @@
     d_w_down_ref[0] = down_scr[...].T
 
 
-def weight_grads(positions, local_idx, gates, rows, dy_rows, w_gate, w_up, w_down, capacity):
+def weight_grads(positions, slot_gates, rows, dy_rows, w_gate, w_up, w_down, capacity):
     group = 4
     chunk = 256
     sources, num_tokens, width = rows.shape
@@ -245,7 +374,8 @@
     return pl.pallas_call(
         functools.partial(weight_grad_kernel, capacity, group, chunk),
         grid=(num_experts,),
-        in_specs=[pl.BlockSpec((group, sources, num_tokens), lambda step: (step // group, 0, 0)), whole(local_idx), whole(gates),
+        in_specs=[pl.BlockSpec((group, sources, num_tokens), lambda step: (step // group, 0, 0)),
+                  pl.BlockSpec((group, sources, 128), lambda step: (step // group, 0, 0)),
                   whole(rows), whole(dy_rows), per_step(w_gate), per_step(w_up), per_step(w_down)],
         out_specs=[per_step(w_gate), per_step(w_up), per_step(w_down)],
         out_shape=[jax.ShapeDtypeStruct(arr.shape, F32) for arr in (w_gate, w_up, w_down)],
@@ -253,7 +383,7 @@
         compiler_params=pltpu.CompilerParams(vmem_limit_bytes=67_000_000, dimension_semantics=("arbitrary",)),
         cost_estimate=pl.CostEstimate(flops=280_000_000_000, bytes_accessed=150_000_000, transcendentals=0),
         name="expert_weight_grads",
-    )(positions, local_idx, gates, rows, dy_rows, w_gate, w_up, w_down)
+    )(positions, slot_gates, rows, dy_rows, w_gate, w_up, w_down)
 
 
 def dense_forward(x_rows, idx_cols, num_seqs, norm1_gain, norm2_gain, w_qkv, w_attn_out, w_router):
@@ -301,25 +431,29 @@
         x_rows = x_tokens.reshape(num_tokens, model_width)
         dy_rows = dy_tokens.reshape(num_tokens, model_width)
         idx_cols = route_idx.reshape(num_tokens, top_k).T
-        dy_all = lax.all_gather(dy_rows, ('dp', 'ep'))
-        idx_all = lax.all_gather(idx_cols, ('dp', 'ep'))
-        local_idx = idx_all - lax.axis_index('ep') * local_experts
-        positions = slot_positions(local_idx, local_experts, capacity)
+        routes = idx_cols.astype(BF16).reshape(-1, model_width)
+        payload = jnp.concatenate([dy_rows, routes], axis=0)
+        dy_all = lax.all_gather(payload, ('dp', 'ep'))
+        moved = [lax.ppermute(payload, 'ep', [(i, i ^ k) for i in range(ep_size)]) for k in range(1, ep_size)]
+        dy_near = jnp.stack([payload] + moved)
+
+        def expert_of(gathered):
+            return gathered[:, num_tokens:].reshape(-1, top_k, num_tokens).astype(jnp.int32) - lax.axis_index('ep') * local_experts
+
+        idx_near = expert_of(dy_near)
+        positions_near = slot_positions(idx_near, local_experts, capacity)
         normed2, gate_vals, saved_state = dense_forward(x_rows, idx_cols, num_seqs, norm1_gain, norm2_gain, w_qkv, w_attn_out, w_router)
-        near_rows = lax.all_gather(normed2, 'ep')
-        near_gates = lax.all_gather(gate_vals, 'ep')
         rows_all = lax.all_gather(normed2, ('dp', 'ep'))
-        gates_all = lax.all_gather(gate_vals, ('dp', 'ep'))
-        near = lax.axis_index('dp') * ep_size
-        d_near, d_gate_near = token_grads(lax.dynamic_slice_in_dim(positions, near, ep_size, 1), lax.dynamic_slice_in_dim(local_idx, near, ep_size, 0),
-                                          near_gates, near_rows, lax.all_gather(dy_rows, 'ep'), w_gate, w_up, w_down, capacity)
-        d_normed2_moe = jnp.sum(lax.all_to_all(d_near, 'ep', 0, 0, tiled=True), axis=0)
-        d_gates = jnp.sum(lax.all_to_all(d_gate_near, 'ep', 0, 0, tiled=True), axis=0)
+        rows_near, gates_near = near_gather(normed2, gate_vals)
+        d_near, d_gate_near, slot_gates = token_grads(positions_near, idx_near, gates_near, rows_near, dy_near, w_gate, w_up, w_down, capacity)
+        d_normed2_moe, d_gates, slot_gates_all = near_return(d_near, d_gate_near, slot_gates, mesh.shape['dp'])
+        slot_gates_all = slot_gates_all.transpose(1, 0, 2, 3).reshape(local_experts, -1, 128)
         d_x, dense_grads = dense_backward(saved_state, x_rows, dy_rows, d_gates, d_normed2_moe, norm1_gain, norm2_gain, w_qkv, w_attn_out, w_router)
         gain_cols = jnp.zeros((model_width, 128), F32).at[:, 0].set(dense_grads[0]).at[:, 1].set(dense_grads[1])
         packed = jnp.concatenate(dense_grads[2:] + (gain_cols,), axis=1)
-        packed, gates_all = lax.optimization_barrier((packed, gates_all))
-        expert_grads = weight_grads(positions, local_idx, gates_all, rows_all, dy_all, w_gate, w_up, w_down, capacity)
+        packed, slot_gates_all = lax.optimization_barrier((packed, slot_gates_all))
+        positions = slot_positions(expert_of(dy_all), local_experts, capacity)
+        expert_grads = weight_grads(positions, slot_gates_all, rows_all, dy_all, w_gate, w_up, w_down, capacity)
         packed = lax.psum(packed, ('dp', 'ep'))
         qkv_end = w_qkv.shape[1]
         out_end = qkv_end + w_attn_out.shape[1]

time: 1100 us -> 980 us (0.89)
  waiting for transfers between devices: 445 us -> 337 us
  blocking collectives: 15.3 us -> 0 us
    pallas_call x0 -> x2, Pallas kernels: none -> 53.3 us  [the longest x1 34.7 us: near_return(): pl.pallas_call(near_return_kernel, in_specs=[vmem] * 3, out_specs=[vmem]...]
    pallas_call x1, Pallas kernels: 430 us -> 378 us  [weight_grads(): pl.pallas_call(functools.partial(weight_grad_kernel, capacity, group, chu...]
    all_gather x5 -> x1, waiting for transfers between devices: 159 us -> 112 us  [local_step(): dy_all = lax.all_gather(payload, ('dp', 'ep'))]
    all_to_all x1 -> x0, waiting for transfers between devices: 39.3 us -> none  [local_step(): lax.all_to_all(d_near, 'ep', 0, 0, tiled=True)]
    all_gather x1, waiting for transfers between devices: 115 us -> 97.2 us  [local_step(): rows_all = lax.all_gather(normed2, ('dp', 'ep'))]
  transfers between devices with their start and end apart: 8 -> 6, of which waited for: 7 -> 3; matrix products, arithmetic and copies ran while one was open for 9% -> 6% of each run, Pallas kernels for 0% -> 2%
where the time goes in v2:
time: 980 us; the launch traced here: 971 us
  Pallas kernels  506 us (52%)
  waiting for transfers between devices  337 us (34%)
  other arithmetic  51.4 us (5%)
  matrix products  30 us (3%)
  local copies, waits for them, and re-layouts  29.5 us (3%)
  between operations  14.7 us (2%)
    pallas_call x1, Pallas kernels, weight_grads(): pl.pallas_call(functools.partial(weight_grad_kernel, capacity, group, chu...  378 us
    psum x1, waiting for transfers between devices, local_step(): packed = lax.psum(packed, ('dp', 'ep'))  127 us
    all_gather x1, waiting for transfers between devices, local_step(): dy_all = lax.all_gather(payload, ('dp', 'ep'))  112 us
    all_gather x1, waiting for transfers between devices, local_step(): rows_all = lax.all_gather(normed2, ('dp', 'ep'))  97.2 us
    pallas_call x1, Pallas kernels, token_grads(): pl.pallas_call(functools.partial(token_grad_kernel, capacity, group), gri...  74.9 us
    pallas_call x1, Pallas kernels, near_return(): pl.pallas_call(near_return_kernel, in_specs=[vmem] * 3, out_specs=[vmem]...  34.7 us
  transfers between devices with their start and end apart: 6, of which 3 were waited for; matrix products, arithmetic and copies ran while one was open for 6% of the time, Pallas kernels for 2%

profile of v2, /device:TPU:0, one launch (start us, length us, event | category | flops | bytes accessed | tf_op | source)
XLA Modules:
  0.0 971.4 jit_solution(6564114178106700874)
XLA Ops:
  8.0 2.1 fusion.76
  10.1 2.4 collective-permute-start.2
  24.2 4.9 fusion.79
  29.1 2.8 divide_convert_fusion
  39.2 2.8 select_reduce_fusion
  42.6 18.6 %near_gather.1 = (bf16[4,1024,256]{2,1,0:T(8,128)(2,1)}, f32[4,8,1024]{2,1,0:T(8,128)}) custom-call(bf16[1024,256]{1,0:T(8,128)(2,1)} %copy-done.7, f32[8,1024]{1,0:T(8,128)} %broadcast_divide_fusion.gates_ref), custom_call_target="tpu_custom_call" | custom-call | flops 10000000000 | bytes 10000000 | tf_op jit(solution)/shard_map/near_gather/pallas_call | solution.py:236
  66.2 1.8 fusion.8
  69.9 74.9 %expert_token_grads.1 = (f32[4,1024,256]{2,1,0:T(8,128)}, f32[4,8,1024]{2,1,0:T(8,128)}, f32[32,4,128]{2,1,0:T(4,128)}) custom-call(s32[32,4,1024]{2,1,0:T(4,128)} %convert_select_fusion.1.pos_ref, s32[4,8,1024]{2,1,0:T(8,128)} %copy-done.25, f32[4,8,1024]{2,1,0:T(8,128)} %get-tuple-element.46.gate_ref, bf16[4,1024,256]{2,1,0:T(8,128)(2,1)} %get-tuple-element.47.rows_ref, ...), custom_call_target="tpu_custom_call" | custom-call | flops 44999999488 | bytes 60000000 | tf_op jit(solution)/shard_map/expert_token_grads/pallas_call | solution.py:178
  144.7 2.2 copy-done
  148.7 34.7 %near_return.1 = (f32[1024,256]{1,0:T(8,128)S(1)}, f32[8,1024]{1,0:T(8,128)S(1)}, f32[8,32,4,128]{3,2,1,0:T(4,128)S(1)}) custom-call(f32[4,1024,256]{2,1,0:T(8,128)S(1)} %copy-done, f32[4,8,1024]{2,1,0:T(8,128)S(1)} %copy-done.1, f32[32,4,128]{2,1,0:T(4,128)S(1)} %copy-done.2), custom_call_target="tpu_custom_call" | custom-call | flops 15000000512 | bytes 20000000 | tf_op jit(solution)/shard_map/near_return/pallas_call | solution.py:289
  183.4 3.6 select_reduce_fusion.2
  187.0 2.0 copy.68
  191.9 1.8 fusion.36
  200.8 3.4 fusion.7
  211.3 2.2 copy.75
  216.0 2.9 fusion.46
  221.3 2.1 pad_maximum_fusion.1
  226.2 126.6 %all-reduce.10.cloned.1.call-done = f32[256,1280]{1,0:T(8,128)} async-done(((f32[256,1280]{1,0:T(8,128)}), f32[256,1280]{1,0:T(8,128)}) %all-reduce.10.cloned.1.call-update) | async-done | bytes 1310736 | tf_op jit(solution)/shard_map/psum | solution.py:457
  356.1 2.1 slice.96
  359.9 111.6 %all-gather.5.cloned.1.call-done = bf16[33792,256]{1,0:T(8,128)(2,1)} async-done(((bf16[1056,256]{1,0:T(8,128)(2,1)}), bf16[33792,256]{1,0:T(8,128)(2,1)}) %all-gather.5.cloned.1.call-update) | async-done | bytes 17301520 | tf_op jit(solution)/shard_map/all_gather | solution.py:436
  473.0 11.9 %fusion.1 = pred[32,32,1024]{2,1,0:T(8,128)(4,1)S(1)} fusion(s32[32,8,1024]{2,1,0:T(8,128)S(1)} %sub.62), kind=kLoop, calls=%fused_computation.2 | loop fusion | flops 15728640 | bytes 2097152 | tf_op jit(solution)/shard_map/reduce_or | solution.py:74
  485.0 4.9 convert_select_fusion.pos_ref
  489.9 97.2 %all-gather.7.cloned.1.call-done = bf16[32768,256]{1,0:T(8,128)(2,1)} async-done(((bf16[1024,256]{1,0:T(8,128)(2,1)}), bf16[32768,256]{1,0:T(8,128)(2,1)}) %all-gather.7.cloned.1.call-update) | async-done | bytes 16777232 | tf_op jit(solution)/shard_map/all_gather | solution.py:446
  587.0 377.6 %expert_weight_grads.1 = (f32[32,256,768]{2,1,0:T(8,128)}, f32[32,256,768]{2,1,0:T(8,128)}, f32[32,768,256]{2,1,0:T(8,128)}) custom-call(s32[32,32,1024]{2,1,0:T(8,128)} %convert_select_fusion.pos_ref, f32[32,32,128]{2,1,0:T(8,128)} %bitcast.123, bf16[32,1024,256]{2,1,0:T(8,128)(2,1)} %bitcast.135, bf16[32,1056,256]{2,1,0:T(8,128)(2,1)} %bitcast.132, ...), custom_call_target="tpu_custom_call" | custom-call | flops 280000004096 | bytes 150000000 | tf_op jit(solution)/shard_map/expert_weight_grads/pallas_call | solution.py:374
  (162 shorter events, 59.6 us)
Async XLA Ops:
  7.2 345.7 %all-reduce.10.cloned.1.call-start = ((), (), s32[]{:S(2)}) async-start(), calls=%async_computation | async-start | bytes 2621440 | tf_op jit(solution)/shard_map/psum | solution.py:457
  10.1 53.0 %collective-permute-start.2 = (bf16[1056,256]{1,0:T(8,128)(2,1)}, bf16[1056,256]{1,0:T(8,128)(2,1)}, u32[]{:S(2)}, u32[]{:S(2)}) collective-permute-start(bf16[1056,256]{1,0:T(8,128)(2,1)} %get-tuple-element.78), channel_id=1, source_target_pairs={{0,3},{1,2},{2,1},{3,0},{4,7},{5,6},{6,5},{7,4},{8,11},{9,10},{10,... | collective-permute-start | bytes 1622024 | tf_op jit(solution)/shard_map/ppermute | solution.py:437
  12.5 50.6 %collective-permute-start.1 = (bf16[1056,256]{1,0:T(8,128)(2,1)}, bf16[1056,256]{1,0:T(8,128)(2,1)}, u32[]{:S(2)}, u32[]{:S(2)}) collective-permute-start(bf16[1056,256]{1,0:T(8,128)(2,1)} %get-tuple-element.78), channel_id=1, source_target_pairs={{0,2},{1,3},{2,0},{3,1},{4,6},{5,7},{6,4},{7,5},{8,10},{9,11},{10,... | collective-permute-start | bytes 1622024 | tf_op jit(solution)/shard_map/ppermute | solution.py:437
  13.1 50.0 %collective-permute-start = (bf16[1056,256]{1,0:T(8,128)(2,1)}, bf16[1056,256]{1,0:T(8,128)(2,1)}, u32[]{:S(2)}, u32[]{:S(2)}) collective-permute-start(bf16[1056,256]{1,0:T(8,128)(2,1)} %get-tuple-element.78), channel_id=1, source_target_pairs={{0,1},{1,0},{2,3},{3,2},{4,5},{5,4},{6,7},{7,6},{8,9},{9,8},{10,11... | collective-permute-start | bytes 1622024 | tf_op jit(solution)/shard_map/ppermute | solution.py:437
  14.6 7.8 copy-start.38
  15.3 22.9 %copy-start.36 = (f32[256]{0:T(256)}, f32[256]{0:T(256)S(1)}, u32[]{:S(2)}) copy-start(f32[256]{0:T(256)S(1)} %convert_element_type.157) | copy-start | bytes 3076
  22.2 9.7 %copy-start.5 = (f32[2,512,3,2,128]{1,4,3,2,0:T(8,128)}, f32[2,512,3,2,128]{1,4,3,2,0:T(8,128)S(1)}, u32[]{:S(2)}) copy-start(f32[2,512,3,2,128]{1,4,3,2,0:T(8,128)S(1)} %fusion.51) | copy-start | bytes 9437188
  29.1 6.7 copy-start.34
  33.3 5.1 copy-start.27
  34.5 4.6 copy-start.26
  37.5 154.3 %copy-start.9 = (bf16[1024,256]{1,0:T(8,128)(2,1)}, bf16[1024,256]{1,0:T(8,128)(2,1)S(1)}, u32[]{:S(2)}) copy-start(bf16[1024,256]{1,0:T(8,128)(2,1)S(1)} %get-tuple-element.92) | copy-start | bytes 1572868
  38.4 4.1 copy-start.7
  42.6 18.6 %copy-start.35 = (f32[1,4,2,128]{3,2,1,0:T(2,128)S(1)}, f32[1,4,2,128]{3,2,1,0:T(2,128)}, u32[]{:S(2)}) copy-start(f32[1,4,2,128]{3,2,1,0:T(2,128)} %get-tuple-element.83) | copy-start | bytes 12292
  42.6 20.6 %copy-start.15 = (bf16[1,1056,256]{2,1,0:T(8,128)(2,1)S(1)}, bf16[1,1056,256]{2,1,0:T(8,128)(2,1)}, u32[]{:S(2)}) copy-start(bf16[1,1056,256]{2,1,0:T(8,128)(2,1)} %get-tuple-element.77) | copy-start | bytes 1622020
  183.4 8.1 copy-start.8
  189.0 4.7 copy-start.16
  190.3 5.2 copy-start.24
  193.7 5.5 copy-start.4
  211.2 4.7 copy-start.39
  215.9 9.0 copy-start.11
  215.9 9.0 copy-start.12
  218.8 6.1 copy-start.22
  223.4 248.2 %all-gather.5.cloned.1.call-start = ((), (), s32[]{:S(2)}) async-start(), calls=%async_computation.1 | async-start | bytes 17842176 | tf_op jit(solution)/shard_map/all_gather | solution.py:436
  224.1 362.9 %all-gather.7.cloned.1.call-start = ((), (), s32[]{:S(2)}) async-start(), calls=%async_computation.2 | async-start | bytes 17301504 | tf_op jit(solution)/shard_map/all_gather | solution.py:446
  (22 other events, 49.2 us)
Sparse Core Ops, SparseCore 0:
  223.5 129.2 all-reduce.9
  355.7 115.7 all-gather.4
  474.4 112.5 all-gather.6

commit v3 on v2

--- a/solution.py
+++ b/solution.py
@@ -89,18 +89,20 @@
     return lax.dot_general(left, right, (((0,), (0,)), ((), ())), preferred_element_type=F32)
 
 
-def swiglu_bwd(act_gate, act_up, d_hidden):
-    sig = 0.5 * jnp.tanh(0.5 * act_gate) + 0.5
-    silu = act_gate * sig
+def swiglu_bwd(half_gate, act_up, d_hidden):
+    twice_sig = 1.0 + jnp.tanh(half_gate)
+    silu = half_gate * twice_sig
     hidden = (silu * act_up).astype(BF16)
     d_act_up = (d_hidden * silu).astype(BF16)
-    d_act_gate = (d_hidden * act_up * (sig + silu * (1.0 - sig))).astype(BF16)
-    return hidden, d_act_gate, d_act_up
-
-
-def token_grad_kernel(capacity, group, pos_ref, idx_ref, gate_ref, rows_ref, dy_ref, w_gate_ref, w_up_ref, w_down_ref,
-                      d_rows_ref, d_gates_ref, slot_gate_ref, select_scr, in_scr, raw_scr, dout_scr, din_scr):
+    twice_d_act_gate = (d_hidden * act_up * (twice_sig + silu * (2.0 - twice_sig))).astype(BF16)
+    return hidden, twice_d_act_gate, d_act_up
+
+
+def token_grad_kernel(capacity, group, f_tile, pos_ref, idx_ref, gate_ref, rows_ref, dy_ref, w_gate_ref, w_up_ref, w_down_ref,
+                      d_rows_ref, d_gates_ref, slot_gate_ref, d_w_gate_ref, d_w_up_ref, d_w_down_ref,
+                      select_scr, in_scr, raw_scr, dout_scr, din_scr):
     sources, num_tokens, _ = rows_ref.shape
+    ff = w_gate_ref.shape[2]
     first = pl.program_id(0) * group
     slot_iota = lax.broadcasted_iota(jnp.int32, (capacity, num_tokens), 0)
     diagonal = lax.broadcasted_iota(jnp.int32, (capacity, 128), 0) == lax.broadcasted_iota(jnp.int32, (capacity, 128), 1)
@@ -138,25 +140,34 @@
             raw_scr[member, span] = raw_dy[part]
             dout_scr[member, span] = scaled_dy[part]
 
-    def forward(member):
+    def forward(member, cols):
         slot_rows = in_scr[member]
-        return mat_nn(slot_rows, w_gate_ref[member]), mat_nn(slot_rows, w_up_ref[member]), mat_nt(dout_scr[member], w_down_ref[member])
-
-    ahead = forward(0)
-    for member in range(group):
-        act_gate, act_up, d_hidden = ahead
-        if member + 1 < group:
-            ahead = forward(member + 1)
-        hidden, d_act_gate, d_act_up = swiglu_bwd(act_gate, act_up, d_hidden)
-        expert_out = mat_nn(hidden, w_down_ref[member]).astype(BF16)
-        d_gate = jnp.sum(raw_scr[member].astype(F32) * expert_out.astype(F32), axis=1, keepdims=True)
-        d_in = (mat_nt(d_act_gate, w_gate_ref[member]) + mat_nt(d_act_up, w_up_ref[member])).astype(BF16)
-        for source in range(sources):
-            part = slice(source * capacity, (source + 1) * capacity)
-            din_scr[source, member * capacity:(member + 1) * capacity] = d_in[part]
-            hit = slot_iota == pos_ref[member, source:source + 1, :]
-            d_gate_row = jnp.sum(jnp.where(hit, d_gate[part], 0.0), axis=0, keepdims=True)
-            d_gates_ref[source] += jnp.where(idx_ref[source] == first + member, d_gate_row, 0.0)
+        half_w_gate = w_gate_ref[member, :, cols] * jnp.asarray(0.5, BF16)
+        return (half_w_gate, mat_nn(slot_rows, half_w_gate), mat_nn(slot_rows, w_up_ref[member, :, cols]),
+                mat_nt(dout_scr[member], w_down_ref[member, cols, :]))
+
+    steps = [(member, slice(f, f + f_tile)) for member in range(group) for f in range(0, ff, f_tile)]
+    ahead = forward(*steps[0])
+    for at, (member, cols) in enumerate(steps):
+        half_w_gate, half_gate, act_up, d_hidden = ahead
+        if at + 1 < len(steps):
+            ahead = forward(*steps[at + 1])
+        hidden, twice_d_act_gate, d_act_up = swiglu_bwd(half_gate, act_up, d_hidden)
+        out_part = mat_nn(hidden, w_down_ref[member, cols, :])
+        in_part = mat_nt(twice_d_act_gate, half_w_gate) + mat_nt(d_act_up, w_up_ref[member, :, cols])
+        d_w_gate_ref[member, :, cols] = 0.5 * mat_tn(in_scr[member], twice_d_act_gate)
+        d_w_up_ref[member, :, cols] = mat_tn(in_scr[member], d_act_up)
+        d_w_down_ref[member, cols, :] = mat_tn(hidden, dout_scr[member])
+        out_sum, in_sum = (out_part, in_part) if cols.start == 0 else (out_sum + out_part, in_sum + in_part)
+        if cols.stop == ff:
+            d_gate = jnp.sum(raw_scr[member].astype(F32) * out_sum.astype(BF16).astype(F32), axis=1, keepdims=True)
+            d_in = in_sum.astype(BF16)
+            for source in range(sources):
+                part = slice(source * capacity, (source + 1) * capacity)
+                din_scr[source, member * capacity:(member + 1) * capacity] = d_in[part]
+                hit = slot_iota == pos_ref[member, source:source + 1, :]
+                d_gate_row = jnp.sum(jnp.where(hit, d_gate[part], 0.0), axis=0, keepdims=True)
+                d_gates_ref[source] += jnp.where(idx_ref[source] == first + member, d_gate_row, 0.0)
 
     for source in range(sources):
         d_rows_ref[source] += mat_tn(select_scr[source], din_scr[source])
@@ -175,18 +186,20 @@
         return pl.BlockSpec((group,) + arr.shape[1:], lambda step: (step, 0, 0))
 
     slot_gates = jax.ShapeDtypeStruct((num_experts, sources, 128), F32)
+    weights = [jax.ShapeDtypeStruct(arr.shape, F32) for arr in (w_gate, w_up, w_down)]
     return pl.pallas_call(
-        functools.partial(token_grad_kernel, capacity, group),
+        functools.partial(token_grad_kernel, capacity, group, 256),
         grid=(num_experts // group,),
         in_specs=[per_step(positions), whole(local_idx), whole(gates), whole(rows), whole(dy_rows),
                   per_step(w_gate), per_step(w_up), per_step(w_down)],
-        out_specs=[pl.BlockSpec(rows.shape, lambda step: (0, 0, 0)), pl.BlockSpec(gates.shape, lambda step: (0, 0, 0)), per_step(slot_gates)],
-        out_shape=[jax.ShapeDtypeStruct(rows.shape, F32), jax.ShapeDtypeStruct(gates.shape, F32), slot_gates],
+        out_specs=[pl.BlockSpec(rows.shape, lambda step: (0, 0, 0)), pl.BlockSpec(gates.shape, lambda step: (0, 0, 0)),
+                   per_step(slot_gates)] + [per_step(arr) for arr in weights],
+        out_shape=[jax.ShapeDtypeStruct(rows.shape, F32), jax.ShapeDtypeStruct(gates.shape, F32), slot_gates] + weights,
         scratch_shapes=[pltpu.VMEM((sources, group * capacity, num_tokens), BF16),
                         pltpu.VMEM((group, slots, width), BF16), pltpu.VMEM((group, slots, width), BF16),
                         pltpu.VMEM((group, slots, width), BF16), pltpu.VMEM((sources, group * capacity, width), BF16)],
-        compiler_params=pltpu.CompilerParams(vmem_limit_bytes=60_000_000, dimension_semantics=("arbitrary",)),
-        cost_estimate=pl.CostEstimate(flops=45_000_000_000, bytes_accessed=60_000_000, transcendentals=0),
+        compiler_params=pltpu.CompilerParams(vmem_limit_bytes=64_000_000, dimension_semantics=("arbitrary",)),
+        cost_estimate=pl.CostEstimate(flops=60_000_000_000, bytes_accessed=130_000_000, transcendentals=0),
         name="expert_token_grads",
     )(positions, local_idx, gates, rows, dy_rows, w_gate, w_up, w_down)
 
@@ -249,7 +262,7 @@
                        send_sem, recv_sem, far_send_sem, far_recv_sem):
     core_peer, chip_peer = near_peers()
     dp = lax.axis_index('dp')
-    dp_size = slot_gates_out.shape[0]
+    dp_size = slot_gates_out.shape[0] + 1
     far_peers = [{'dp': lax.rem(dp + k, dp_size)} for k in range(1, dp_size)]
     meet([core_peer, chip_peer] + far_peers)
     first = [remote(d_rows_ref.at[3], pass_rows, send_sem.at[0], recv_sem.at[0], core_peer),
@@ -258,7 +271,7 @@
               remote(d_gates_ref.at[1], own_gates, send_sem.at[3], recv_sem.at[3], core_peer)]
     third = [remote(sum_rows, last_rows, send_sem.at[4], recv_sem.at[4], chip_peer),
              remote(sum_gates, last_gates, send_sem.at[5], recv_sem.at[5], chip_peer)]
-    far = [remote(slot_gates_ref, slot_gates_out.at[dp], far_send_sem.at[k], far_recv_sem.at[k], peer) for k, peer in enumerate(far_peers)]
+    far = [remote(slot_gates_ref, slot_gates_out.at[dp_size - 2 - k], far_send_sem.at[k], far_recv_sem.at[k], peer) for k, peer in enumerate(far_peers)]
     for copy in first + second:
         copy.start()
     for copy in first:
@@ -271,7 +284,6 @@
     gates_out[...] = d_gates_ref[0] + own_gates[...]
     for copy in third + far:
         copy.start()
-    slot_gates_out[dp] = slot_gates_ref[...]
     for copy in third:
         copy.wait_recv()
     rows_out[...] += last_rows[...]
@@ -289,7 +301,7 @@
     return pl.pallas_call(
         near_return_kernel,
         in_specs=[vmem] * 3, out_specs=[vmem] * 3,
-        out_shape=[rows, gates, jax.ShapeDtypeStruct((dp_size,) + slot_gates.shape, F32)],
+        out_shape=[rows, gates, jax.ShapeDtypeStruct((dp_size - 1,) + slot_gates.shape, F32)],
         scratch_shapes=[pltpu.VMEM(rows.shape, F32)] * 4 + [pltpu.VMEM(gates.shape, F32)] * 4
         + [pltpu.SemaphoreType.DMA((6,)), pltpu.SemaphoreType.DMA((6,)), pltpu.SemaphoreType.DMA((dp_size - 1,)), pltpu.SemaphoreType.DMA((dp_size - 1,))],
         compiler_params=pltpu.CompilerParams(collective_id=1, has_side_effects=True, vmem_limit_bytes=40_000_000),
@@ -298,92 +310,177 @@
     )(d_rows, d_gates, slot_gates)
 
 
-def weight_grad_kernel(capacity, group, chunk, pos_ref, slot_gate_ref, rows_ref, dy_ref, w_gate_ref, w_up_ref, w_down_ref,
-                       d_w_gate_ref, d_w_up_ref, d_w_down_ref, in_scr, dout_scr, down_scr):
+def position_kernel(capacity, num_experts, idx_ref, pos_ref, member_scr):
+    choices, sources, num_tokens = idx_ref.shape
+    block = 256
+
+    @pl.loop(0, num_experts)
+    def _(expert):
+        hit = idx_ref[0] == expert
+        for choice in range(1, choices):
+            hit = hit | (idx_ref[choice] == expert)
+        member_scr[pl.ds(expert * sources, sources)] = jnp.where(hit, 1.0, 0.0).astype(BF16)
+
+    before = jnp.where(lax.broadcasted_iota(jnp.int32, (num_tokens, num_tokens), 0) < lax.broadcasted_iota(jnp.int32, (num_tokens, num_tokens), 1), 1.0, 0.0).astype(BF16)
+
+    @pl.loop(0, num_experts * sources // block)
+    def _(step):
+        span = pl.ds(pl.multiple_of(step * block, block), block)
+        member = member_scr[span]
+        earlier = mat_nn(member, before)
+        pos_ref[span] = jnp.where((member.astype(F32) > 0.5) & (earlier < capacity), earlier, -1.0).astype(jnp.int32)
+
+
+def all_positions(idx_by_choice, num_experts, capacity):
+    _, sources, num_tokens = idx_by_choice.shape
+    flat = pl.pallas_call(
+        functools.partial(position_kernel, capacity, num_experts),
+        out_shape=jax.ShapeDtypeStruct((num_experts * sources, num_tokens), jnp.int32),
+        scratch_shapes=[pltpu.VMEM((num_experts * sources, num_tokens), BF16)],
+        compiler_params=pltpu.CompilerParams(vmem_limit_bytes=32_000_000),
+        cost_estimate=pl.CostEstimate(flops=4_000_000_000, bytes_accessed=5_000_000, transcendentals=0),
+        name="slot_positions",
+    )(idx_by_choice)
+    return flat.reshape(num_experts, sources, num_tokens)
+
+
+def weight_grad_kernel(capacity, group, f_tile, near, chunks, tail, count_ref, place_ref, pos_ref, slot_gate_ref, table_hbm,
+                       w_gate_ref, w_up_ref, w_down_ref, near_gate_ref, near_up_ref, near_down_ref,
+                       d_w_gate_ref, d_w_up_ref, d_w_down_ref, rows_scr, dy_scr, in_scr, dout_scr, down_scr, total_scr, load_sem):
     expert = pl.program_id(0)
     member = lax.rem(expert, group)
-    sources, num_tokens, _ = rows_ref.shape
-    ep = lax.axis_index('ep')
+    far, num_tokens, _ = rows_scr.shape
+    sources = far + near
+    ff = w_gate_ref.shape[2]
     slot_iota = lax.broadcasted_iota(jnp.int32, (capacity, num_tokens), 0)
     diagonal = lax.broadcasted_iota(jnp.int32, (capacity, 128), 0) == lax.broadcasted_iota(jnp.int32, (capacity, 128), 1)
 
-    def select(source):
-        gate_at = source - lax.rem(source, 4) + jnp.bitwise_xor(lax.rem(source, 4), ep)
+    def source_of(index):
+        return lax.rem(place_ref[0] * near + near + index - lax.rem(index, near), sources) + jnp.bitwise_xor(lax.rem(index, near), place_ref[1])
+
+    def loads(index):
+        source = source_of(index)
+        return (pltpu.make_async_copy(table_hbm.at[source, pl.ds(0, num_tokens)], rows_scr.at[index], load_sem.at[0, index]),
+                pltpu.make_async_copy(table_hbm.at[source, pl.ds(num_tokens, num_tokens)], dy_scr.at[index], load_sem.at[1, index]))
+
+    @pl.when(expert == 0)
+    def _():
+        @pl.loop(0, far)
+        def _(index):
+            for copy in loads(index):
+                copy.start()
+
+    def select(index):
+        source = source_of(index)
         selectors, gate_cols = [], []
         for k in range(group):
             selectors.append(jnp.where(slot_iota == pos_ref[k, pl.ds(source, 1), :], 1.0, 0.0).astype(BF16))
-            gate_cols.append(jnp.sum(jnp.where(diagonal, slot_gate_ref[k, pl.ds(gate_at, 1), :], 0.0), axis=1, keepdims=True))
+            gate_cols.append(jnp.sum(jnp.where(diagonal, slot_gate_ref[k, pl.ds(index, 1), :], 0.0), axis=1, keepdims=True))
         return jnp.concatenate(selectors, axis=0), jnp.concatenate(gate_cols, axis=0)
 
     @pl.when(member == 0)
     def _():
         unroll = 2
 
-        @pl.loop(0, sources // unroll)
-        def _(step):
+        def body(step, starts):
+            @pl.when(expert == 0)
+            def _():
+                for j in range(unroll):
+                    for copy in loads(step * unroll + j):
+                        copy.wait()
+
             ahead = select(step * unroll)
             for j in range(unroll):
-                source = step * unroll + j
+                index = step * unroll + j
                 selector, gate_col = ahead
                 if j + 1 < unroll:
-                    ahead = select(source + 1)
-                slot_rows = mat_nn(selector, rows_ref[source]).astype(BF16)
-                scaled_dy = (mat_nn(selector, dy_ref[source, :num_tokens]) * gate_col).astype(BF16)
+                    ahead = select(index + 1)
+                slot_rows = mat_nn(selector, rows_scr[index]).astype(BF16)
+                scaled_dy = (mat_nn(selector, dy_scr[index]) * gate_col).astype(BF16)
                 for k in range(group):
-                    span = pl.ds(source * capacity, capacity)
+                    span = pl.ds(pl.multiple_of(starts[k], 16), capacity)
                     part = slice(k * capacity, (k + 1) * capacity)
                     in_scr[k, span] = slot_rows[part]
                     dout_scr[k, span] = scaled_dy[part]
-
-    d_w_gate_ref[...] = jnp.zeros_like(d_w_gate_ref)
-    d_w_up_ref[...] = jnp.zeros_like(d_w_up_ref)
-    down_scr[...] = jnp.zeros_like(down_scr)
-
-    def forward(start):
-        span = pl.ds(start, chunk)
-        slot_rows = in_scr[member, span]
-        d_out = dout_scr[member, span]
-        return slot_rows, d_out, mat_nn(slot_rows, w_gate_ref[0]), mat_nn(slot_rows, w_up_ref[0]), mat_nt(d_out, w_down_ref[0])
-
-    ahead = forward(0)
-    for start in range(0, sources * capacity, chunk):
-        slot_rows, d_out, act_gate, act_up, d_hidden = ahead
-        if start + chunk < sources * capacity:
-            ahead = forward(start + chunk)
-        hidden, d_act_gate, d_act_up = swiglu_bwd(act_gate, act_up, d_hidden)
-        d_w_gate_ref[0] += mat_tn(slot_rows, d_act_gate)
-        d_w_up_ref[0] += mat_tn(slot_rows, d_act_up)
-        down_scr[...] += mat_tn(d_out, hidden)
-
-    d_w_down_ref[0] = down_scr[...].T
-
-
-def weight_grads(positions, slot_gates, rows, dy_rows, w_gate, w_up, w_down, capacity):
+                starts = tuple(starts[k] + count_ref[expert + k, source_of(index)] for k in range(group))
+            return starts
+
+        ends = lax.fori_loop(0, far // unroll, body, (jnp.int32(0),) * group)
+        empty = jnp.zeros((tail, in_scr.shape[2]), BF16)
+        for k in range(group):
+            total_scr[k] = ends[k]
+            span = pl.ds(pl.multiple_of(ends[k], 16), tail)
+            in_scr[k, span] = empty
+            dout_scr[k, span] = empty
+
+            @pl.loop((ends[k] + tail - 1) // tail, sum(chunks) // tail)
+            def _(block):
+                span = pl.ds(pl.multiple_of(block * tail, tail), tail)
+                in_scr[k, span] = empty
+                dout_scr[k, span] = empty
+
+    def forward(start, size, cols):
+        slot_rows = in_scr[member, pl.ds(start, size)]
+        d_out = dout_scr[member, pl.ds(start, size)]
+        return (slot_rows, d_out, mat_nn(slot_rows, w_gate_ref[0, :, cols] * jnp.asarray(0.5, BF16)), mat_nn(slot_rows, w_up_ref[0, :, cols]),
+                mat_nt(d_out, w_down_ref[0, cols, :]))
+
+    def accumulate(steps):
+        ahead = forward(*steps[0])
+        for at, (start, _, cols) in enumerate(steps):
+            slot_rows, d_out, half_gate, act_up, d_hidden = ahead
+            if at + 1 < len(steps):
+                ahead = forward(*steps[at + 1])
+            hidden, twice_d_act_gate, d_act_up = swiglu_bwd(half_gate, act_up, d_hidden)
+            gate_base, up_base = (near_gate_ref, near_up_ref) if start == 0 else (d_w_gate_ref, d_w_up_ref)
+            d_w_gate_ref[0, :, cols] = gate_base[0, :, cols] + 0.5 * mat_tn(slot_rows, twice_d_act_gate)
+            d_w_up_ref[0, :, cols] = up_base[0, :, cols] + mat_tn(slot_rows, d_act_up)
+            down_part = mat_tn(d_out, hidden)
+            down_scr[:, cols] = down_part if start == 0 else down_scr[:, cols] + down_part
+
+    tiles = [slice(f, f + f_tile) for f in range(0, ff, f_tile)]
+    accumulate([(sum(chunks[:c]), size, cols) for c, size in enumerate(chunks) for cols in tiles])
+
+    @pl.when(total_scr[member] > sum(chunks))
+    def _():
+        for start in range(sum(chunks), far * capacity, tail):
+            accumulate([(start, tail, cols) for cols in tiles])
+
+    d_w_down_ref[0] = near_down_ref[0] + down_scr[...].T
+
+
+def weight_grads(positions, counts, place, slot_gates, table, w_gate, w_up, w_down, near_grads, capacity):
     group = 4
-    chunk = 256
-    sources, num_tokens, width = rows.shape
+    near = 4
+    tail = 256
+    sources, num_tokens = positions.shape[1:]
+    width = table.shape[2]
+    far = sources - near
     num_experts, _, ff = w_gate.shape
-    slots = sources * capacity
-
-    def whole(arr):
-        return pl.BlockSpec(arr.shape, lambda step: (0,) * arr.ndim, pipeline_mode=pl.Buffered(1))
+    chunks = (1024, 1024)
+    slots = far * capacity + tail
 
     def per_step(arr):
-        return pl.BlockSpec((1,) + arr.shape[1:], lambda step: (step, 0, 0))
-
+        return pl.BlockSpec((1,) + arr.shape[1:], lambda step, *_: (step, 0, 0))
+
+    hbm = pl.BlockSpec(memory_space=pl.ANY)
+    weights = (w_gate, w_up, w_down)
     return pl.pallas_call(
-        functools.partial(weight_grad_kernel, capacity, group, chunk),
-        grid=(num_experts,),
-        in_specs=[pl.BlockSpec((group, sources, num_tokens), lambda step: (step // group, 0, 0)),
-                  pl.BlockSpec((group, sources, 128), lambda step: (step // group, 0, 0)),
-                  whole(rows), whole(dy_rows), per_step(w_gate), per_step(w_up), per_step(w_down)],
-        out_specs=[per_step(w_gate), per_step(w_up), per_step(w_down)],
-        out_shape=[jax.ShapeDtypeStruct(arr.shape, F32) for arr in (w_gate, w_up, w_down)],
-        scratch_shapes=[pltpu.VMEM((group, slots, width), BF16), pltpu.VMEM((group, slots, width), BF16), pltpu.VMEM((width, ff), F32)],
+        functools.partial(weight_grad_kernel, capacity, group, 256, near, chunks, tail),
+        grid_spec=pltpu.PrefetchScalarGridSpec(
+            num_scalar_prefetch=2, grid=(num_experts,),
+            in_specs=[pl.BlockSpec((group, sources, num_tokens), lambda step, *_: (step // group, 0, 0)),
+                      pl.BlockSpec((group, far, 128), lambda step, *_: (step // group, 0, 0)),
+                      hbm] + [per_step(arr) for arr in weights] * 2,
+            out_specs=[per_step(arr) for arr in weights],
+            scratch_shapes=[pltpu.VMEM((far, num_tokens, width), BF16), pltpu.VMEM((far, num_tokens, width), BF16),
+                            pltpu.VMEM((group, slots, width), BF16), pltpu.VMEM((group, slots, width), BF16),
+                            pltpu.VMEM((width, ff), F32), pltpu.SMEM((group,), jnp.int32), pltpu.SemaphoreType.DMA((2, far))]),
+        out_shape=[jax.ShapeDtypeStruct(arr.shape, F32) for arr in weights],
         compiler_params=pltpu.CompilerParams(vmem_limit_bytes=67_000_000, dimension_semantics=("arbitrary",)),
-        cost_estimate=pl.CostEstimate(flops=280_000_000_000, bytes_accessed=150_000_000, transcendentals=0),
+        cost_estimate=pl.CostEstimate(flops=280_000_000_000, bytes_accessed=225_000_000, transcendentals=0),
         name="expert_weight_grads",
-    )(positions, slot_gates, rows, dy_rows, w_gate, w_up, w_down)
+    )(counts, place, positions, slot_gates, table, w_gate, w_up, w_down, *near_grads)
 
 
 def dense_forward(x_rows, idx_cols, num_seqs, norm1_gain, norm2_gain, w_qkv, w_attn_out, w_router):
@@ -433,27 +530,28 @@
         idx_cols = route_idx.reshape(num_tokens, top_k).T
         routes = idx_cols.astype(BF16).reshape(-1, model_width)
         payload = jnp.concatenate([dy_rows, routes], axis=0)
-        dy_all = lax.all_gather(payload, ('dp', 'ep'))
         moved = [lax.ppermute(payload, 'ep', [(i, i ^ k) for i in range(ep_size)]) for k in range(1, ep_size)]
         dy_near = jnp.stack([payload] + moved)
 
         def expert_of(gathered):
-            return gathered[:, num_tokens:].reshape(-1, top_k, num_tokens).astype(jnp.int32) - lax.axis_index('ep') * local_experts
-
-        idx_near = expert_of(dy_near)
+            return gathered.reshape(-1, top_k, num_tokens).astype(jnp.int32) - lax.axis_index('ep') * local_experts
+
+        idx_near = expert_of(dy_near[:, num_tokens:])
         positions_near = slot_positions(idx_near, local_experts, capacity)
         normed2, gate_vals, saved_state = dense_forward(x_rows, idx_cols, num_seqs, norm1_gain, norm2_gain, w_qkv, w_attn_out, w_router)
-        rows_all = lax.all_gather(normed2, ('dp', 'ep'))
+        table = lax.all_gather(jnp.concatenate([normed2, payload], axis=0), ('dp', 'ep'))
         rows_near, gates_near = near_gather(normed2, gate_vals)
-        d_near, d_gate_near, slot_gates = token_grads(positions_near, idx_near, gates_near, rows_near, dy_near, w_gate, w_up, w_down, capacity)
+        d_near, d_gate_near, slot_gates, *near_grads = token_grads(positions_near, idx_near, gates_near, rows_near, dy_near, w_gate, w_up, w_down, capacity)
         d_normed2_moe, d_gates, slot_gates_all = near_return(d_near, d_gate_near, slot_gates, mesh.shape['dp'])
         slot_gates_all = slot_gates_all.transpose(1, 0, 2, 3).reshape(local_experts, -1, 128)
         d_x, dense_grads = dense_backward(saved_state, x_rows, dy_rows, d_gates, d_normed2_moe, norm1_gain, norm2_gain, w_qkv, w_attn_out, w_router)
         gain_cols = jnp.zeros((model_width, 128), F32).at[:, 0].set(dense_grads[0]).at[:, 1].set(dense_grads[1])
         packed = jnp.concatenate(dense_grads[2:] + (gain_cols,), axis=1)
         packed, slot_gates_all = lax.optimization_barrier((packed, slot_gates_all))
-        positions = slot_positions(expert_of(dy_all), local_experts, capacity)
-        expert_grads = weight_grads(positions, slot_gates_all, rows_all, dy_all, w_gate, w_up, w_down, capacity)
+        positions = all_positions(expert_of(table[:, 2 * num_tokens:]).transpose(1, 0, 2), local_experts, capacity)
+        counts = (jnp.max(positions, axis=2) + 16) // 16 * 16
+        place = jnp.stack([lax.axis_index('dp'), lax.axis_index('ep')]).astype(jnp.int32)
+        expert_grads = weight_grads(positions, counts, place, slot_gates_all, table, w_gate, w_up, w_down, near_grads, capacity)
         packed = lax.psum(packed, ('dp', 'ep'))
         qkv_end = w_qkv.shape[1]
         out_end = qkv_end + w_attn_out.shape[1]

time: 980 us -> 926 us (0.945)
  Pallas kernels: 506 us -> 469 us
  waiting for transfers between devices: 337 us -> 316 us
    pallas_call x2 -> x3, Pallas kernels: 452 us -> 415 us  [the longest x1 319 us: weight_grads(): pl.pallas_call(functools.partial(weight_grad_kernel, capacity, group, 256...]
    all_gather x2 -> x1, waiting for transfers between devices: 209 us -> 192 us  [local_step(): lax.all_gather(jnp.concatenate([normed2, payload], axis=0), ('dp', 'ep'))]
    reduce_or x2 -> x1, other arithmetic: 13.8 us -> 1.82 us  [slot_positions(): member = jnp.any(local_idx[None] == expert_ids[:, None, None, None], axis=2)]
  transfers between devices with their start and end apart: 6 -> 5, of which waited for: 3 -> 2; matrix products, arithmetic and copies ran while one was open for 6% -> 4% of each run, Pallas kernels for 2% -> 2%
where the time goes in v3:
time: 926 us; the launch traced here: 916 us
  Pallas kernels  469 us (51%)
  waiting for transfers between devices  316 us (34%)
  other arithmetic  47.7 us (5%)
  local copies, waits for them, and re-layouts  35.5 us (4%)
  matrix products  29.5 us (3%)
  between operations  15 us (2%)
    pallas_call x1, Pallas kernels, weight_grads(): pl.pallas_call(functools.partial(weight_grad_kernel, capacity, group, 256...  319 us
    all_gather x1, waiting for transfers between devices, local_step(): lax.all_gather(jnp.concatenate([normed2, payload], axis=0), ('dp', 'ep'))  192 us
    psum x1, waiting for transfers between devices, local_step(): packed = lax.psum(packed, ('dp', 'ep'))  124 us
    pallas_call x1, Pallas kernels, token_grads(): pl.pallas_call(functools.partial(token_grad_kernel, capacity, group, 256)...  88.6 us
    pallas_call x1, Pallas kernels, near_return(): pl.pallas_call(near_return_kernel, in_specs=[vmem] * 3, out_specs=[vmem]...  34.6 us
    pallas_call x1, Pallas kernels, near_gather(): pl.pallas_call(near_gather_kernel, in_specs=[vmem, vmem], out_specs=[vmem...  18.8 us
  transfers between devices with their start and end apart: 5, of which 2 were waited for; matrix products, arithmetic and copies ran while one was open for 4% of the time, Pallas kernels for 2%

profile of v3, /device:TPU:0, one launch (start us, length us, event | category | flops | bytes accessed | tf_op | source)
XLA Modules:
  0.0 915.6 jit_solution(14000139571545629175)
XLA Ops:
  8.0 2.1 fusion.74
  10.1 3.0 collective-permute-start.1
  24.8 4.9 fusion.77
  29.8 2.8 divide_convert_fusion
  39.1 2.8 select_reduce_fusion
  42.5 18.8 %near_gather.1 = (bf16[4,1024,256]{2,1,0:T(8,128)(2,1)}, f32[4,8,1024]{2,1,0:T(8,128)}) custom-call(bf16[1024,256]{1,0:T(8,128)(2,1)} %copy-done.8, f32[8,1024]{1,0:T(8,128)} %broadcast_divide_fusion.gates_ref), custom_call_target="tpu_custom_call" | custom-call | flops 10000000000 | bytes 10000000 | tf_op jit(solution)/shard_map/near_gather/pallas_call | solution.py:249
  69.5 88.6 %expert_token_grads.1 = (f32[4,1024,256]{2,1,0:T(8,128)}, f32[4,8,1024]{2,1,0:T(8,128)}, f32[32,4,128]{2,1,0:T(4,128)}, f32[32,256,768]{2,1,0:T(8,128)}, f32[32,...) custom-call(s32[32,4,1024]{2,1,0:T(4,128)} %convert_select_fusion.pos_ref, s32[4,8,1024]{2,1,0:T(8,128)} %copy-done.27, ...), custom_call_target="tpu_custom_call" | custom-call | flops 60000002048 | bytes 130000000 | tf_op jit(solution)/shard_map/expert_token_grads/pallas_call | solution.py:190
  158.1 2.2 copy-done.1
  162.1 34.6 %near_return.1 = (f32[1024,256]{1,0:T(8,128)S(1)}, f32[8,1024]{1,0:T(8,128)S(1)}, f32[7,32,4,128]{3,2,1,0:T(4,128)S(1)}) custom-call(f32[4,1024,256]{2,1,0:T(8,128)S(1)} %copy-done.1, f32[4,8,1024]{2,1,0:T(8,128)S(1)} %copy-done.2, f32[32,4,128]{2,1,0:T(4,128)S(1)} %copy-done.3), custom_call_target="tpu_custom_call" | custom-call | flops 15000000512 | bytes 20000000 | tf_op jit(solution)/shard_map/near_return/pallas_call | solution.py:301
  196.7 3.6 select_reduce_fusion.2
  213.6 2.6 fusion.21
  216.3 3.6 fusion.6
  220.3 2.4 fusion.18
  222.7 2.4 fusion.16
  230.2 4.3 copy.78
  236.2 3.1 fusion.79
  239.3 3.1 fusion.41
  243.8 2.3 pad_maximum_fusion.1
  249.0 2.5 fusion.38
  251.5 124.0 %all-reduce.10.cloned.1.call-done = f32[256,1280]{1,0:T(8,128)} async-done(((f32[256,1280]{1,0:T(8,128)}), f32[256,1280]{1,0:T(8,128)}) %all-reduce.10.cloned.1.call-update) | async-done | bytes 1310736 | tf_op jit(solution)/shard_map/psum | solution.py:555
  382.6 192.1 %all-gather.3.cloned.1.call-done = bf16[66560,256]{1,0:T(8,128)(2,1)} async-done(((bf16[2080,256]{1,0:T(8,128)(2,1)}), bf16[66560,256]{1,0:T(8,128)(2,1)}) %all-gather.3.cloned.1.call-update) | async-done | bytes 34078736 | tf_op jit(solution)/shard_map/all_gather | solution.py:542
  576.8 7.3 slot_positions.1
  586.0 2.5 reduce_max.29
  589.2 319.3 %expert_weight_grads.1 = (f32[32,256,768]{2,1,0:T(8,128)}, f32[32,256,768]{2,1,0:T(8,128)}, f32[32,768,256]{2,1,0:T(8,128)}) custom-call(s32[32,32]{1,0:T(8,128)} %fusion.63.count_ref, s32[2]{0:T(128)} %pad_add_fusion.place_ref, s32[32,32,1024]{2,1,0:T(8,128)} %bitcast.116, f32[32,28,128]{2,1,0:T(8,128)} %copy.85.slot_gate_ref, ...), custom_call_target="tpu_custom_call" | custom-call | flops 280000004096 | bytes 225000000 | tf_op jit(solution)/shard_map/expert_weight_grads/pallas_call | solution.py:468
  (170 shorter events, 65.7 us)
Async XLA Ops:
  7.2 368.4 %all-reduce.10.cloned.1.call-start = ((), (), s32[]{:S(2)}) async-start(), calls=%async_computation | async-start | bytes 2621440 | tf_op jit(solution)/shard_map/psum | solution.py:555
  10.1 52.6 %collective-permute-start.1 = (bf16[1056,256]{1,0:T(8,128)(2,1)}, bf16[1056,256]{1,0:T(8,128)(2,1)}, u32[]{:S(2)}, u32[]{:S(2)}) collective-permute-start(bf16[1056,256]{1,0:T(8,128)(2,1)} %get-tuple-element.84), channel_id=1, source_target_pairs={{0,2},{1,3},{2,0},{3,1},{4,6},{5,7},{6,4},{7,5},{8,10},{9,11},{10,... | collective-permute-start | bytes 1622024 | tf_op jit(solution)/shard_map/ppermute | solution.py:533
  13.1 49.7 %collective-permute-start = (bf16[1056,256]{1,0:T(8,128)(2,1)}, bf16[1056,256]{1,0:T(8,128)(2,1)}, u32[]{:S(2)}, u32[]{:S(2)}) collective-permute-start(bf16[1056,256]{1,0:T(8,128)(2,1)} %get-tuple-element.84), channel_id=1, source_target_pairs={{0,1},{1,0},{2,3},{3,2},{4,5},{5,4},{6,7},{7,6},{8,9},{9,8},{10,11... | collective-permute-start | bytes 1622024 | tf_op jit(solution)/shard_map/ppermute | solution.py:533
  13.1 49.7 %collective-permute-start.2 = (bf16[1056,256]{1,0:T(8,128)(2,1)}, bf16[1056,256]{1,0:T(8,128)(2,1)}, u32[]{:S(2)}, u32[]{:S(2)}) collective-permute-start(bf16[1056,256]{1,0:T(8,128)(2,1)} %get-tuple-element.84), channel_id=1, source_target_pairs={{0,3},{1,2},{2,1},{3,0},{4,7},{5,6},{6,5},{7,4},{8,11},{9,10},{10,... | collective-permute-start | bytes 1622024 | tf_op jit(solution)/shard_map/ppermute | solution.py:533
  14.6 6.8 copy-start.40
  22.8 9.7 %copy-start.6 = (f32[2,512,3,2,128]{1,4,3,2,0:T(8,128)}, f32[2,512,3,2,128]{1,4,3,2,0:T(8,128)S(1)}, u32[]{:S(2)}) copy-start(f32[2,512,3,2,128]{1,4,3,2,0:T(8,128)S(1)} %fusion.46) | copy-start | bytes 9437188
  29.8 6.7 copy-start.37
  33.9 4.3 copy-start.39
  33.9 4.5 copy-start.30
  38.1 167.0 %copy-start.10 = (bf16[1024,256]{1,0:T(8,128)(2,1)}, bf16[1024,256]{1,0:T(8,128)(2,1)S(1)}, u32[]{:S(2)}) copy-start(bf16[1024,256]{1,0:T(8,128)(2,1)S(1)} %get-tuple-element.98) | copy-start | bytes 1572868
  38.4 4.1 copy-start.8
  42.5 18.8 %copy-start.38 = (f32[1,4,2,128]{3,2,1,0:T(2,128)S(1)}, f32[1,4,2,128]{3,2,1,0:T(2,128)}, u32[]{:S(2)}) copy-start(f32[1,4,2,128]{3,2,1,0:T(2,128)} %get-tuple-element.89) | copy-start | bytes 12292
  42.5 20.2 %copy-start.18 = (bf16[1,1056,256]{2,1,0:T(8,128)(2,1)S(1)}, bf16[1,1056,256]{2,1,0:T(8,128)(2,1)}, u32[]{:S(2)}) copy-start(bf16[1,1056,256]{2,1,0:T(8,128)(2,1)} %get-tuple-element.83) | copy-start | bytes 1622020
  196.7 8.1 copy-start.9
  205.8 7.9 copy-start.5
  216.3 4.0 copy-start.35
  216.3 4.1 copy-start.36
  230.2 9.1 copy-start.15
  230.2 9.1 copy-start.41
  236.2 7.0 copy-start.26
  236.2 7.6 copy-start.29
  239.3 6.9 copy-start.14
  243.2 5.8 copy-start.12
  246.1 328.5 %all-gather.3.cloned.1.call-start = ((), (), s32[]{:S(2)}) async-start(), calls=%async_computation.1 | async-start | bytes 35143680 | tf_op jit(solution)/shard_map/all_gather | solution.py:542
  (23 other events, 55.7 us)
Sparse Core Ops, SparseCore 0:
  246.3 129.2 all-reduce.9
  378.9 195.6 all-gather.2

commit v4 on v3

--- a/solution.py
+++ b/solution.py
@@ -17,55 +17,6 @@
 
 def capacity_rows(num_tokens, top_k, num_experts):
     return 8 * ((5 * num_tokens * top_k + 32 * num_experts - 1) // (32 * num_experts))
-
-
-def rms_norm(x_rows, gain_vec):
-    x_f32 = x_rows.astype(jnp.float32)
-    inv_rms = lax.rsqrt(jnp.mean(x_f32 * x_f32, axis=-1, keepdims=True) + EPS)
-    return (x_f32 * inv_rms * gain_vec.astype(jnp.float32)).astype(jnp.bfloat16)
-
-
-def rms_norm_bwd(x_rows, gain_vec, d_out):
-    x_f32 = x_rows.astype(jnp.float32)
-    inv_rms = lax.rsqrt(jnp.mean(x_f32 * x_f32, axis=-1, keepdims=True) + EPS)
-    d_gain = jnp.sum(d_out * x_f32 * inv_rms, axis=0)
-    d_scaled = d_out * gain_vec.astype(jnp.float32)
-    d_x = inv_rms * d_scaled - x_f32 * inv_rms ** 3 * jnp.mean(d_scaled * x_f32, axis=-1, keepdims=True)
-    return d_x, d_gain
-
-
-def rope_rotate(head_vals):
-    seq_len = head_vals.shape[1]
-    half_dim = head_vals.shape[-1] // 2
-    inv_freq = ROPE_BASE ** (-jnp.arange(half_dim, dtype=jnp.float32) / half_dim)
-    angles = jnp.arange(seq_len, dtype=jnp.float32)[:, None] * inv_freq[None, :]
-    cos_b = jnp.cos(angles)[None, :, None, :]
-    sin_b = jnp.sin(angles)[None, :, None, :]
-    lower_half = head_vals[..., :half_dim]
-    upper_half = head_vals[..., half_dim:]
-    return jnp.concatenate([lower_half * cos_b - upper_half * sin_b, upper_half * cos_b + lower_half * sin_b], axis=-1)
-
-
-def attention_core(qkv_rows, num_seqs):
-    num_tokens = qkv_rows.shape[0]
-    seq_len = num_tokens // num_seqs
-    model_width = qkv_rows.shape[1] // 3
-    qkv_heads = qkv_rows.reshape(num_seqs, seq_len, 3, model_width // HEAD_DIM, HEAD_DIM)
-    query_rot = rope_rotate(qkv_heads[:, :, 0]).astype(jnp.bfloat16)
-    key_rot = rope_rotate(qkv_heads[:, :, 1]).astype(jnp.bfloat16)
-    value_h = qkv_heads[:, :, 2].astype(jnp.bfloat16)
-    scores = jnp.einsum('bqhd,bkhd->bhqk', query_rot, key_rot, preferred_element_type=jnp.float32) * HEAD_DIM ** -0.5
-    causal = jnp.arange(seq_len)[:, None] >= jnp.arange(seq_len)[None, :]
-    attn_probs = jax.nn.softmax(jnp.where(causal, scores, -1e30), axis=-1).astype(jnp.bfloat16)
-    context = jnp.einsum('bhqk,bkhd->bqhd', attn_probs, value_h, preferred_element_type=jnp.float32)
-    return context.astype(jnp.bfloat16).reshape(num_tokens, model_width)
-
-
-def gate_probs(logits, idx_cols):
-    probs_all = jax.nn.softmax(logits, axis=-1)
-    chosen = idx_cols[:, :, None] == jnp.arange(logits.shape[1], dtype=jnp.int32)[None, None, :]
-    picked = jnp.sum(jnp.where(chosen, probs_all[None], 0.0), axis=2)
-    return picked / jnp.sum(picked, axis=0, keepdims=True)
 
 
 def slot_positions(local_idx, local_experts, capacity):
@@ -224,7 +175,8 @@
 def near_gather_kernel(rows_ref, gates_ref, rows_out, gates_out, send_sem, recv_sem):
     core_peer, chip_peer = near_peers()
     meet((core_peer, chip_peer))
-    half = rows_ref.shape[0] // 2
+    num_tokens = rows_out.shape[1]
+    half = num_tokens // 2
     pieces = [(rows_ref.at[pl.ds(0, half)], lambda slot: rows_out.at[slot, pl.ds(0, half)]),
               (rows_ref.at[pl.ds(half, half)], lambda slot: rows_out.at[slot, pl.ds(half, half)]),
               (gates_ref, lambda slot: gates_out.at[slot])]
@@ -233,7 +185,7 @@
     onward = [remote(place(2), place(3), send_sem.at[2, i], recv_sem.at[2, i], core_peer) for i, (_, place) in enumerate(pieces)]
     for copy in across + beside:
         copy.start()
-    rows_out[0] = rows_ref[...]
+    rows_out[0] = rows_ref[0:num_tokens]
     gates_out[0] = gates_ref[...]
     for copy, forward in zip(across, onward):
         copy.wait_recv()
@@ -244,12 +196,12 @@
         copy.wait_send()
 
 
-def near_gather(rows, gates):
+def near_gather(rows, gates, num_tokens):
     vmem = pl.BlockSpec(memory_space=pltpu.VMEM)
     return pl.pallas_call(
         near_gather_kernel,
         in_specs=[vmem, vmem], out_specs=[vmem, vmem],
-        out_shape=[jax.ShapeDtypeStruct((4,) + rows.shape, rows.dtype), jax.ShapeDtypeStruct((4,) + gates.shape, gates.dtype)],
+        out_shape=[jax.ShapeDtypeStruct((4, num_tokens, rows.shape[1]), rows.dtype), jax.ShapeDtypeStruct((4,) + gates.shape, gates.dtype)],
         scratch_shapes=[pltpu.SemaphoreType.DMA((3, 3)), pltpu.SemaphoreType.DMA((3, 3))],
         compiler_params=pltpu.CompilerParams(collective_id=0, has_side_effects=True),
         cost_estimate=pl.CostEstimate(flops=10_000_000_000, bytes_accessed=10_000_000, transcendentals=0),
@@ -257,7 +209,7 @@
     )(rows, gates)
 
 
-def near_return_kernel(d_rows_ref, d_gates_ref, slot_gates_ref, rows_out, gates_out, slot_gates_out,
+def near_return_kernel(d_rows_ref, d_gates_ref, slot_gates_ref, routes_ref, rows_out, gates_out, slot_gates_out, routes_out,
                        own_rows, pass_rows, sum_rows, last_rows, own_gates, pass_gates, sum_gates, last_gates,
                        send_sem, recv_sem, far_send_sem, far_recv_sem):
     core_peer, chip_peer = near_peers()
@@ -271,7 +223,8 @@
               remote(d_gates_ref.at[1], own_gates, send_sem.at[3], recv_sem.at[3], core_peer)]
     third = [remote(sum_rows, last_rows, send_sem.at[4], recv_sem.at[4], chip_peer),
              remote(sum_gates, last_gates, send_sem.at[5], recv_sem.at[5], chip_peer)]
-    far = [remote(slot_gates_ref, slot_gates_out.at[dp_size - 2 - k], far_send_sem.at[k], far_recv_sem.at[k], peer) for k, peer in enumerate(far_peers)]
+    far = [remote(slot_gates_ref, slot_gates_out.at[dp_size - 2 - k], far_send_sem.at[0, k], far_recv_sem.at[0, k], peer) for k, peer in enumerate(far_peers)]
+    far += [remote(routes_ref, routes_out.at[dp_size - 1 - k], far_send_sem.at[1, k], far_recv_sem.at[1, k], peer) for k, peer in enumerate(far_peers)]
     for copy in first + second:
         copy.start()
     for copy in first:
@@ -284,6 +237,7 @@
     gates_out[...] = d_gates_ref[0] + own_gates[...]
     for copy in third + far:
         copy.start()
+    routes_out[0] = routes_ref[...]
     for copy in third:
         copy.wait_recv()
     rows_out[...] += last_rows[...]
@@ -294,20 +248,20 @@
         copy.wait_send()
 
 
-def near_return(d_rows, d_gates, slot_gates, dp_size):
+def near_return(d_rows, d_gates, slot_gates, routes, dp_size):
     vmem = pl.BlockSpec(memory_space=pltpu.VMEM)
     rows = jax.ShapeDtypeStruct(d_rows.shape[1:], F32)
     gates = jax.ShapeDtypeStruct(d_gates.shape[1:], F32)
     return pl.pallas_call(
         near_return_kernel,
-        in_specs=[vmem] * 3, out_specs=[vmem] * 3,
-        out_shape=[rows, gates, jax.ShapeDtypeStruct((dp_size - 1,) + slot_gates.shape, F32)],
+        in_specs=[vmem] * 4, out_specs=[vmem] * 4,
+        out_shape=[rows, gates, jax.ShapeDtypeStruct((dp_size - 1,) + slot_gates.shape, F32), jax.ShapeDtypeStruct((dp_size,) + routes.shape, BF16)],
         scratch_shapes=[pltpu.VMEM(rows.shape, F32)] * 4 + [pltpu.VMEM(gates.shape, F32)] * 4
-        + [pltpu.SemaphoreType.DMA((6,)), pltpu.SemaphoreType.DMA((6,)), pltpu.SemaphoreType.DMA((dp_size - 1,)), pltpu.SemaphoreType.DMA((dp_size - 1,))],
+        + [pltpu.SemaphoreType.DMA((6,)), pltpu.SemaphoreType.DMA((6,)), pltpu.SemaphoreType.DMA((2, dp_size - 1)), pltpu.SemaphoreType.DMA((2, dp_size - 1))],
         compiler_params=pltpu.CompilerParams(collective_id=1, has_side_effects=True, vmem_limit_bytes=40_000_000),
         cost_estimate=pl.CostEstimate(flops=15_000_000_000, bytes_accessed=20_000_000, transcendentals=0),
         name="near_return",
-    )(d_rows, d_gates, slot_gates)
+    )(d_rows, d_gates, slot_gates, routes)
 
 
 def position_kernel(capacity, num_experts, idx_ref, pos_ref, member_scr):
@@ -346,7 +300,7 @@
 
 def weight_grad_kernel(capacity, group, f_tile, near, chunks, tail, count_ref, place_ref, pos_ref, slot_gate_ref, table_hbm,
                        w_gate_ref, w_up_ref, w_down_ref, near_gate_ref, near_up_ref, near_down_ref,
-                       d_w_gate_ref, d_w_up_ref, d_w_down_ref, rows_scr, dy_scr, in_scr, dout_scr, down_scr, total_scr, load_sem):
+                       d_w_gate_ref, d_w_up_ref, d_w_down_ref, rows_scr, dy_scr, in_scr, dout_scr, total_scr, load_sem):
     expert = pl.program_id(0)
     member = lax.rem(expert, group)
     far, num_tokens, _ = rows_scr.shape
@@ -371,16 +325,15 @@
                 copy.start()
 
     def select(index):
-        source = source_of(index)
         selectors, gate_cols = [], []
         for k in range(group):
-            selectors.append(jnp.where(slot_iota == pos_ref[k, pl.ds(source, 1), :], 1.0, 0.0).astype(BF16))
+            selectors.append(jnp.where(slot_iota == pos_ref[k, pl.ds(index + near, 1), :], 1.0, 0.0).astype(BF16))
             gate_cols.append(jnp.sum(jnp.where(diagonal, slot_gate_ref[k, pl.ds(index, 1), :], 0.0), axis=1, keepdims=True))
         return jnp.concatenate(selectors, axis=0), jnp.concatenate(gate_cols, axis=0)
 
     @pl.when(member == 0)
     def _():
-        unroll = 2
+        unroll = 7
 
         def body(step, starts):
             @pl.when(expert == 0)
@@ -402,7 +355,7 @@
                     part = slice(k * capacity, (k + 1) * capacity)
                     in_scr[k, span] = slot_rows[part]
                     dout_scr[k, span] = scaled_dy[part]
-                starts = tuple(starts[k] + count_ref[expert + k, source_of(index)] for k in range(group))
+                starts = tuple(starts[k] + count_ref[expert + k, index + near] for k in range(group))
             return starts
 
         ends = lax.fori_loop(0, far // unroll, body, (jnp.int32(0),) * group)
@@ -435,8 +388,7 @@
             gate_base, up_base = (near_gate_ref, near_up_ref) if start == 0 else (d_w_gate_ref, d_w_up_ref)
             d_w_gate_ref[0, :, cols] = gate_base[0, :, cols] + 0.5 * mat_tn(slot_rows, twice_d_act_gate)
             d_w_up_ref[0, :, cols] = up_base[0, :, cols] + mat_tn(slot_rows, d_act_up)
-            down_part = mat_tn(d_out, hidden)
-            down_scr[:, cols] = down_part if start == 0 else down_scr[:, cols] + down_part
+            d_w_down_ref[0, cols, :] = (near_down_ref if start == 0 else d_w_down_ref)[0, cols, :] + mat_tn(hidden, d_out)
 
     tiles = [slice(f, f + f_tile) for f in range(0, ff, f_tile)]
     accumulate([(sum(chunks[:c]), size, cols) for c, size in enumerate(chunks) for cols in tiles])
@@ -445,8 +397,6 @@
     def _():
         for start in range(sum(chunks), far * capacity, tail):
             accumulate([(start, tail, cols) for cols in tiles])
-
-    d_w_down_ref[0] = near_down_ref[0] + down_scr[...].T
 
 
 def weight_grads(positions, counts, place, slot_gates, table, w_gate, w_up, w_down, near_grads, capacity):
@@ -456,7 +406,7 @@
     sources, num_tokens = positions.shape[1:]
     width = table.shape[2]
     far = sources - near
-    num_experts, _, ff = w_gate.shape
+    num_experts, _, _ = w_gate.shape
     chunks = (1024, 1024)
     slots = far * capacity + tail
 
@@ -475,7 +425,7 @@
             out_specs=[per_step(arr) for arr in weights],
             scratch_shapes=[pltpu.VMEM((far, num_tokens, width), BF16), pltpu.VMEM((far, num_tokens, width), BF16),
                             pltpu.VMEM((group, slots, width), BF16), pltpu.VMEM((group, slots, width), BF16),
-                            pltpu.VMEM((width, ff), F32), pltpu.SMEM((group,), jnp.int32), pltpu.SemaphoreType.DMA((2, far))]),
+                            pltpu.SMEM((group,), jnp.int32), pltpu.SemaphoreType.DMA((2, far))]),
         out_shape=[jax.ShapeDtypeStruct(arr.shape, F32) for arr in weights],
         compiler_params=pltpu.CompilerParams(vmem_limit_bytes=67_000_000, dimension_semantics=("arbitrary",)),
         cost_estimate=pl.CostEstimate(flops=280_000_000_000, bytes_accessed=225_000_000, transcendentals=0),
@@ -483,33 +433,180 @@
     )(counts, place, positions, slot_gates, table, w_gate, w_up, w_down, *near_grads)
 
 
-def dense_forward(x_rows, idx_cols, num_seqs, norm1_gain, norm2_gain, w_qkv, w_attn_out, w_router):
-    normed1 = rms_norm(x_rows, norm1_gain)
-    qkv_rows = jnp.dot(normed1, w_qkv, preferred_element_type=jnp.float32)
-    context, attn_pullback = jax.vjp(lambda qkv_in: attention_core(qkv_in, num_seqs), qkv_rows)
-    h_rows = (x_rows.astype(jnp.float32) + jnp.dot(context, w_attn_out, preferred_element_type=jnp.float32)).astype(jnp.bfloat16)
-    normed2 = rms_norm(h_rows, norm2_gain)
-    logits = jnp.dot(normed2, w_router, preferred_element_type=jnp.float32)
-    gate_vals, gate_pullback = jax.vjp(lambda logit_in: gate_probs(logit_in, idx_cols), logits)
-    saved_state = (normed1, attn_pullback, context, h_rows, normed2, gate_pullback)
-    return normed2, gate_vals, saved_state
-
-
-def dense_backward(saved_state, x_rows, dy_rows, d_gates, d_normed2_moe, norm1_gain, norm2_gain, w_qkv, w_attn_out, w_router):
-    normed1, attn_pullback, context, h_rows, normed2, gate_pullback = saved_state
-    d_logits = gate_pullback(d_gates)[0].astype(jnp.bfloat16)
-    d_w_router = jnp.einsum('td,te->de', normed2, d_logits, preferred_element_type=jnp.float32)
-    d_normed2 = d_normed2_moe + jnp.einsum('te,de->td', d_logits, w_router, preferred_element_type=jnp.float32)
-    d_h_part, d_norm2_gain = rms_norm_bwd(h_rows, norm2_gain, d_normed2)
-    d_h = (dy_rows.astype(jnp.float32) + d_h_part).astype(jnp.bfloat16)
-    d_w_attn_out = jnp.einsum('td,te->de', context, d_h, preferred_element_type=jnp.float32)
-    d_context = jnp.einsum('te,de->td', d_h, w_attn_out, preferred_element_type=jnp.float32).astype(jnp.bfloat16)
-    d_qkv = attn_pullback(d_context)[0].astype(jnp.bfloat16)
-    d_w_qkv = jnp.einsum('td,te->de', normed1, d_qkv, preferred_element_type=jnp.float32)
-    d_normed1 = jnp.einsum('te,de->td', d_qkv, w_qkv, preferred_element_type=jnp.float32)
-    d_x_part, d_norm1_gain = rms_norm_bwd(x_rows, norm1_gain, d_normed1)
-    d_x = (d_h.astype(jnp.float32) + d_x_part).astype(jnp.bfloat16)
-    return d_x, (d_norm1_gain, d_norm2_gain, d_w_qkv, d_w_attn_out, d_w_router)
+def rms_parts(x_f32):
+    return lax.rsqrt(jnp.mean(x_f32 * x_f32, axis=-1, keepdims=True) + EPS)
+
+
+def rms_back(x_f32, inv_rms, gain_row, d_out):
+    d_gain = jnp.sum(d_out * x_f32 * inv_rms, axis=0, keepdims=True)
+    d_scaled = d_out * gain_row
+    d_x = inv_rms * d_scaled - x_f32 * inv_rms ** 3 * jnp.mean(d_scaled * x_f32, axis=-1, keepdims=True)
+    return d_x, d_gain
+
+
+def rope_tables(seq_len):
+    half_dim = HEAD_DIM // 2
+    inv_freq = ROPE_BASE ** (-jnp.arange(half_dim, dtype=F32) / half_dim)
+    angles = jnp.arange(seq_len, dtype=F32)[:, None] * inv_freq[None, :]
+    cos, sin = jnp.cos(angles), jnp.sin(angles)
+    return jnp.concatenate([cos, cos], axis=1), jnp.concatenate([-sin, sin], axis=1)
+
+
+def causal_probs(query, keys, start):
+    scores = mat_nt(query, keys) * HEAD_DIM ** -0.5
+    rows = lax.broadcasted_iota(jnp.int32, scores.shape, 0) + start
+    scores = jnp.where(rows >= lax.broadcasted_iota(jnp.int32, scores.shape, 1), scores, -1e30)
+    weights = jnp.exp(scores - jnp.max(scores, axis=1, keepdims=True))
+    return weights / jnp.sum(weights, axis=1, keepdims=True)
+
+
+def router_probs(rows, w_router_t):
+    logits = mat_nt(w_router_t, rows)
+    weights = jnp.exp(logits - jnp.max(logits, axis=0, keepdims=True))
+    return weights / jnp.sum(weights, axis=0, keepdims=True)
+
+
+def forward_kernel(num_seqs, x_ref, dy_ref, idx_ref, gains_ref, w_qkv_ref, w_out_ref, w_router_t_ref, cos_ref, sin_ref,
+                   payload_ref, gates_ref, qkv_ref, context_ref, h_ref, x_scr, w_qkv_scr, w_out_scr, load_sem):
+    num_tokens, width = x_ref.shape
+    seq_len = num_tokens // num_seqs
+    block = 256
+    loads = [pltpu.make_async_copy(src, dst, load_sem.at[i]) for i, (src, dst) in enumerate([
+        (x_ref, x_scr), (w_qkv_ref, w_qkv_scr), (w_out_ref, w_out_scr), (dy_ref, payload_ref.at[pl.ds(num_tokens, num_tokens)])])]
+    for copy in loads:
+        copy.start()
+    loads[0].wait()
+    x_ref = x_scr
+    x_f32 = x_ref[...].astype(F32)
+    normed1 = (x_f32 * rms_parts(x_f32) * gains_ref[0:1].astype(F32)).astype(BF16)
+    loads[1].wait()
+    for head_col in range(0, 3 * width, HEAD_DIM):
+        vals = mat_nn(normed1, w_qkv_scr[:, head_col:head_col + HEAD_DIM])
+        for seq in range(num_seqs):
+            span = slice(seq * seq_len, (seq + 1) * seq_len)
+            part = vals[span]
+            if head_col < 2 * width:
+                part = part * cos_ref[...] + pltpu.roll(part, HEAD_DIM // 2, 1) * sin_ref[...]
+            qkv_ref[span, head_col:head_col + HEAD_DIM] = part.astype(BF16)
+    for seq in range(num_seqs):
+        for head in range(width // HEAD_DIM):
+            cols = [slice(part * width + head * HEAD_DIM, part * width + (head + 1) * HEAD_DIM) for part in range(3)]
+            for start in range(0, seq_len, block):
+                rows = slice(seq * seq_len + start, seq * seq_len + start + block)
+                seen = slice(seq * seq_len, seq * seq_len + start + block)
+                probs = causal_probs(qkv_ref[rows, cols[0]], qkv_ref[seen, cols[1]], start).astype(BF16)
+                context_ref[rows, cols[0]] = mat_nn(probs, qkv_ref[seen, cols[2]]).astype(BF16)
+    loads[2].wait()
+    h_rows = (x_f32 + mat_nn(context_ref[...], w_out_scr[...])).astype(BF16)
+    h_ref[...] = h_rows
+    h_f32 = h_rows.astype(F32)
+    normed2 = (h_f32 * rms_parts(h_f32) * gains_ref[1:2].astype(F32)).astype(BF16)
+    payload_ref[0:num_tokens] = normed2
+    probs = router_probs(normed2, w_router_t_ref[...])
+    expert_iota = lax.broadcasted_iota(jnp.int32, probs.shape, 0)
+    picked = [jnp.sum(jnp.where(expert_iota == idx_ref[choice:choice + 1], probs, 0.0), axis=0, keepdims=True) for choice in range(idx_ref.shape[0])]
+    total = functools.reduce(lambda a, b: a + b, picked)
+    for choice, part in enumerate(picked):
+        gates_ref[choice:choice + 1] = part / total
+    loads[3].wait()
+
+
+def dense_forward(x_rows, dy_rows, idx_cols, num_seqs, gains, w_qkv, w_attn_out, w_router_t, tables):
+    num_tokens, width = x_rows.shape
+    rows = jax.ShapeDtypeStruct(x_rows.shape, BF16)
+    hbm, vmem = pl.BlockSpec(memory_space=pl.ANY), pl.BlockSpec(memory_space=pltpu.VMEM)
+    return pl.pallas_call(
+        functools.partial(forward_kernel, num_seqs),
+        in_specs=[hbm, hbm, vmem, vmem, hbm, hbm, vmem, vmem, vmem],
+        scratch_shapes=[pltpu.VMEM(x_rows.shape, BF16), pltpu.VMEM(w_qkv.shape, BF16), pltpu.VMEM(w_attn_out.shape, BF16), pltpu.SemaphoreType.DMA((4,))],
+        out_shape=[jax.ShapeDtypeStruct((2 * num_tokens, width), BF16), jax.ShapeDtypeStruct(idx_cols.shape, F32),
+                   jax.ShapeDtypeStruct((num_tokens, 3 * width), BF16), rows, rows],
+        compiler_params=pltpu.CompilerParams(vmem_limit_bytes=66_000_000),
+        cost_estimate=pl.CostEstimate(flops=10_000_000_000, bytes_accessed=8_000_000, transcendentals=0),
+        name="dense_forward",
+    )(x_rows, dy_rows, idx_cols, gains, w_qkv, w_attn_out, w_router_t, *tables)
+
+
+def backward_kernel(num_seqs, x_ref, dy_ref, d_rows_ref, d_gates_ref, idx_ref, payload_ref, qkv_ref, context_ref, h_ref,
+                    gains_ref, w_qkv_ref, w_out_ref, w_router_t_ref, cos_ref, sin_ref, d_x_ref, d_w_qkv_ref, d_w_out_ref, packed_ref, d_qkv_scr):
+    num_tokens, width = x_ref.shape
+    seq_len = num_tokens // num_seqs
+    num_experts = w_router_t_ref.shape[0]
+    block = 256
+    normed2 = payload_ref[0:num_tokens]
+    probs = router_probs(normed2, w_router_t_ref[...])
+    expert_iota = lax.broadcasted_iota(jnp.int32, probs.shape, 0)
+    chosen = jnp.zeros(probs.shape, F32)
+    d_gate = jnp.zeros(probs.shape, F32)
+    for choice in range(idx_ref.shape[0]):
+        hit = expert_iota == idx_ref[choice:choice + 1]
+        chosen = jnp.where(hit, probs, chosen)
+        d_gate = jnp.where(hit, d_gates_ref[choice:choice + 1], d_gate)
+    total = jnp.sum(chosen, axis=0, keepdims=True)
+    mixed = jnp.sum(d_gate * chosen, axis=0, keepdims=True) / total
+    d_weighted = chosen * ((d_gate - mixed) / total)
+    d_logits = (d_weighted - probs * jnp.sum(d_weighted, axis=0, keepdims=True)).astype(BF16)
+    packed_ref[0:width] = mat_nn(d_logits, normed2).T
+    d_normed2 = d_rows_ref[...] + mat_tn(d_logits, w_router_t_ref[...])
+    h_f32 = h_ref[...].astype(F32)
+    d_h_part, d_gain2 = rms_back(h_f32, rms_parts(h_f32), gains_ref[1:2].astype(F32), d_normed2)
+    d_h = (dy_ref[...].astype(F32) + d_h_part).astype(BF16)
+    d_w_out_ref[...] = mat_tn(context_ref[...], d_h)
+    d_context = mat_nt(d_h, w_out_ref[...]).astype(BF16)
+    for seq in range(num_seqs):
+        whole = slice(seq * seq_len, (seq + 1) * seq_len)
+        for head in range(width // HEAD_DIM):
+            cols = [slice(part * width + head * HEAD_DIM, part * width + (head + 1) * HEAD_DIM) for part in range(3)]
+            d_key = jnp.zeros((seq_len, HEAD_DIM), F32)
+            d_value = jnp.zeros((seq_len, HEAD_DIM), F32)
+            for start in reversed(range(0, seq_len, block)):
+                rows = slice(seq * seq_len + start, seq * seq_len + start + block)
+                seen = slice(seq * seq_len, seq * seq_len + start + block)
+                query, keys = qkv_ref[rows, cols[0]], qkv_ref[seen, cols[1]]
+                weights = causal_probs(query, keys, start)
+                d_out = d_context[rows, cols[0]]
+                d_weights = mat_nt(d_out, qkv_ref[seen, cols[2]]).astype(BF16).astype(F32)
+                d_scores = (weights * (d_weights - jnp.sum(weights * d_weights, axis=1, keepdims=True)) * HEAD_DIM ** -0.5).astype(BF16)
+                d_query = mat_nn(d_scores, keys).astype(BF16).astype(F32)
+                at = slice(start, start + block)
+                d_query = d_query * cos_ref[at] - pltpu.roll(d_query, HEAD_DIM // 2, 1) * sin_ref[at]
+                d_qkv_scr[rows, cols[0]] = d_query.astype(BF16)
+                key_part, value_part = mat_tn(d_scores, query), mat_tn(weights.astype(BF16), d_out)
+                if start + block == seq_len:
+                    d_key, d_value = key_part, value_part
+                else:
+                    d_key = jnp.concatenate([d_key[:start + block] + key_part, d_key[start + block:]], axis=0)
+                    d_value = jnp.concatenate([d_value[:start + block] + value_part, d_value[start + block:]], axis=0)
+            d_key = d_key.astype(BF16).astype(F32)
+            d_key = d_key * cos_ref[...] - pltpu.roll(d_key, HEAD_DIM // 2, 1) * sin_ref[...]
+            d_qkv_scr[whole, cols[1]] = d_key.astype(BF16)
+            d_qkv_scr[whole, cols[2]] = d_value.astype(BF16)
+    d_qkv = d_qkv_scr[...]
+    x_f32 = x_ref[...].astype(F32)
+    inv_rms = rms_parts(x_f32)
+    gain1 = gains_ref[0:1].astype(F32)
+    d_w_qkv_ref[...] = mat_tn((x_f32 * inv_rms * gain1).astype(BF16), d_qkv)
+    d_x_part, d_gain1 = rms_back(x_f32, inv_rms, gain1, mat_nt(d_qkv, w_qkv_ref[...]))
+    d_x_ref[...] = (d_h.astype(F32) + d_x_part).astype(BF16)
+    packed_ref[width:] = jnp.zeros((packed_ref.shape[0] - width, num_experts), F32)
+    for row, d_gain in enumerate((d_gain1, d_gain2)):
+        for part in range(width // num_experts):
+            at = width + row * (width // num_experts) + part
+            packed_ref[at:at + 1] = d_gain[:, part * num_experts:(part + 1) * num_experts]
+
+
+def dense_backward(x_rows, dy_rows, d_rows, d_gates, idx_cols, saved, num_seqs, gains, w_qkv, w_attn_out, w_router_t, tables):
+    width = x_rows.shape[1]
+    num_experts = w_router_t.shape[0]
+    return pl.pallas_call(
+        functools.partial(backward_kernel, num_seqs),
+        out_shape=[jax.ShapeDtypeStruct(x_rows.shape, BF16), jax.ShapeDtypeStruct(w_qkv.shape, F32),
+                   jax.ShapeDtypeStruct(w_attn_out.shape, F32), jax.ShapeDtypeStruct((width + 8 * pl.cdiv(2 * width, 8 * num_experts), num_experts), F32)],
+        scratch_shapes=[pltpu.VMEM((x_rows.shape[0], 3 * width), BF16)],
+        compiler_params=pltpu.CompilerParams(vmem_limit_bytes=48_000_000),
+        cost_estimate=pl.CostEstimate(flops=15_000_000_000, bytes_accessed=12_000_000, transcendentals=0),
+        name="dense_backward",
+    )(x_rows, dy_rows, d_rows, d_gates, idx_cols, *saved, gains, w_qkv, w_attn_out, w_router_t, *tables)
 
 
 def solution(mesh):
@@ -529,34 +626,34 @@
         dy_rows = dy_tokens.reshape(num_tokens, model_width)
         idx_cols = route_idx.reshape(num_tokens, top_k).T
         routes = idx_cols.astype(BF16).reshape(-1, model_width)
-        payload = jnp.concatenate([dy_rows, routes], axis=0)
-        moved = [lax.ppermute(payload, 'ep', [(i, i ^ k) for i in range(ep_size)]) for k in range(1, ep_size)]
-        dy_near = jnp.stack([payload] + moved)
+        near_part = jnp.concatenate([dy_rows, routes], axis=0)
+        from_core, from_chip = [lax.ppermute(near_part, 'ep', [(i, i ^ k) for i in range(ep_size)]) for k in (1, 2)]
+        from_far = lax.ppermute(from_chip, 'ep', [(i, i ^ 1) for i in range(ep_size)])
+        dy_near = jnp.stack([near_part, from_core, from_chip, from_far])
 
         def expert_of(gathered):
             return gathered.reshape(-1, top_k, num_tokens).astype(jnp.int32) - lax.axis_index('ep') * local_experts
 
         idx_near = expert_of(dy_near[:, num_tokens:])
         positions_near = slot_positions(idx_near, local_experts, capacity)
-        normed2, gate_vals, saved_state = dense_forward(x_rows, idx_cols, num_seqs, norm1_gain, norm2_gain, w_qkv, w_attn_out, w_router)
-        table = lax.all_gather(jnp.concatenate([normed2, payload], axis=0), ('dp', 'ep'))
-        rows_near, gates_near = near_gather(normed2, gate_vals)
+        tables = rope_tables(seq_len)
+        w_router_t = w_router.T
+        dense_weights = (num_seqs, jnp.stack([norm1_gain, norm2_gain]), w_qkv, w_attn_out, w_router_t, tables)
+        payload, gate_vals, qkv_rows, context, h_rows = dense_forward(x_rows, dy_rows, idx_cols, *dense_weights)
+        table = lax.all_gather(payload, ('dp', 'ep'))
+        rows_near, gates_near = near_gather(payload, gate_vals, num_tokens)
         d_near, d_gate_near, slot_gates, *near_grads = token_grads(positions_near, idx_near, gates_near, rows_near, dy_near, w_gate, w_up, w_down, capacity)
-        d_normed2_moe, d_gates, slot_gates_all = near_return(d_near, d_gate_near, slot_gates, mesh.shape['dp'])
+        d_rows, d_gates, slot_gates_all, routes_all = near_return(d_near, d_gate_near, slot_gates, dy_near[:, num_tokens:], mesh.shape['dp'])
         slot_gates_all = slot_gates_all.transpose(1, 0, 2, 3).reshape(local_experts, -1, 128)
-        d_x, dense_grads = dense_backward(saved_state, x_rows, dy_rows, d_gates, d_normed2_moe, norm1_gain, norm2_gain, w_qkv, w_attn_out, w_router)
-        gain_cols = jnp.zeros((model_width, 128), F32).at[:, 0].set(dense_grads[0]).at[:, 1].set(dense_grads[1])
-        packed = jnp.concatenate(dense_grads[2:] + (gain_cols,), axis=1)
-        packed, slot_gates_all = lax.optimization_barrier((packed, slot_gates_all))
-        positions = all_positions(expert_of(table[:, 2 * num_tokens:]).transpose(1, 0, 2), local_experts, capacity)
+        d_x, *dense_grads = dense_backward(x_rows, dy_rows, d_rows, d_gates, idx_cols, (payload, qkv_rows, context, h_rows), *dense_weights)
+        dense_grads, slot_gates_all = lax.optimization_barrier((dense_grads, slot_gates_all))
+        positions = all_positions(expert_of(routes_all).transpose(1, 0, 2), local_experts, capacity)
         counts = (jnp.max(positions, axis=2) + 16) // 16 * 16
         place = jnp.stack([lax.axis_index('dp'), lax.axis_index('ep')]).astype(jnp.int32)
         expert_grads = weight_grads(positions, counts, place, slot_gates_all, table, w_gate, w_up, w_down, near_grads, capacity)
-        packed = lax.psum(packed, ('dp', 'ep'))
-        qkv_end = w_qkv.shape[1]
-        out_end = qkv_end + w_attn_out.shape[1]
-        router_end = out_end + num_experts
-        dense_out = (packed[:, router_end], packed[:, router_end + 1], packed[:, :qkv_end], packed[:, qkv_end:out_end], packed[:, out_end:router_end])
+        d_w_qkv, d_w_out, packed = lax.psum(tuple(dense_grads), ('dp', 'ep'))
+        gain_rows = packed[model_width:model_width + 2 * model_width // num_experts].reshape(2, model_width)
+        dense_out = (gain_rows[0], gain_rows[1], d_w_qkv, d_w_out, packed[:model_width])
         return (d_x.reshape(x_tokens.shape),) + dense_out + tuple(expert_grads)
 
     return jax.shard_map(local_step, mesh=mesh,

time: 926 us -> 830 us (0.90)
  other arithmetic: 47.7 us -> 13.8 us
  matrix products: 29.5 us -> 0.45 us
  local copies, waits for them, and re-layouts: 35.5 us -> 18.9 us
    pallas_call x1, Pallas kernels: 319 us -> 291 us  [weight_grads(): pl.pallas_call(functools.partial(weight_grad_kernel, capacity, group, 256...]
    dot_general x14 -> x0, matrix products: 24.2 us -> none  [the longest x3 7.5 us: attention_core(): jnp.einsum('bhqk,bkhd->bqhd', attn_probs, value_h, preferred_element_type...]
    pallas_call x1 -> x3, Pallas kernels: 34.6 us -> 54.3 us  [the longest x1 34.1 us: near_return(): pl.pallas_call(near_return_kernel, in_specs=[vmem] * 4, out_specs=[vmem]...]
    convert_element_type x9 -> x0, other arithmetic: 12.9 us -> none  [the longest x4 3.32 us: rms_norm(): return (x_f32 * inv_rms * gain_vec.astype(jnp.float32)).astype(jnp.bfloat16)]
    psum x1, waiting for transfers between devices: 124 us -> 114 us  [local_step(): d_w_qkv, d_w_out, packed = lax.psum(tuple(dense_grads), ('dp', 'ep'))]
  transfers between devices with their start and end apart: 5 -> 5, of which waited for: 2 -> 2; matrix products, arithmetic and copies ran while one was open for 4% -> 2% of each run, Pallas kernels for 2% -> 4%
where the time goes in v4:
time: 830 us; the launch traced here: 820 us
  Pallas kernels  460 us (55%)
  waiting for transfers between devices  309 us (37%)
  local copies, waits for them, and re-layouts  18.9 us (2%)
  between operations  14.7 us (2%)
  other arithmetic  13.8 us (2%)
    pallas_call x1, Pallas kernels, weight_grads(): pl.pallas_call(functools.partial(weight_grad_kernel, capacity, group, 256...  291 us
    all_gather x1, waiting for transfers between devices, local_step(): table = lax.all_gather(payload, ('dp', 'ep'))  194 us
    psum x1, waiting for transfers between devices, local_step(): d_w_qkv, d_w_out, packed = lax.psum(tuple(dense_grads), ('dp', 'ep'))  114 us
    pallas_call x1, Pallas kernels, token_grads(): pl.pallas_call(functools.partial(token_grad_kernel, capacity, group, 256)...  88.8 us
    pallas_call x1, Pallas kernels, near_return(): pl.pallas_call(near_return_kernel, in_specs=[vmem] * 4, out_specs=[vmem]...  34.1 us
    pallas_call x1, Pallas kernels, near_gather(): pl.pallas_call(near_gather_kernel, in_specs=[vmem, vmem], out_specs=[vmem...  18.4 us
  transfers between devices with their start and end apart: 5, of which 2 were waited for; matrix products, arithmetic and copies ran while one was open for 2% of the time, Pallas kernels for 4%

profile of v4, /device:TPU:0, one launch (start us, length us, event | category | flops | bytes accessed | tf_op | source)
XLA Modules:
  0.0 819.8 jit_solution(5115125917672739048)
XLA Ops:
  8.0 1.9 fusion.11
  10.4 2.5 collective-permute-start.1
  14.2 1.6 copy.35
  18.4 10.0 %dense_forward.1 = (bf16[2048,256]{1,0:T(8,128)(2,1)}, f32[8,1024]{1,0:T(8,128)}, bf16[1024,768]{1,0:T(8,128)(2,1)}, bf16[1024,256]{1,0:T(8,128)(2,1)}, bf16[1024,256]{1,0:T(8,128)(2,1)}) custom-call(bf16[1024,256]{1,0:T(8,128)(2,1)} %bitcast.41, bf16[1024,256]{1,0:T(8,128)(2,1)} %bitcast.33, s32[8,1024]{1,0:T(8,128)} %bitcast.39, ...), custom_call_target="tpu_custom_call" | custom-call | flops 10000000000 | bytes 8000000 | tf_op jit(solution)/shard_map/dense_forward/pallas_call | solution.py:518
  28.7 18.4 %near_gather.1 = (bf16[4,1024,256]{2,1,0:T(8,128)(2,1)}, f32[4,8,1024]{2,1,0:T(8,128)}) custom-call(bf16[2048,256]{1,0:T(8,128)(2,1)} %get-tuple-element.37.rows_ref.payload_ref, f32[8,1024]{1,0:T(8,128)} %get-tuple-element.38.gates_ref), custom_call_target="tpu_custom_call" | custom-call | flops 10000000000 | bytes 10000000 | tf_op jit(solution)/shard_map/near_gather/pallas_call | solution.py:201
  47.2 1.5 pad_maximum_fusion.dy_ref
  48.7 1.3 copy-done.17
  50.1 1.8 fusion
  52.4 1.4 convert_select_fusion.pos_ref
  53.7 88.8 %expert_token_grads.1 = (f32[4,1024,256]{2,1,0:T(8,128)}, f32[4,8,1024]{2,1,0:T(8,128)}, f32[32,4,128]{2,1,0:T(4,128)}, f32[32,256,768]{2,1,0:T(8,128)}, f32[32,...) custom-call(s32[32,4,1024]{2,1,0:T(4,128)} %convert_select_fusion.pos_ref, s32[4,8,1024]{2,1,0:T(8,128)} %copy-done.18, ...), custom_call_target="tpu_custom_call" | custom-call | flops 60000002048 | bytes 130000000 | tf_op jit(solution)/shard_map/expert_token_grads/pallas_call | solution.py:141
  142.5 2.2 copy-done.11
  146.6 34.1 %near_return.1 = (f32[1024,256]{1,0:T(8,128)S(1)}, f32[8,1024]{1,0:T(8,128)S(1)}, f32[7,32,4,128]{3,2,1,0:T(4,128)S(1)}, bf16[8,4,32,256]{3,2,1,0:T(8,128)(2,1)S(1)}) custom-call(f32[4,1024,256]{2,1,0:T(8,128)S(1)} %copy-done.11, f32[4,8,1024]{2,1,0:T(8,128)S(1)} %copy-done.15, f32[32,4,128]{2,1,0:T(4,128)S(1)} %copy-done.16, ...), custom_call_target="tpu_custom_call" | custom-call | flops 15000000512 | bytes 20000000 | tf_op jit(solution)/shard_map/near_return/pallas_call | solution.py:255
  180.9 10.1 %dense_backward.1 = (bf16[1024,256]{1,0:T(8,128)(2,1)}, f32[256,768]{1,0:T(8,128)}, f32[256,256]{1,0:T(8,128)}, f32[264,128]{1,0:T(8,128)}) custom-call(bf16[1024,256]{1,0:T(8,128)(2,1)S(1)} %bitcast.42, bf16[1024,256]{1,0:T(8,128)(2,1)S(1)} %bitcast.34, f32[1024,256]{1,0:T(8,128)S(1)} %get-tuple-element.44.d_rows_ref, ...), custom_call_target="tpu_custom_call" | custom-call | flops 15000000512 | bytes 12000000 | tf_op jit(solution)/shard_map/dense_backward/pallas_call | solution.py:601
  192.3 1.1 copy.38.slot_gate_ref
  194.5 7.3 slot_positions.1
  201.8 1.9 copy-done
  203.7 2.5 reduce_max.9
  206.9 114.2 %all-reduce.3.cloned.1.call-done = (f32[264,128]{1,0:T(8,128)}, f32[256,768]{1,0:T(8,128)}, f32[256,256]{1,0:T(8,128)}) async-done(((f32[264,128]{1,0:T(8,128)}, f32[256,768]{1,0:T(8,128)}, f32[256,256]{1,0:T(8,128)}), (f32[264,128]{1,0:T(8,128)}, f32[256,768]{1,0:T(8,128)}, f32[256,256]{1,0:T(8,128)})) %all-reduce.3.cloned.1.call-update) | async-done | bytes 1183760 | tf_op jit(solution)/shard_map/psum | solution.py:654
  321.1 1.6 slice.25
  322.7 1.3 slice_bitcast_fusion
  324.0 194.2 %all-gather.3.cloned.1.call-done = bf16[65536,256]{1,0:T(8,128)(2,1)} async-done(((bf16[2048,256]{1,0:T(8,128)(2,1)}), bf16[65536,256]{1,0:T(8,128)(2,1)}) %all-gather.3.cloned.1.call-update) | async-done | bytes 33554448 | tf_op jit(solution)/shard_map/all_gather | solution.py:643
  518.2 290.8 %expert_weight_grads.1 = (f32[32,256,768]{2,1,0:T(8,128)}, f32[32,256,768]{2,1,0:T(8,128)}, f32[32,768,256]{2,1,0:T(8,128)}) custom-call(s32[32,32]{1,0:T(8,128)} %fusion.9.count_ref, s32[2]{0:T(128)} %pad_add_fusion.place_ref, s32[32,32,1024]{2,1,0:T(8,128)} %bitcast.30, f32[32,28,128]{2,1,0:T(8,128)} %copy.38.slot_gate_ref, ...), custom_call_target="tpu_custom_call" | custom-call | flops 280000004096 | bytes 225000000 | tf_op jit(solution)/shard_map/expert_weight_grads/pallas_call | solution.py:418
  809.0 2.1 copy.47
  811.1 1.7 copy.48
  (64 shorter events, 11.0 us)
Async XLA Ops:
  7.2 313.9 %all-reduce.3.cloned.1.call-start = ((), (), s32[]{:S(2)}) async-start(), calls=%async_computation.1 | async-start | bytes 2367488 | tf_op jit(solution)/shard_map/psum | solution.py:654
  9.9 37.2 %collective-permute-start = (bf16[1056,256]{1,0:T(8,128)(2,1)}, bf16[1056,256]{1,0:T(8,128)(2,1)}, u32[]{:S(2)}, u32[]{:S(2)}) collective-permute-start(bf16[1056,256]{1,0:T(8,128)(2,1)} %get-tuple-element.69), channel_id=1, source_target_pairs={{0,1},{1,0},{2,3},{3,2},{4,5},{5,4},{6,7},{7,6},{8,9},{9,8},{10,11... | collective-permute-start | bytes 1622024 | tf_op jit(solution)/shard_map/ppermute | solution.py:630
  10.4 18.0 %collective-permute-start.1 = (bf16[1056,256]{1,0:T(8,128)(2,1)}, bf16[1056,256]{1,0:T(8,128)(2,1)}, u32[]{:S(2)}, u32[]{:S(2)}) collective-permute-start(bf16[1056,256]{1,0:T(8,128)(2,1)} %get-tuple-element.69), channel_id=1, source_target_pairs={{0,2},{1,3},{2,0},{3,1},{4,6},{5,7},{6,4},{7,5},{8,10},{9,11},{10,... | collective-permute-start | bytes 1622024 | tf_op jit(solution)/shard_map/ppermute | solution.py:630
  28.4 18.8 %collective-permute-start.2 = (bf16[1056,256]{1,0:T(8,128)(2,1)}, bf16[1056,256]{1,0:T(8,128)(2,1)S(1)}, u32[]{:S(2)}, u32[]{:S(2)}) collective-permute-start(bf16[1056,256]{1,0:T(8,128)(2,1)} %collective-permute-done.1), channel_id=1, source_target_pairs={{0,1},{1,0},{2,3},{3,2},{4,5},{5,4},{6,7},{7,6},{8,9},{9,8},{10,11... | collective-permute-start | bytes 1622024 | tf_op jit(solution)/shard_map/ppermute | solution.py:631
  48.7 1.3 copy-start.17
  50.1 3.6 copy-start.18
  142.5 2.2 copy-start.11
  144.7 0.9 copy-start.15
  145.6 0.8 copy-start.16
  146.5 34.3 %copy-start.1 = (bf16[2048,256]{1,0:T(8,128)(2,1)S(1)}, bf16[2048,256]{1,0:T(8,128)(2,1)}, u32[]{:S(2)}) copy-start(bf16[2048,256]{1,0:T(8,128)(2,1)} %get-tuple-element.37.rows_ref.payload_ref) | copy-start | bytes 3145732
  146.5 34.3 %copy-start.2 = (bf16[2,512,256]{2,1,0:T(8,128)(2,1)S(1)}, bf16[2,512,256]{2,1,0:T(8,128)(2,1)}, u32[]{:S(2)}) copy-start(bf16[2,512,256]{2,1,0:T(8,128)(2,1)} %param.12) | copy-start | bytes 1572868
  146.5 34.3 %copy-start.3 = (f32[512,128]{1,0:T(8,128)S(1)}, f32[512,128]{1,0:T(8,128)}, u32[]{:S(2)}) copy-start(f32[512,128]{1,0:T(8,128)} %get-tuple-element.75.cos_ref) | copy-start | bytes 786436
  146.5 34.3 %copy-start.4 = (f32[512,128]{1,0:T(8,128)S(1)}, f32[512,128]{1,0:T(8,128)}, u32[]{:S(2)}) copy-start(f32[512,128]{1,0:T(8,128)} %get-tuple-element.76.sin_ref) | copy-start | bytes 786436
  146.5 34.3 %copy-start.5 = (bf16[256,128]{0,1:T(8,128)(2,1)S(1)}, bf16[256,128]{0,1:T(8,128)(2,1)}, u32[]{:S(2)}) copy-start(bf16[256,128]{0,1:T(8,128)(2,1)} %copy.35) | copy-start | bytes 196612
  146.5 34.3 %copy-start.6 = (s32[2,512,8]{1,2,0:T(8,128)S(1)}, s32[2,512,8]{1,2,0:T(8,128)}, u32[]{:S(2)}) copy-start(s32[2,512,8]{1,2,0:T(8,128)} %param.13) | copy-start | bytes 98308
  146.5 34.3 %copy-start.7 = (bf16[2,256]{1,0:T(2,128)(2,1)S(1)}, bf16[2,256]{1,0:T(2,128)(2,1)}, u32[]{:S(2)}) copy-start(bf16[2,256]{1,0:T(2,128)(2,1)} %pad_maximum_fusion.4.gains_ref) | copy-start | bytes 3076
  146.5 34.3 %copy-start.8 = (bf16[2,512,256]{2,1,0:T(8,128)(2,1)S(1)}, bf16[2,512,256]{2,1,0:T(8,128)(2,1)}, u32[]{:S(2)}) copy-start(bf16[2,512,256]{2,1,0:T(8,128)(2,1)} %param.11) | copy-start | bytes 1572868
  146.5 34.3 %copy-start.9 = (bf16[256,768]{1,0:T(8,128)(2,1)S(1)}, bf16[256,768]{1,0:T(8,128)(2,1)}, u32[]{:S(2)}) copy-start(bf16[256,768]{1,0:T(8,128)(2,1)} %w_qkv_ref.3) | copy-start | bytes 1179652
  146.5 34.3 %copy-start.10 = (bf16[256,256]{1,0:T(8,128)(2,1)S(1)}, bf16[256,256]{1,0:T(8,128)(2,1)}, u32[]{:S(2)}) copy-start(bf16[256,256]{1,0:T(8,128)(2,1)} %w_out_ref.3) | copy-start | bytes 393220
  146.5 34.3 %copy-start.12 = (bf16[1024,768]{1,0:T(8,128)(2,1)S(1)}, bf16[1024,768]{1,0:T(8,128)(2,1)}, u32[]{:S(2)}) copy-start(bf16[1024,768]{1,0:T(8,128)(2,1)} %get-tuple-element.46.qkv_ref) | copy-start | bytes 4718596
  146.5 34.3 %copy-start.13 = (bf16[1024,256]{1,0:T(8,128)(2,1)S(1)}, bf16[1024,256]{1,0:T(8,128)(2,1)}, u32[]{:S(2)}) copy-start(bf16[1024,256]{1,0:T(8,128)(2,1)} %get-tuple-element.47.context_ref) | copy-start | bytes 1572868
  146.6 34.3 %copy-start.14 = (bf16[1024,256]{1,0:T(8,128)(2,1)S(1)}, bf16[1024,256]{1,0:T(8,128)(2,1)}, u32[]{:S(2)}) copy-start(bf16[1024,256]{1,0:T(8,128)(2,1)} %get-tuple-element.48.h_ref) | copy-start | bytes 1572868
  191.0 327.2 %all-gather.3.cloned.1.call-start = ((), (), s32[]{:S(2)}) async-start(), calls=%async_computation | async-start | bytes 34603008 | tf_op jit(solution)/shard_map/all_gather | solution.py:643
  201.7 1.9 copy-start
Sparse Core Ops, SparseCore 0:
  191.1 129.9 all-reduce.2
  324.0 194.1 all-gather.2

commit v5 on v4

--- a/solution.py
+++ b/solution.py
@@ -217,26 +217,31 @@
     dp_size = slot_gates_out.shape[0] + 1
     far_peers = [{'dp': lax.rem(dp + k, dp_size)} for k in range(1, dp_size)]
     meet([core_peer, chip_peer] + far_peers)
-    first = [remote(d_rows_ref.at[3], pass_rows, send_sem.at[0], recv_sem.at[0], core_peer),
-             remote(d_gates_ref.at[3], pass_gates, send_sem.at[1], recv_sem.at[1], core_peer)]
-    second = [remote(d_rows_ref.at[1], own_rows, send_sem.at[2], recv_sem.at[2], core_peer),
-              remote(d_gates_ref.at[1], own_gates, send_sem.at[3], recv_sem.at[3], core_peer)]
-    third = [remote(sum_rows, last_rows, send_sem.at[4], recv_sem.at[4], chip_peer),
-             remote(sum_gates, last_gates, send_sem.at[5], recv_sem.at[5], chip_peer)]
+    half = d_rows_ref.shape[1] // 2
+    halves = [pl.ds(0, half), pl.ds(half, half)]
     far = [remote(slot_gates_ref, slot_gates_out.at[dp_size - 2 - k], far_send_sem.at[0, k], far_recv_sem.at[0, k], peer) for k, peer in enumerate(far_peers)]
     far += [remote(routes_ref, routes_out.at[dp_size - 1 - k], far_send_sem.at[1, k], far_recv_sem.at[1, k], peer) for k, peer in enumerate(far_peers)]
-    for copy in first + second:
+    first = [remote(d_rows_ref.at[3, span], pass_rows.at[span], send_sem.at[i], recv_sem.at[i], core_peer) for i, span in enumerate(halves)]
+    first.append(remote(d_gates_ref.at[3], pass_gates, send_sem.at[2], recv_sem.at[2], core_peer))
+    second = [remote(d_rows_ref.at[1], own_rows, send_sem.at[3], recv_sem.at[3], core_peer),
+              remote(d_gates_ref.at[1], own_gates, send_sem.at[4], recv_sem.at[4], core_peer)]
+    third = [remote(sum_rows.at[span], last_rows.at[span], send_sem.at[5 + i], recv_sem.at[5 + i], chip_peer) for i, span in enumerate(halves)]
+    third.append(remote(sum_gates, last_gates, send_sem.at[7], recv_sem.at[7], chip_peer))
+    for copy in first + second + far:
         copy.start()
-    for copy in first:
-        copy.wait_recv()
-    sum_rows[...] = d_rows_ref[2] + pass_rows[...]
+    first[0].wait_recv()
+    sum_rows[halves[0]] = d_rows_ref[2, halves[0]] + pass_rows[halves[0]]
+    first[1].wait_recv()
+    first[2].wait_recv()
     sum_gates[...] = d_gates_ref[2] + pass_gates[...]
+    third[0].start()
+    sum_rows[halves[1]] = d_rows_ref[2, halves[1]] + pass_rows[halves[1]]
     for copy in second:
         copy.wait_recv()
     rows_out[...] = d_rows_ref[0] + own_rows[...]
     gates_out[...] = d_gates_ref[0] + own_gates[...]
-    for copy in third + far:
-        copy.start()
+    third[1].start()
+    third[2].start()
     routes_out[0] = routes_ref[...]
     for copy in third:
         copy.wait_recv()
@@ -257,7 +262,7 @@
         in_specs=[vmem] * 4, out_specs=[vmem] * 4,
         out_shape=[rows, gates, jax.ShapeDtypeStruct((dp_size - 1,) + slot_gates.shape, F32), jax.ShapeDtypeStruct((dp_size,) + routes.shape, BF16)],
         scratch_shapes=[pltpu.VMEM(rows.shape, F32)] * 4 + [pltpu.VMEM(gates.shape, F32)] * 4
-        + [pltpu.SemaphoreType.DMA((6,)), pltpu.SemaphoreType.DMA((6,)), pltpu.SemaphoreType.DMA((2, dp_size - 1)), pltpu.SemaphoreType.DMA((2, dp_size - 1))],
+        + [pltpu.SemaphoreType.DMA((8,)), pltpu.SemaphoreType.DMA((8,)), pltpu.SemaphoreType.DMA((2, dp_size - 1)), pltpu.SemaphoreType.DMA((2, dp_size - 1))],
         compiler_params=pltpu.CompilerParams(collective_id=1, has_side_effects=True, vmem_limit_bytes=40_000_000),
         cost_estimate=pl.CostEstimate(flops=15_000_000_000, bytes_accessed=20_000_000, transcendentals=0),
         name="near_return",
@@ -446,10 +451,10 @@
 
 def rope_tables(seq_len):
     half_dim = HEAD_DIM // 2
-    inv_freq = ROPE_BASE ** (-jnp.arange(half_dim, dtype=F32) / half_dim)
+    lane = jnp.arange(HEAD_DIM, dtype=jnp.int32)
+    inv_freq = ROPE_BASE ** (-(lane % half_dim).astype(F32) / half_dim)
     angles = jnp.arange(seq_len, dtype=F32)[:, None] * inv_freq[None, :]
-    cos, sin = jnp.cos(angles), jnp.sin(angles)
-    return jnp.concatenate([cos, cos], axis=1), jnp.concatenate([-sin, sin], axis=1)
+    return jnp.cos(angles), jnp.where(lane < half_dim, -1.0, 1.0) * jnp.sin(angles)
 
 
 def causal_probs(query, keys, start):
@@ -466,7 +471,7 @@
     return weights / jnp.sum(weights, axis=0, keepdims=True)
 
 
-def forward_kernel(num_seqs, x_ref, dy_ref, idx_ref, gains_ref, w_qkv_ref, w_out_ref, w_router_t_ref, cos_ref, sin_ref,
+def forward_kernel(num_seqs, x_ref, dy_ref, idx_ref, gain1_ref, gain2_ref, w_qkv_ref, w_out_ref, w_router_ref, cos_ref, sin_ref,
                    payload_ref, gates_ref, qkv_ref, context_ref, h_ref, x_scr, w_qkv_scr, w_out_scr, load_sem):
     num_tokens, width = x_ref.shape
     seq_len = num_tokens // num_seqs
@@ -478,7 +483,7 @@
     loads[0].wait()
     x_ref = x_scr
     x_f32 = x_ref[...].astype(F32)
-    normed1 = (x_f32 * rms_parts(x_f32) * gains_ref[0:1].astype(F32)).astype(BF16)
+    normed1 = (x_f32 * rms_parts(x_f32) * gain1_ref[...].astype(F32)[None]).astype(BF16)
     loads[1].wait()
     for head_col in range(0, 3 * width, HEAD_DIM):
         vals = mat_nn(normed1, w_qkv_scr[:, head_col:head_col + HEAD_DIM])
@@ -500,9 +505,9 @@
     h_rows = (x_f32 + mat_nn(context_ref[...], w_out_scr[...])).astype(BF16)
     h_ref[...] = h_rows
     h_f32 = h_rows.astype(F32)
-    normed2 = (h_f32 * rms_parts(h_f32) * gains_ref[1:2].astype(F32)).astype(BF16)
+    normed2 = (h_f32 * rms_parts(h_f32) * gain2_ref[...].astype(F32)[None]).astype(BF16)
     payload_ref[0:num_tokens] = normed2
-    probs = router_probs(normed2, w_router_t_ref[...])
+    probs = router_probs(normed2, w_router_ref[...].T)
     expert_iota = lax.broadcasted_iota(jnp.int32, probs.shape, 0)
     picked = [jnp.sum(jnp.where(expert_iota == idx_ref[choice:choice + 1], probs, 0.0), axis=0, keepdims=True) for choice in range(idx_ref.shape[0])]
     total = functools.reduce(lambda a, b: a + b, picked)
@@ -511,30 +516,31 @@
     loads[3].wait()
 
 
-def dense_forward(x_rows, dy_rows, idx_cols, num_seqs, gains, w_qkv, w_attn_out, w_router_t, tables):
+def dense_forward(x_rows, dy_rows, idx_cols, num_seqs, norm1_gain, norm2_gain, w_qkv, w_attn_out, w_router, tables):
     num_tokens, width = x_rows.shape
     rows = jax.ShapeDtypeStruct(x_rows.shape, BF16)
     hbm, vmem = pl.BlockSpec(memory_space=pl.ANY), pl.BlockSpec(memory_space=pltpu.VMEM)
     return pl.pallas_call(
         functools.partial(forward_kernel, num_seqs),
-        in_specs=[hbm, hbm, vmem, vmem, hbm, hbm, vmem, vmem, vmem],
+        in_specs=[hbm, hbm, vmem, vmem, vmem, hbm, hbm, vmem, vmem, vmem],
         scratch_shapes=[pltpu.VMEM(x_rows.shape, BF16), pltpu.VMEM(w_qkv.shape, BF16), pltpu.VMEM(w_attn_out.shape, BF16), pltpu.SemaphoreType.DMA((4,))],
         out_shape=[jax.ShapeDtypeStruct((2 * num_tokens, width), BF16), jax.ShapeDtypeStruct(idx_cols.shape, F32),
                    jax.ShapeDtypeStruct((num_tokens, 3 * width), BF16), rows, rows],
         compiler_params=pltpu.CompilerParams(vmem_limit_bytes=66_000_000),
         cost_estimate=pl.CostEstimate(flops=10_000_000_000, bytes_accessed=8_000_000, transcendentals=0),
         name="dense_forward",
-    )(x_rows, dy_rows, idx_cols, gains, w_qkv, w_attn_out, w_router_t, *tables)
+    )(x_rows, dy_rows, idx_cols, norm1_gain, norm2_gain, w_qkv, w_attn_out, w_router, *tables)
 
 
 def backward_kernel(num_seqs, x_ref, dy_ref, d_rows_ref, d_gates_ref, idx_ref, payload_ref, qkv_ref, context_ref, h_ref,
-                    gains_ref, w_qkv_ref, w_out_ref, w_router_t_ref, cos_ref, sin_ref, d_x_ref, d_w_qkv_ref, d_w_out_ref, packed_ref, d_qkv_scr):
+                    gain1_ref, gain2_ref, w_qkv_ref, w_out_ref, w_router_ref, cos_ref, sin_ref, d_x_ref, d_w_qkv_ref, d_w_out_ref, packed_ref, d_qkv_scr):
     num_tokens, width = x_ref.shape
     seq_len = num_tokens // num_seqs
-    num_experts = w_router_t_ref.shape[0]
+    num_experts = w_router_ref.shape[1]
     block = 256
     normed2 = payload_ref[0:num_tokens]
-    probs = router_probs(normed2, w_router_t_ref[...])
+    w_router_t = w_router_ref[...].T
+    probs = router_probs(normed2, w_router_t)
     expert_iota = lax.broadcasted_iota(jnp.int32, probs.shape, 0)
     chosen = jnp.zeros(probs.shape, F32)
     d_gate = jnp.zeros(probs.shape, F32)
@@ -547,9 +553,9 @@
     d_weighted = chosen * ((d_gate - mixed) / total)
     d_logits = (d_weighted - probs * jnp.sum(d_weighted, axis=0, keepdims=True)).astype(BF16)
     packed_ref[0:width] = mat_nn(d_logits, normed2).T
-    d_normed2 = d_rows_ref[...] + mat_tn(d_logits, w_router_t_ref[...])
+    d_normed2 = d_rows_ref[...] + mat_tn(d_logits, w_router_t)
     h_f32 = h_ref[...].astype(F32)
-    d_h_part, d_gain2 = rms_back(h_f32, rms_parts(h_f32), gains_ref[1:2].astype(F32), d_normed2)
+    d_h_part, d_gain2 = rms_back(h_f32, rms_parts(h_f32), gain2_ref[...].astype(F32)[None], d_normed2)
     d_h = (dy_ref[...].astype(F32) + d_h_part).astype(BF16)
     d_w_out_ref[...] = mat_tn(context_ref[...], d_h)
     d_context = mat_nt(d_h, w_out_ref[...]).astype(BF16)
@@ -584,7 +590,7 @@
     d_qkv = d_qkv_scr[...]
     x_f32 = x_ref[...].astype(F32)
     inv_rms = rms_parts(x_f32)
-    gain1 = gains_ref[0:1].astype(F32)
+    gain1 = gain1_ref[...].astype(F32)[None]
     d_w_qkv_ref[...] = mat_tn((x_f32 * inv_rms * gain1).astype(BF16), d_qkv)
     d_x_part, d_gain1 = rms_back(x_f32, inv_rms, gain1, mat_nt(d_qkv, w_qkv_ref[...]))
     d_x_ref[...] = (d_h.astype(F32) + d_x_part).astype(BF16)
@@ -595,9 +601,9 @@
             packed_ref[at:at + 1] = d_gain[:, part * num_experts:(part + 1) * num_experts]
 
 
-def dense_backward(x_rows, dy_rows, d_rows, d_gates, idx_cols, saved, num_seqs, gains, w_qkv, w_attn_out, w_router_t, tables):
+def dense_backward(x_rows, dy_rows, d_rows, d_gates, idx_cols, saved, num_seqs, norm1_gain, norm2_gain, w_qkv, w_attn_out, w_router, tables):
     width = x_rows.shape[1]
-    num_experts = w_router_t.shape[0]
+    num_experts = w_router.shape[1]
     return pl.pallas_call(
         functools.partial(backward_kernel, num_seqs),
         out_shape=[jax.ShapeDtypeStruct(x_rows.shape, BF16), jax.ShapeDtypeStruct(w_qkv.shape, F32),
@@ -606,7 +612,28 @@
         compiler_params=pltpu.CompilerParams(vmem_limit_bytes=48_000_000),
         cost_estimate=pl.CostEstimate(flops=15_000_000_000, bytes_accessed=12_000_000, transcendentals=0),
         name="dense_backward",
-    )(x_rows, dy_rows, d_rows, d_gates, idx_cols, *saved, gains, w_qkv, w_attn_out, w_router_t, *tables)
+    )(x_rows, dy_rows, d_rows, d_gates, idx_cols, *saved, norm1_gain, norm2_gain, w_qkv, w_attn_out, w_router, *tables)
+
+
+def unpack_kernel(width, d_w_qkv_ref, d_w_out_ref, packed_ref, d_w_qkv_out, d_w_out_out, d_w_router_out, gains_out):
+    d_w_qkv_out[...] = d_w_qkv_ref[...]
+    d_w_out_out[...] = d_w_out_ref[...]
+    d_w_router_out[...] = packed_ref[0:width]
+    lanes = packed_ref.shape[1]
+    for row in range(2):
+        for part in range(width // lanes):
+            at = width + row * (width // lanes) + part
+            gains_out[row:row + 1, part * lanes:(part + 1) * lanes] = packed_ref[at:at + 1]
+
+
+def unpack(d_w_qkv, d_w_out, packed):
+    width = d_w_out.shape[0]
+    return pl.pallas_call(
+        functools.partial(unpack_kernel, width),
+        out_shape=[jax.ShapeDtypeStruct(d_w_qkv.shape, F32), jax.ShapeDtypeStruct(d_w_out.shape, F32),
+                   jax.ShapeDtypeStruct((width, packed.shape[1]), F32), jax.ShapeDtypeStruct((2, width), F32)],
+        name="unpack_grads",
+    )(d_w_qkv, d_w_out, packed)
 
 
 def solution(mesh):
@@ -637,8 +664,7 @@
         idx_near = expert_of(dy_near[:, num_tokens:])
         positions_near = slot_positions(idx_near, local_experts, capacity)
         tables = rope_tables(seq_len)
-        w_router_t = w_router.T
-        dense_weights = (num_seqs, jnp.stack([norm1_gain, norm2_gain]), w_qkv, w_attn_out, w_router_t, tables)
+        dense_weights = (num_seqs, norm1_gain, norm2_gain, w_qkv, w_attn_out, w_router, tables)
         payload, gate_vals, qkv_rows, context, h_rows = dense_forward(x_rows, dy_rows, idx_cols, *dense_weights)
         table = lax.all_gather(payload, ('dp', 'ep'))
         rows_near, gates_near = near_gather(payload, gate_vals, num_tokens)
@@ -651,9 +677,8 @@
         counts = (jnp.max(positions, axis=2) + 16) // 16 * 16
         place = jnp.stack([lax.axis_index('dp'), lax.axis_index('ep')]).astype(jnp.int32)
         expert_grads = weight_grads(positions, counts, place, slot_gates_all, table, w_gate, w_up, w_down, near_grads, capacity)
-        d_w_qkv, d_w_out, packed = lax.psum(tuple(dense_grads), ('dp', 'ep'))
-        gain_rows = packed[model_width:model_width + 2 * model_width // num_experts].reshape(2, model_width)
-        dense_out = (gain_rows[0], gain_rows[1], d_w_qkv, d_w_out, packed[:model_width])
+        d_w_qkv, d_w_out, d_w_router, gain_rows = unpack(*lax.psum(tuple(dense_grads), ('dp', 'ep')))
+        dense_out = (gain_rows[0], gain_rows[1], d_w_qkv, d_w_out, d_w_router)
         return (d_x.reshape(x_tokens.shape),) + dense_out + tuple(expert_grads)
 
     return jax.shard_map(local_step, mesh=mesh,

time: 830 us -> 822 us (level)
  transfers between devices with their start and end apart: 5 -> 5, of which waited for: 2 -> 3; matrix products, arithmetic and copies ran while one was open for 2% -> 1% of each run, Pallas kernels for 4% -> 5%
where the time goes in v5:
time: 822 us; the launch traced here: 812 us
  Pallas kernels  462 us (56%)
  waiting for transfers between devices  309 us (38%)
  between operations  14.7 us (2%)
  other arithmetic  13 us (2%)
  local copies, waits for them, and re-layouts  10.7 us (1%)
    pallas_call x1, Pallas kernels, weight_grads(): pl.pallas_call(functools.partial(weight_grad_kernel, capacity, group, 256...  291 us
    all_gather x1, waiting for transfers between devices, local_step(): table = lax.all_gather(payload, ('dp', 'ep'))  194 us
    psum x1, waiting for transfers between devices, local_step(): lax.psum(tuple(dense_grads), ('dp', 'ep'))  113 us
    pallas_call x1, Pallas kernels, token_grads(): pl.pallas_call(functools.partial(token_grad_kernel, capacity, group, 256)...  88.8 us
    pallas_call x1, Pallas kernels, near_return(): pl.pallas_call(near_return_kernel, in_specs=[vmem] * 4, out_specs=[vmem]...  33.6 us
    pallas_call x1, Pallas kernels, near_gather(): pl.pallas_call(near_gather_kernel, in_specs=[vmem, vmem], out_specs=[vmem...  18.7 us
  transfers between devices with their start and end apart: 5, of which 3 were waited for; matrix products, arithmetic and copies ran while one was open for 1% of the time, Pallas kernels for 5%

profile of v5, /device:TPU:0, one launch (start us, length us, event | category | flops | bytes accessed | tf_op | source)
XLA Modules:
  0.0 812.3 jit_solution(12648358152105946982)
XLA Ops:
  8.0 1.9 fusion.13
  10.4 2.5 collective-permute-start.1
  12.9 1.7 sine_multiply_fusion
  14.6 10.1 %dense_forward.1 = (bf16[2048,256]{1,0:T(8,128)(2,1)}, f32[8,1024]{1,0:T(8,128)}, bf16[1024,768]{1,0:T(8,128)(2,1)}, bf16[1024,256]{1,0:T(8,128)(2,1)}, bf16[1024,256]{1,0:T(8,128)(2,1)}) custom-call(bf16[1024,256]{1,0:T(8,128)(2,1)} %bitcast.36, bf16[1024,256]{1,0:T(8,128)(2,1)} %bitcast.30, s32[8,1024]{1,0:T(8,128)} %bitcast.34, bf16[256]{0:T(256)(128)(2,1)} %gain1_ref.3, ...), custom_call_target="tpu_custom_call" | custom-call | flops 10000000000 | bytes 8000000 | tf_op jit(solution)/shard_map/dense_forward/pallas_call | solution.py:523
  24.7 1.4 collective-permute-done.1
  26.2 18.7 %near_gather.1 = (bf16[4,1024,256]{2,1,0:T(8,128)(2,1)}, f32[4,8,1024]{2,1,0:T(8,128)}) custom-call(bf16[2048,256]{1,0:T(8,128)(2,1)} %get-tuple-element.41.rows_ref.payload_ref, f32[8,1024]{1,0:T(8,128)} %get-tuple-element.42.gates_ref), custom_call_target="tpu_custom_call" | custom-call | flops 10000000000 | bytes 10000000 | tf_op jit(solution)/shard_map/near_gather/pallas_call | solution.py:201
  44.8 1.5 pad_maximum_fusion.dy_ref
  46.4 1.3 copy-done.18
  47.8 1.8 fusion
  50.0 1.4 convert_select_fusion.pos_ref
  51.4 88.8 %expert_token_grads.1 = (f32[4,1024,256]{2,1,0:T(8,128)}, f32[4,8,1024]{2,1,0:T(8,128)}, f32[32,4,128]{2,1,0:T(4,128)}, f32[32,256,768]{2,1,0:T(8,128)}, f32[32,...) custom-call(s32[32,4,1024]{2,1,0:T(4,128)} %convert_select_fusion.pos_ref, s32[4,8,1024]{2,1,0:T(8,128)} %copy-done.19, ...), custom_call_target="tpu_custom_call" | custom-call | flops 60000002048 | bytes 130000000 | tf_op jit(solution)/shard_map/expert_token_grads/pallas_call | solution.py:141
  140.2 2.2 copy-done.12
  142.4 0.9 copy-done.16
  144.2 33.6 %near_return.1 = (f32[1024,256]{1,0:T(8,128)S(1)}, f32[8,1024]{1,0:T(8,128)S(1)}, f32[7,32,4,128]{3,2,1,0:T(4,128)S(1)}, bf16[8,4,32,256]{3,2,1,0:T(8,128)(2,1)S(1)}) custom-call(f32[4,1024,256]{2,1,0:T(8,128)S(1)} %copy-done.12, f32[4,8,1024]{2,1,0:T(8,128)S(1)} %copy-done.16, f32[32,4,128]{2,1,0:T(4,128)S(1)} %copy-done.17, ...), custom_call_target="tpu_custom_call" | custom-call | flops 15000000512 | bytes 20000000 | tf_op jit(solution)/shard_map/near_return/pallas_call | solution.py:260
  178.1 10.1 %dense_backward.1 = (bf16[1024,256]{1,0:T(8,128)(2,1)}, f32[256,768]{1,0:T(8,128)}, f32[256,256]{1,0:T(8,128)}, f32[264,128]{1,0:T(8,128)}) custom-call(bf16[1024,256]{1,0:T(8,128)(2,1)S(1)} %bitcast.37, bf16[1024,256]{1,0:T(8,128)(2,1)S(1)} %bitcast.31, f32[1024,256]{1,0:T(8,128)S(1)} %get-tuple-element.48.d_rows_ref, ...), custom_call_target="tpu_custom_call" | custom-call | flops 15000000512 | bytes 12000000 | tf_op jit(solution)/shard_map/dense_backward/pallas_call | solution.py:607
  189.5 1.1 copy.35.slot_gate_ref
  191.6 7.3 slot_positions.1
  198.9 1.9 copy-done
  200.8 2.6 reduce_max.9
  204.1 113.1 %all-reduce.3.cloned.1.call-done = (f32[256,768]{1,0:T(8,128)}, f32[256,256]{1,0:T(8,128)}, f32[264,128]{1,0:T(8,128)}) async-done(((f32[256,768]{1,0:T(8,128)}, f32[256,256]{1,0:T(8,128)}, f32[264,128]{1,0:T(8,128)}), (f32[256,768]{1,0:T(8,128)}, f32[256,256]{1,0:T(8,128)}, f32[264,128]{1,0:T(8,128)})) %all-reduce.3.cloned.1.call-update) | async-done | bytes 1183760 | tf_op jit(solution)/shard_map/psum | solution.py:680
  317.2 2.2 unpack_grads.1
  319.4 1.3 fusion.14
  320.8 193.6 %all-gather.3.cloned.1.call-done = bf16[65536,256]{1,0:T(8,128)(2,1)} async-done(((bf16[2048,256]{1,0:T(8,128)(2,1)}), bf16[65536,256]{1,0:T(8,128)(2,1)}) %all-gather.3.cloned.1.call-update) | async-done | bytes 33554448 | tf_op jit(solution)/shard_map/all_gather | solution.py:669
  514.4 290.8 %expert_weight_grads.1 = (f32[32,256,768]{2,1,0:T(8,128)}, f32[32,256,768]{2,1,0:T(8,128)}, f32[32,768,256]{2,1,0:T(8,128)}) custom-call(s32[32,32]{1,0:T(8,128)} %fusion.7.count_ref, s32[2]{0:T(128)} %pad_add_fusion.place_ref, s32[32,32,1024]{2,1,0:T(8,128)} %bitcast.27, f32[32,28,128]{2,1,0:T(8,128)} %copy.35.slot_gate_ref, ...), custom_call_target="tpu_custom_call" | custom-call | flops 280000004096 | bytes 225000000 | tf_op jit(solution)/shard_map/expert_weight_grads/pallas_call | solution.py:423
  (59 shorter events, 5.9 us)
Async XLA Ops:
  7.2 310.0 %all-reduce.3.cloned.1.call-start = ((), (), s32[]{:S(2)}) async-start(), calls=%async_computation.1 | async-start | bytes 2367488 | tf_op jit(solution)/shard_map/psum | solution.py:680
  9.9 34.9 %collective-permute-start = (bf16[1056,256]{1,0:T(8,128)(2,1)}, bf16[1056,256]{1,0:T(8,128)(2,1)}, u32[]{:S(2)}, u32[]{:S(2)}) collective-permute-start(bf16[1056,256]{1,0:T(8,128)(2,1)} %get-tuple-element.77), channel_id=1, source_target_pairs={{0,1},{1,0},{2,3},{3,2},{4,5},{5,4},{6,7},{7,6},{8,9},{9,8},{10,11... | collective-permute-start | bytes 1622024 | tf_op jit(solution)/shard_map/ppermute | solution.py:657
  10.4 15.7 %collective-permute-start.1 = (bf16[1056,256]{1,0:T(8,128)(2,1)}, bf16[1056,256]{1,0:T(8,128)(2,1)}, u32[]{:S(2)}, u32[]{:S(2)}) collective-permute-start(bf16[1056,256]{1,0:T(8,128)(2,1)} %get-tuple-element.77), channel_id=1, source_target_pairs={{0,2},{1,3},{2,0},{3,1},{4,6},{5,7},{6,4},{7,5},{8,10},{9,11},{10,... | collective-permute-start | bytes 1622024 | tf_op jit(solution)/shard_map/ppermute | solution.py:657
  26.2 18.7 %collective-permute-start.2 = (bf16[1056,256]{1,0:T(8,128)(2,1)}, bf16[1056,256]{1,0:T(8,128)(2,1)S(1)}, u32[]{:S(2)}, u32[]{:S(2)}) collective-permute-start(bf16[1056,256]{1,0:T(8,128)(2,1)} %collective-permute-done.1), channel_id=1, source_target_pairs={{0,1},{1,0},{2,3},{3,2},{4,5},{5,4},{6,7},{7,6},{8,9},{9,8},{10,11... | collective-permute-start | bytes 1622024 | tf_op jit(solution)/shard_map/ppermute | solution.py:658
  46.3 1.3 copy-start.18
  47.7 3.6 copy-start.19
  140.2 2.2 copy-start.12
  142.4 0.9 copy-start.16
  144.1 33.8 %copy-start.1 = (bf16[2048,256]{1,0:T(8,128)(2,1)S(1)}, bf16[2048,256]{1,0:T(8,128)(2,1)}, u32[]{:S(2)}) copy-start(bf16[2048,256]{1,0:T(8,128)(2,1)} %get-tuple-element.41.rows_ref.payload_ref) | copy-start | bytes 3145732
  144.1 33.8 %copy-start.2 = (bf16[2,512,256]{2,1,0:T(8,128)(2,1)S(1)}, bf16[2,512,256]{2,1,0:T(8,128)(2,1)}, u32[]{:S(2)}) copy-start(bf16[2,512,256]{2,1,0:T(8,128)(2,1)} %param.12) | copy-start | bytes 1572868
  144.1 33.8 %copy-start.3 = (f32[512,128]{1,0:T(8,128)S(1)}, f32[512,128]{1,0:T(8,128)}, u32[]{:S(2)}) copy-start(f32[512,128]{1,0:T(8,128)} %get-tuple-element.80.sin_ref) | copy-start | bytes 786436
  144.1 33.8 %copy-start.4 = (f32[512,128]{1,0:T(8,128)S(1)}, f32[512,128]{1,0:T(8,128)}, u32[]{:S(2)}) copy-start(f32[512,128]{1,0:T(8,128)} %get-tuple-element.81.cos_ref) | copy-start | bytes 786436
  144.1 33.8 %copy-start.5 = (s32[2,512,8]{1,2,0:T(8,128)S(1)}, s32[2,512,8]{1,2,0:T(8,128)}, u32[]{:S(2)}) copy-start(s32[2,512,8]{1,2,0:T(8,128)} %param.13) | copy-start | bytes 98308
  144.1 33.8 %copy-start.6 = (bf16[2,512,256]{2,1,0:T(8,128)(2,1)S(1)}, bf16[2,512,256]{2,1,0:T(8,128)(2,1)}, u32[]{:S(2)}) copy-start(bf16[2,512,256]{2,1,0:T(8,128)(2,1)} %param.11) | copy-start | bytes 1572868
  144.2 33.8 %copy-start.7 = (bf16[256,768]{1,0:T(8,128)(2,1)S(1)}, bf16[256,768]{1,0:T(8,128)(2,1)}, u32[]{:S(2)}) copy-start(bf16[256,768]{1,0:T(8,128)(2,1)} %w_qkv_ref.3) | copy-start | bytes 1179652
  144.2 33.8 %copy-start.8 = (bf16[256,256]{1,0:T(8,128)(2,1)S(1)}, bf16[256,256]{1,0:T(8,128)(2,1)}, u32[]{:S(2)}) copy-start(bf16[256,256]{1,0:T(8,128)(2,1)} %w_out_ref.3) | copy-start | bytes 393220
  144.2 33.8 %copy-start.9 = (bf16[256,128]{1,0:T(8,128)(2,1)S(1)}, bf16[256,128]{1,0:T(8,128)(2,1)}, u32[]{:S(2)}) copy-start(bf16[256,128]{1,0:T(8,128)(2,1)} %w_router_ref.3) | copy-start | bytes 196612
  144.2 33.8 %copy-start.10 = (bf16[256]{0:T(256)(128)(2,1)S(1)}, bf16[256]{0:T(256)(128)(2,1)}, u32[]{:S(2)}) copy-start(bf16[256]{0:T(256)(128)(2,1)} %gain1_ref.3) | copy-start | bytes 1540
  144.2 33.8 %copy-start.11 = (bf16[256]{0:T(256)(128)(2,1)S(1)}, bf16[256]{0:T(256)(128)(2,1)}, u32[]{:S(2)}) copy-start(bf16[256]{0:T(256)(128)(2,1)} %gain2_ref.3) | copy-start | bytes 1540
  144.2 33.8 %copy-start.13 = (bf16[1024,768]{1,0:T(8,128)(2,1)S(1)}, bf16[1024,768]{1,0:T(8,128)(2,1)}, u32[]{:S(2)}) copy-start(bf16[1024,768]{1,0:T(8,128)(2,1)} %get-tuple-element.50.qkv_ref) | copy-start | bytes 4718596
  144.2 33.8 %copy-start.14 = (bf16[1024,256]{1,0:T(8,128)(2,1)S(1)}, bf16[1024,256]{1,0:T(8,128)(2,1)}, u32[]{:S(2)}) copy-start(bf16[1024,256]{1,0:T(8,128)(2,1)} %get-tuple-element.51.context_ref) | copy-start | bytes 1572868
  144.2 33.8 %copy-start.15 = (bf16[1024,256]{1,0:T(8,128)(2,1)S(1)}, bf16[1024,256]{1,0:T(8,128)(2,1)}, u32[]{:S(2)}) copy-start(bf16[1024,256]{1,0:T(8,128)(2,1)} %get-tuple-element.52.h_ref) | copy-start | bytes 1572868
  188.2 326.2 %all-gather.3.cloned.1.call-start = ((), (), s32[]{:S(2)}) async-start(), calls=%async_computation | async-start | bytes 34603008 | tf_op jit(solution)/shard_map/all_gather | solution.py:669
  198.9 1.9 copy-start
  (1 other events, 0.8 us)
Sparse Core Ops, SparseCore 0:
  188.3 128.8 all-reduce.2
  320.1 194.2 all-gather.2

commit v6 on v5

--- a/solution.py
+++ b/solution.py
@@ -269,7 +269,7 @@
     )(d_rows, d_gates, slot_gates, routes)
 
 
-def position_kernel(capacity, num_experts, idx_ref, pos_ref, member_scr):
+def position_kernel(capacity, num_experts, idx_ref, pos_ref, count_ref, member_scr):
     choices, sources, num_tokens = idx_ref.shape
     block = 256
 
@@ -287,20 +287,22 @@
         span = pl.ds(pl.multiple_of(step * block, block), block)
         member = member_scr[span]
         earlier = mat_nn(member, before)
+        held = jnp.minimum(earlier[:, num_tokens - 1:] + member[:, num_tokens - 1:].astype(F32), capacity).astype(jnp.int32)
+        count_ref[span] = jnp.broadcast_to((held + 15) // 16 * 16, (block, 128))
         pos_ref[span] = jnp.where((member.astype(F32) > 0.5) & (earlier < capacity), earlier, -1.0).astype(jnp.int32)
 
 
 def all_positions(idx_by_choice, num_experts, capacity):
     _, sources, num_tokens = idx_by_choice.shape
-    flat = pl.pallas_call(
+    flat, counts = pl.pallas_call(
         functools.partial(position_kernel, capacity, num_experts),
-        out_shape=jax.ShapeDtypeStruct((num_experts * sources, num_tokens), jnp.int32),
+        out_shape=[jax.ShapeDtypeStruct((num_experts * sources, num_tokens), jnp.int32), jax.ShapeDtypeStruct((num_experts * sources, 128), jnp.int32)],
         scratch_shapes=[pltpu.VMEM((num_experts * sources, num_tokens), BF16)],
         compiler_params=pltpu.CompilerParams(vmem_limit_bytes=32_000_000),
         cost_estimate=pl.CostEstimate(flops=4_000_000_000, bytes_accessed=5_000_000, transcendentals=0),
         name="slot_positions",
     )(idx_by_choice)
-    return flat.reshape(num_experts, sources, num_tokens)
+    return flat.reshape(num_experts, sources, num_tokens), counts[:, 0].reshape(num_experts, sources)
 
 
 def weight_grad_kernel(capacity, group, f_tile, near, chunks, tail, count_ref, place_ref, pos_ref, slot_gate_ref, table_hbm,
@@ -673,8 +675,7 @@
         slot_gates_all = slot_gates_all.transpose(1, 0, 2, 3).reshape(local_experts, -1, 128)
         d_x, *dense_grads = dense_backward(x_rows, dy_rows, d_rows, d_gates, idx_cols, (payload, qkv_rows, context, h_rows), *dense_weights)
         dense_grads, slot_gates_all = lax.optimization_barrier((dense_grads, slot_gates_all))
-        positions = all_positions(expert_of(routes_all).transpose(1, 0, 2), local_experts, capacity)
-        counts = (jnp.max(positions, axis=2) + 16) // 16 * 16
+        positions, counts = all_positions(expert_of(routes_all).transpose(1, 0, 2), local_experts, capacity)
         place = jnp.stack([lax.axis_index('dp'), lax.axis_index('ep')]).astype(jnp.int32)
         expert_grads = weight_grads(positions, counts, place, slot_gates_all, table, w_gate, w_up, w_down, near_grads, capacity)
         d_w_qkv, d_w_out, d_w_router, gain_rows = unpack(*lax.psum(tuple(dense_grads), ('dp', 'ep')))

time: 822 us -> 822 us (level)
  no operation moved by 1% of the time
where the time goes in v6:
time: 822 us; the launch traced here: 812 us
  Pallas kernels  462 us (56%)
  waiting for transfers between devices  310 us (38%)
  between operations  14.6 us (2%)
  local copies, waits for them, and re-layouts  11.6 us (1%)
  other arithmetic  9.81 us (1%)
    pallas_call x1, Pallas kernels, weight_grads(): pl.pallas_call(functools.partial(weight_grad_kernel, capacity, group, 256...  291 us
    all_gather x1, waiting for transfers between devices, local_step(): table = lax.all_gather(payload, ('dp', 'ep'))  194 us
    psum x1, waiting for transfers between devices, local_step(): lax.psum(tuple(dense_grads), ('dp', 'ep'))  115 us
    pallas_call x1, Pallas kernels, token_grads(): pl.pallas_call(functools.partial(token_grad_kernel, capacity, group, 256)...  88.8 us
    pallas_call x1, Pallas kernels, near_return(): pl.pallas_call(near_return_kernel, in_specs=[vmem] * 4, out_specs=[vmem]...  33.6 us
    pallas_call x1, Pallas kernels, near_gather(): pl.pallas_call(near_gather_kernel, in_specs=[vmem, vmem], out_specs=[vmem...  18.6 us
  transfers between devices with their start and end apart: 5, of which 3 were waited for; matrix products, arithmetic and copies ran while one was open for 1% of the time, Pallas kernels for 5%

profile of v6, /device:TPU:0, one launch (start us, length us, event | category | flops | bytes accessed | tf_op | source)
XLA Modules:
  0.0 812.3 jit_solution(7044006184381998810)
XLA Ops:
  8.0 1.9 fusion.10
  10.4 2.5 collective-permute-start.1
  12.9 1.7 sine_multiply_fusion
  14.6 10.1 %dense_forward.1 = (bf16[2048,256]{1,0:T(8,128)(2,1)}, f32[8,1024]{1,0:T(8,128)}, bf16[1024,768]{1,0:T(8,128)(2,1)}, bf16[1024,256]{1,0:T(8,128)(2,1)}, bf16[1024,256]{1,0:T(8,128)(2,1)}) custom-call(bf16[1024,256]{1,0:T(8,128)(2,1)} %bitcast.35, bf16[1024,256]{1,0:T(8,128)(2,1)} %bitcast.29, s32[8,1024]{1,0:T(8,128)} %bitcast.33, bf16[256]{0:T(256)(128)(2,1)} %gain1_ref.3, ...), custom_call_target="tpu_custom_call" | custom-call | flops 10000000000 | bytes 8000000 | tf_op jit(solution)/shard_map/dense_forward/pallas_call | solution.py:525
  24.7 1.4 collective-permute-done.1
  26.2 18.6 %near_gather.1 = (bf16[4,1024,256]{2,1,0:T(8,128)(2,1)}, f32[4,8,1024]{2,1,0:T(8,128)}) custom-call(bf16[2048,256]{1,0:T(8,128)(2,1)} %get-tuple-element.43.rows_ref.payload_ref, f32[8,1024]{1,0:T(8,128)} %get-tuple-element.44.gates_ref), custom_call_target="tpu_custom_call" | custom-call | flops 10000000000 | bytes 10000000 | tf_op jit(solution)/shard_map/near_gather/pallas_call | solution.py:201
  44.8 1.5 pad_maximum_fusion.dy_ref
  46.3 1.3 copy-done.18
  47.7 1.8 fusion
  50.0 1.4 convert_select_fusion.pos_ref
  51.4 88.8 %expert_token_grads.1 = (f32[4,1024,256]{2,1,0:T(8,128)}, f32[4,8,1024]{2,1,0:T(8,128)}, f32[32,4,128]{2,1,0:T(4,128)}, f32[32,256,768]{2,1,0:T(8,128)}, f32[32,...) custom-call(s32[32,4,1024]{2,1,0:T(4,128)} %convert_select_fusion.pos_ref, s32[4,8,1024]{2,1,0:T(8,128)} %copy-done.19, ...), custom_call_target="tpu_custom_call" | custom-call | flops 60000002048 | bytes 130000000 | tf_op jit(solution)/shard_map/expert_token_grads/pallas_call | solution.py:141
  140.2 2.2 copy-done.12
  142.4 0.9 copy-done.16
  143.3 0.8 copy-done.17
  144.2 33.6 %near_return.1 = (f32[1024,256]{1,0:T(8,128)S(1)}, f32[8,1024]{1,0:T(8,128)S(1)}, f32[7,32,4,128]{3,2,1,0:T(4,128)S(1)}, bf16[8,4,32,256]{3,2,1,0:T(8,128)(2,1)S(1)}) custom-call(f32[4,1024,256]{2,1,0:T(8,128)S(1)} %copy-done.12, f32[4,8,1024]{2,1,0:T(8,128)S(1)} %copy-done.16, f32[32,4,128]{2,1,0:T(4,128)S(1)} %copy-done.17, ...), custom_call_target="tpu_custom_call" | custom-call | flops 15000000512 | bytes 20000000 | tf_op jit(solution)/shard_map/near_return/pallas_call | solution.py:260
  178.1 10.1 %dense_backward.1 = (bf16[1024,256]{1,0:T(8,128)(2,1)}, f32[256,768]{1,0:T(8,128)}, f32[256,256]{1,0:T(8,128)}, f32[264,128]{1,0:T(8,128)}) custom-call(bf16[1024,256]{1,0:T(8,128)(2,1)S(1)} %bitcast.36, bf16[1024,256]{1,0:T(8,128)(2,1)S(1)} %bitcast.30, f32[1024,256]{1,0:T(8,128)S(1)} %get-tuple-element.50.d_rows_ref, ...), custom_call_target="tpu_custom_call" | custom-call | flops 15000000512 | bytes 12000000 | tf_op jit(solution)/shard_map/dense_backward/pallas_call | solution.py:609
  189.5 1.1 copy.35.slot_gate_ref
  191.7 8.0 slot_positions.1
  199.7 1.9 copy-done.11
  202.5 114.7 %all-reduce.3.cloned.1.call-done = (f32[256,768]{1,0:T(8,128)}, f32[256,256]{1,0:T(8,128)}, f32[264,128]{1,0:T(8,128)}) async-done(((f32[256,768]{1,0:T(8,128)}, f32[256,256]{1,0:T(8,128)}, f32[264,128]{1,0:T(8,128)}), (f32[256,768]{1,0:T(8,128)}, f32[256,256]{1,0:T(8,128)}, f32[264,128]{1,0:T(8,128)})) %all-reduce.3.cloned.1.call-update) | async-done | bytes 1183760 | tf_op jit(solution)/shard_map/psum | solution.py:681
  317.2 2.2 unpack_grads.1
  319.4 1.3 fusion.11
  320.7 193.6 %all-gather.3.cloned.1.call-done = bf16[65536,256]{1,0:T(8,128)(2,1)} async-done(((bf16[2048,256]{1,0:T(8,128)(2,1)}), bf16[65536,256]{1,0:T(8,128)(2,1)}) %all-gather.3.cloned.1.call-update) | async-done | bytes 33554448 | tf_op jit(solution)/shard_map/all_gather | solution.py:671
  514.3 290.8 %expert_weight_grads.1 = (f32[32,256,768]{2,1,0:T(8,128)}, f32[32,256,768]{2,1,0:T(8,128)}, f32[32,768,256]{2,1,0:T(8,128)}) custom-call(s32[32,32]{1,0:T(8,128)} %reshape_squeeze.3.count_ref, s32[2]{0:T(128)} %pad_add_fusion.place_ref, s32[32,32,1024]{2,1,0:T(8,128)} %bitcast.37, f32[32,28,128]{2,1,0:T(8,128)} %copy.35.slot_gate_ref, ...), custom_call_target="tpu_custom_call" | custom-call | flops 280000004096 | bytes 225000000 | tf_op jit(solution)/shard_map/expert_weight_grads/pallas_call | solution.py:425
  (57 shorter events, 5.2 us)
Async XLA Ops:
  7.2 310.0 %all-reduce.3.cloned.1.call-start = ((), (), s32[]{:S(2)}) async-start(), calls=%async_computation.1 | async-start | bytes 2367488 | tf_op jit(solution)/shard_map/psum | solution.py:681
  9.9 34.9 %collective-permute-start = (bf16[1056,256]{1,0:T(8,128)(2,1)}, bf16[1056,256]{1,0:T(8,128)(2,1)}, u32[]{:S(2)}, u32[]{:S(2)}) collective-permute-start(bf16[1056,256]{1,0:T(8,128)(2,1)} %get-tuple-element.81), channel_id=1, source_target_pairs={{0,1},{1,0},{2,3},{3,2},{4,5},{5,4},{6,7},{7,6},{8,9},{9,8},{10,11... | collective-permute-start | bytes 1622024 | tf_op jit(solution)/shard_map/ppermute | solution.py:659
  10.4 15.7 %collective-permute-start.1 = (bf16[1056,256]{1,0:T(8,128)(2,1)}, bf16[1056,256]{1,0:T(8,128)(2,1)}, u32[]{:S(2)}, u32[]{:S(2)}) collective-permute-start(bf16[1056,256]{1,0:T(8,128)(2,1)} %get-tuple-element.81), channel_id=1, source_target_pairs={{0,2},{1,3},{2,0},{3,1},{4,6},{5,7},{6,4},{7,5},{8,10},{9,11},{10,... | collective-permute-start | bytes 1622024 | tf_op jit(solution)/shard_map/ppermute | solution.py:659
  26.2 18.7 %collective-permute-start.2 = (bf16[1056,256]{1,0:T(8,128)(2,1)}, bf16[1056,256]{1,0:T(8,128)(2,1)S(1)}, u32[]{:S(2)}, u32[]{:S(2)}) collective-permute-start(bf16[1056,256]{1,0:T(8,128)(2,1)} %collective-permute-done.1), channel_id=1, source_target_pairs={{0,1},{1,0},{2,3},{3,2},{4,5},{5,4},{6,7},{7,6},{8,9},{9,8},{10,11... | collective-permute-start | bytes 1622024 | tf_op jit(solution)/shard_map/ppermute | solution.py:660
  46.3 1.3 copy-start.18
  47.7 3.6 copy-start.19
  140.2 2.2 copy-start.12
  142.4 0.9 copy-start.16
  144.1 33.8 %copy-start = (bf16[2048,256]{1,0:T(8,128)(2,1)S(1)}, bf16[2048,256]{1,0:T(8,128)(2,1)}, u32[]{:S(2)}) copy-start(bf16[2048,256]{1,0:T(8,128)(2,1)} %get-tuple-element.43.rows_ref.payload_ref) | copy-start | bytes 3145732
  144.1 33.8 %copy-start.1 = (bf16[2,512,256]{2,1,0:T(8,128)(2,1)S(1)}, bf16[2,512,256]{2,1,0:T(8,128)(2,1)}, u32[]{:S(2)}) copy-start(bf16[2,512,256]{2,1,0:T(8,128)(2,1)} %param.12) | copy-start | bytes 1572868
  144.1 33.8 %copy-start.2 = (f32[512,128]{1,0:T(8,128)S(1)}, f32[512,128]{1,0:T(8,128)}, u32[]{:S(2)}) copy-start(f32[512,128]{1,0:T(8,128)} %get-tuple-element.84.sin_ref) | copy-start | bytes 786436
  144.1 33.8 %copy-start.3 = (f32[512,128]{1,0:T(8,128)S(1)}, f32[512,128]{1,0:T(8,128)}, u32[]{:S(2)}) copy-start(f32[512,128]{1,0:T(8,128)} %get-tuple-element.85.cos_ref) | copy-start | bytes 786436
  144.1 33.8 %copy-start.4 = (s32[2,512,8]{1,2,0:T(8,128)S(1)}, s32[2,512,8]{1,2,0:T(8,128)}, u32[]{:S(2)}) copy-start(s32[2,512,8]{1,2,0:T(8,128)} %param.13) | copy-start | bytes 98308
  144.1 33.8 %copy-start.5 = (bf16[2,512,256]{2,1,0:T(8,128)(2,1)S(1)}, bf16[2,512,256]{2,1,0:T(8,128)(2,1)}, u32[]{:S(2)}) copy-start(bf16[2,512,256]{2,1,0:T(8,128)(2,1)} %param.11) | copy-start | bytes 1572868
  144.1 33.8 %copy-start.6 = (bf16[256,768]{1,0:T(8,128)(2,1)S(1)}, bf16[256,768]{1,0:T(8,128)(2,1)}, u32[]{:S(2)}) copy-start(bf16[256,768]{1,0:T(8,128)(2,1)} %w_qkv_ref.3) | copy-start | bytes 1179652
  144.1 33.8 %copy-start.7 = (bf16[256,256]{1,0:T(8,128)(2,1)S(1)}, bf16[256,256]{1,0:T(8,128)(2,1)}, u32[]{:S(2)}) copy-start(bf16[256,256]{1,0:T(8,128)(2,1)} %w_out_ref.3) | copy-start | bytes 393220
  144.2 33.8 %copy-start.8 = (bf16[256,128]{1,0:T(8,128)(2,1)S(1)}, bf16[256,128]{1,0:T(8,128)(2,1)}, u32[]{:S(2)}) copy-start(bf16[256,128]{1,0:T(8,128)(2,1)} %w_router_ref.3) | copy-start | bytes 196612
  144.2 33.8 %copy-start.9 = (bf16[256]{0:T(256)(128)(2,1)S(1)}, bf16[256]{0:T(256)(128)(2,1)}, u32[]{:S(2)}) copy-start(bf16[256]{0:T(256)(128)(2,1)} %gain1_ref.3) | copy-start | bytes 1540
  144.2 33.8 %copy-start.10 = (bf16[256]{0:T(256)(128)(2,1)S(1)}, bf16[256]{0:T(256)(128)(2,1)}, u32[]{:S(2)}) copy-start(bf16[256]{0:T(256)(128)(2,1)} %gain2_ref.3) | copy-start | bytes 1540
  144.2 33.8 %copy-start.13 = (bf16[1024,768]{1,0:T(8,128)(2,1)S(1)}, bf16[1024,768]{1,0:T(8,128)(2,1)}, u32[]{:S(2)}) copy-start(bf16[1024,768]{1,0:T(8,128)(2,1)} %get-tuple-element.52.qkv_ref) | copy-start | bytes 4718596
  144.2 33.8 %copy-start.14 = (bf16[1024,256]{1,0:T(8,128)(2,1)S(1)}, bf16[1024,256]{1,0:T(8,128)(2,1)}, u32[]{:S(2)}) copy-start(bf16[1024,256]{1,0:T(8,128)(2,1)} %get-tuple-element.53.context_ref) | copy-start | bytes 1572868
  144.2 33.8 %copy-start.15 = (bf16[1024,256]{1,0:T(8,128)(2,1)S(1)}, bf16[1024,256]{1,0:T(8,128)(2,1)}, u32[]{:S(2)}) copy-start(bf16[1024,256]{1,0:T(8,128)(2,1)} %get-tuple-element.54.h_ref) | copy-start | bytes 1572868
  188.2 326.2 %all-gather.3.cloned.1.call-start = ((), (), s32[]{:S(2)}) async-start(), calls=%async_computation | async-start | bytes 34603008 | tf_op jit(solution)/shard_map/all_gather | solution.py:671
  199.7 1.9 copy-start.11
  (1 other events, 0.8 us)
Sparse Core Ops, SparseCore 0:
  188.3 128.8 all-reduce.2
  320.0 194.2 all-gather.2
